TPU v7x, 32 devices: a whole 2x2x4 slice. The times are simulated.
32 devices in a mesh: dp: 8 (over y, x, core), seq: 4 (over z).
Axes of the slice: x: 2, y: 2, z: 4, core: 2. Of those that a mesh axis runs over, the one named last changes fastest.
Arguments:
- tokens: bfloat16 [32, 512, 768], P('dp', 'seq'), may hold values from -6 to 6
- cotangent: bfloat16 [32, 512, 768], P('dp', 'seq'), may hold values from -6 to 6
- tok_weight: int32 [32, 512], P('dp', 'seq'), may hold values from 1 to 4
- mask_count: int32 [32], P('dp'), may hold values from 0 to 512
- owner_list: int32 [384], replicated, may hold values from 0 to 383, as said below
- masters: float32 [384, 36864], P('dp'), may hold values from -0.5412659 to 0.5412659
- moment_one: float32 [384, 36864], P('dp'), may hold values from -13.568 to 13.568
- moment_two: float32 [384, 36864], P('dp'), may hold values from 0.98304 to 1114.112, as said below
- left_basis: float32 [384, 36864], P('dp'), may hold values from -1 to 1, as said below
- right_basis: float32 [384, 36864], P('dp'), may hold values from -1 to 1, as said below
- vectors: float32 [2, 9216], replicated, may hold values from -1.5 to 1.5, as said below
- vec_moment_one: float32 [2, 9216], replicated, may hold values from -23.68 to 23.68
- vec_moment_two: float32 [2, 9216], replicated, may hold values from 209.7152 to 3391.488, as said below
Outputs:
- layer_out: bfloat16 [32, 512, 768], P('dp', 'seq')
- input_grad: float32 [32, 512, 768], P('dp', 'seq')
- new_moment_one: float32 [384, 36864], P('dp')
- new_moment_two: float32 [384, 36864], P('dp')
- new_masters: float32 [384, 36864], P('dp')
- master_copies: bfloat16 [384, 36864], P('dp')
- new_vectors: float32 [2, 9216], replicated
- new_vec_moment_one: float32 [2, 9216], replicated
- new_vec_moment_two: float32 [2, 9216], replicated
Inputs may be any that keep to these rules, and one draw needn't show every extreme that they name: `owner_list`: a permutation: each row of the block arrays is named by exactly one block. `moment_two`: all entries positive. `left_basis`: each row, read as a 192 x 192 matrix, is orthogonal. `right_basis`: each row, read as a 192 x 192 matrix, is orthogonal. `vectors`: gains lie in 0.6 to 1.4. `vec_moment_two`: all entries positive.
All inputs are finite; a program needn't handle non-finite values.
Results may differ from a plain program's by a relative error of at most 0.015.
The roundings to bfloat16 on the way count: a program that leaves them out, or rounds other values in their place, can miss the bound.
Values may be sent and summed in bfloat16 or wider, within the bound.
A program may use at most 512 MiB of HBM per device.

v0:
```python
import jax
import jax.numpy as jnp
from jax import lax
from jax.sharding import PartitionSpec as P

HEADS = 12
HDIM = 64
BLK = 192


norm_eps = 1e-05
beta_one = 0.95
beta_two = 0.95
adam_eps = 1e-08
matrix_rate = 0.02
vector_rate = 0.2
decay_rate = 0.01
step_count = 6


def project(left, right):
    return jnp.dot(left, right, preferred_element_type=jnp.float32)


def matrix_shapes(width, inner_width):
    return [
        (width, width),
        (width, width),
        (width, width),
        (width, width),
        (width, inner_width),
        (inner_width, width),
    ]


def to_matrices(blocks, layer_count, width, inner_width):
    block_edge = blocks.shape[-1]
    result = []
    cursor = 0
    for layer_num in range(layer_count):
        members = []
        for row_size, col_size in matrix_shapes(width, inner_width):
            row_count = row_size // block_edge
            col_count = col_size // block_edge
            tile_set = blocks[cursor : cursor + row_count * col_count]
            members.append(
                tile_set.reshape(row_count, col_count, block_edge, block_edge)
                .transpose(0, 2, 1, 3)
                .reshape(row_size, col_size)
            )
            cursor = cursor + row_count * col_count
        result.append(members)
    return result


def to_blocks(matrices, block_edge):
    tile_list = []
    for members in matrices:
        for matrix in members:
            row_size, col_size = matrix.shape
            tile_list.append(
                matrix.reshape(
                    row_size // block_edge, block_edge, col_size // block_edge, block_edge
                )
                .transpose(0, 2, 1, 3)
                .reshape(-1, block_edge, block_edge)
            )
    return jnp.concatenate(tile_list, axis=0)


def unpack(vector, width):
    return [vector[number * width : (number + 1) * width] for number in range(8)] + [
        vector[8 * width :]
    ]


def norm_forward(hidden, gain, shift):
    center = hidden - jnp.mean(hidden, axis=-1, keepdims=True)
    spread = jnp.mean(center * center, axis=-1, keepdims=True)
    inverse = lax.rsqrt(spread + norm_eps)
    unit = center * inverse
    return (unit * gain + shift, unit, inverse)


def norm_backward(incoming, unit, inverse, gain):
    scaled = incoming * gain
    grad_hidden = inverse * (
        scaled
        - jnp.mean(scaled, axis=-1, keepdims=True)
        - unit * jnp.mean(scaled * unit, axis=-1, keepdims=True)
    )
    return (grad_hidden, jnp.sum(incoming * unit, axis=(0, 1)), jnp.sum(incoming, axis=(0, 1)))


def gelu_exact(value):
    return jax.nn.gelu(value, approximate=False)


def split_heads(tensor, parts):
    return tensor.reshape(tensor.shape[0], tensor.shape[1], parts, tensor.shape[2] // parts)


def forward_layer(hidden, matrices, pieces, parts, scale):
    w_query, w_key, w_value, w_out, w_up, w_down = matrices
    (
        bias_query,
        bias_value,
        bias_out,
        bias_down,
        gain_one,
        shift_one,
        gain_two,
        shift_two,
        bias_up,
    ) = pieces
    seq_block, local_len, width = hidden.shape
    head_local = HEADS // parts
    hid_low = hidden.astype(jnp.bfloat16)
    query = (project(hid_low, w_query) + bias_query).astype(jnp.bfloat16)
    keys = project(hid_low, w_key).astype(jnp.bfloat16)
    values = (project(hid_low, w_value) + bias_value).astype(jnp.bfloat16)
    query_h, keys_h, values_h = (
        lax.all_to_all(split_heads(query, parts), "seq", split_axis=2, concat_axis=1, tiled=True),
        lax.all_to_all(split_heads(keys, parts), "seq", split_axis=2, concat_axis=1, tiled=True),
        lax.all_to_all(split_heads(values, parts), "seq", split_axis=2, concat_axis=1, tiled=True),
    )
    full_len = query_h.shape[1]
    head_shape = (seq_block, full_len, head_local, HDIM)
    query_h = query_h.reshape(head_shape)
    keys_h = keys_h.reshape(head_shape)
    values_h = values_h.reshape(head_shape)

    def attend(triple):
        query_one, keys_one, values_one = triple
        scores = (
            jnp.einsum("qhe,khe->hqk", query_one, keys_one, preferred_element_type=jnp.float32)
            * scale
        )
        highest = jnp.max(scores, axis=-1, keepdims=True)
        raised = jnp.exp(scores - highest)
        total = jnp.sum(raised, axis=-1, keepdims=True)
        probs = raised / total
        mixed_one = jnp.einsum(
            "hqk,khe->qhe",
            probs.astype(jnp.bfloat16),
            values_one,
            preferred_element_type=jnp.float32,
        )
        return (mixed_one.astype(jnp.bfloat16), (highest + jnp.log(total))[..., 0])

    mixed_h, log_total = lax.map(attend, (query_h, keys_h, values_h))
    mixed = lax.all_to_all(
        mixed_h.reshape(seq_block, full_len, 1, width // parts),
        "seq",
        split_axis=1,
        concat_axis=2,
        tiled=True,
    )
    mixed = mixed.reshape(seq_block, local_len, width)
    branch = project(mixed, w_out) + bias_out
    normed, unit_one, inv_one = norm_forward(hidden + branch, gain_one, shift_one)
    norm_low = normed.astype(jnp.bfloat16)
    pre_act = project(norm_low, w_up) + bias_up
    act_low = gelu_exact(pre_act).astype(jnp.bfloat16)
    down = project(act_low, w_down) + bias_down
    result, unit_two, inv_two = norm_forward(normed + down, gain_two, shift_two)
    kept = (
        hid_low,
        query_h,
        keys_h,
        values_h,
        log_total,
        mixed,
        unit_one,
        inv_one,
        norm_low,
        pre_act,
        act_low,
        unit_two,
        inv_two,
    )
    return (result, kept)


def backward_layer(incoming, matrices, pieces, kept, parts, scale):
    w_query, w_key, w_value, w_out, w_up, w_down = matrices
    (
        bias_query,
        bias_value,
        bias_out,
        bias_down,
        gain_one,
        shift_one,
        gain_two,
        shift_two,
        bias_up,
    ) = pieces
    (
        hid_low,
        query_h,
        keys_h,
        values_h,
        log_total,
        mixed,
        unit_one,
        inv_one,
        norm_low,
        pre_act,
        act_low,
        unit_two,
        inv_two,
    ) = kept
    seq_block, local_len, width = mixed.shape
    full_len = query_h.shape[1]
    grad_two, gain_two_g, shift_two_g = norm_backward(incoming, unit_two, inv_two, gain_two)
    down_low = grad_two.astype(jnp.bfloat16)
    grad_bias_down = jnp.sum(down_low, axis=(0, 1), dtype=jnp.float32)
    grad_w_down = jnp.einsum("stf,std->fd", act_low, down_low, preferred_element_type=jnp.float32)
    grad_act = jnp.einsum("std,fd->stf", down_low, w_down, preferred_element_type=jnp.float32)
    (grad_pre,) = jax.vjp(gelu_exact, pre_act)[1](grad_act)
    up_low = grad_pre.astype(jnp.bfloat16)
    grad_bias_up = jnp.sum(up_low, axis=(0, 1), dtype=jnp.float32)
    grad_w_up = jnp.einsum("std,stf->df", norm_low, up_low, preferred_element_type=jnp.float32)
    grad_norm = grad_two + jnp.einsum(
        "stf,df->std", up_low, w_up, preferred_element_type=jnp.float32
    )
    grad_one, gain_one_g, shift_one_g = norm_backward(grad_norm, unit_one, inv_one, gain_one)
    out_low = grad_one.astype(jnp.bfloat16)
    grad_bias_out = jnp.sum(out_low, axis=(0, 1), dtype=jnp.float32)
    grad_w_out = jnp.einsum("std,ste->de", mixed, out_low, preferred_element_type=jnp.float32)
    grad_mix = jnp.einsum("ste,de->std", out_low, w_out, preferred_element_type=jnp.float32).astype(
        jnp.bfloat16
    )
    grad_mix_h = lax.all_to_all(
        split_heads(grad_mix, parts), "seq", split_axis=2, concat_axis=1, tiled=True
    ).reshape(query_h.shape)

    def attend_back(quintet):
        query_one, keys_one, values_one, total_one, grad_one_h = quintet
        scores = (
            jnp.einsum("qhe,khe->hqk", query_one, keys_one, preferred_element_type=jnp.float32)
            * scale
        )
        probs = jnp.exp(scores - total_one[:, :, None])
        grad_probs = jnp.einsum(
            "qhe,khe->hqk", grad_one_h, values_one, preferred_element_type=jnp.float32
        )
        grad_scores = (
            probs * (grad_probs - jnp.sum(probs * grad_probs, axis=-1, keepdims=True))
        ).astype(jnp.bfloat16)
        grad_query_one = (
            jnp.einsum("hqk,khe->qhe", grad_scores, keys_one, preferred_element_type=jnp.float32)
            * scale
        ).astype(jnp.bfloat16)
        grad_keys_one = (
            jnp.einsum("hqk,qhe->khe", grad_scores, query_one, preferred_element_type=jnp.float32)
            * scale
        ).astype(jnp.bfloat16)
        grad_values_one = jnp.einsum(
            "hqk,qhe->khe",
            probs.astype(jnp.bfloat16),
            grad_one_h,
            preferred_element_type=jnp.float32,
        ).astype(jnp.bfloat16)
        return (grad_query_one, grad_keys_one, grad_values_one)

    grad_query_h, grad_keys_h, grad_values_h = lax.map(
        attend_back, (query_h, keys_h, values_h, log_total, grad_mix_h)
    )
    flat_shape = (seq_block, full_len, 1, width // parts)
    grad_query, grad_keys, grad_values = (
        lax.all_to_all(
            grad_query_h.reshape(flat_shape), "seq", split_axis=1, concat_axis=2, tiled=True
        ),
        lax.all_to_all(
            grad_keys_h.reshape(flat_shape), "seq", split_axis=1, concat_axis=2, tiled=True
        ),
        lax.all_to_all(
            grad_values_h.reshape(flat_shape), "seq", split_axis=1, concat_axis=2, tiled=True
        ),
    )
    grad_query = grad_query.reshape(seq_block, local_len, width)
    grad_keys = grad_keys.reshape(seq_block, local_len, width)
    grad_values = grad_values.reshape(seq_block, local_len, width)
    grad_w_query = jnp.einsum(
        "std,ste->de", hid_low, grad_query, preferred_element_type=jnp.float32
    )
    grad_w_key = jnp.einsum("std,ste->de", hid_low, grad_keys, preferred_element_type=jnp.float32)
    grad_w_value = jnp.einsum(
        "std,ste->de", hid_low, grad_values, preferred_element_type=jnp.float32
    )
    grad_bias_query = jnp.sum(grad_query, axis=(0, 1), dtype=jnp.float32)
    grad_bias_value = jnp.sum(grad_values, axis=(0, 1), dtype=jnp.float32)
    grad_hidden = grad_one + jnp.einsum(
        "ste,de->std", grad_query, w_query, preferred_element_type=jnp.float32
    )
    grad_hidden = grad_hidden + jnp.einsum(
        "ste,de->std", grad_keys, w_key, preferred_element_type=jnp.float32
    )
    grad_hidden = grad_hidden + jnp.einsum(
        "ste,de->std", grad_values, w_value, preferred_element_type=jnp.float32
    )
    vec_grad = jnp.concatenate(
        [
            grad_bias_query,
            grad_bias_value,
            grad_bias_out,
            grad_bias_down,
            gain_one_g,
            shift_one_g,
            gain_two_g,
            shift_two_g,
            grad_bias_up,
        ]
    )
    return (
        grad_hidden,
        [grad_w_query, grad_w_key, grad_w_value, grad_w_out, grad_w_up, grad_w_down],
        vec_grad,
    )


def local(
    tokens,
    cotangent,
    tok_weight,
    mask_count,
    owner_list,
    masters,
    moment_one,
    moment_two,
    left_basis,
    right_basis,
    vectors,
    vec_moment_one,
    vec_moment_two,
):
    parts = lax.axis_size("seq")
    width = tokens.shape[-1]
    local_len = tokens.shape[1]
    layer_count = vectors.shape[0]
    inner_width = vectors.shape[-1] - 8 * width
    block_edge = BLK
    owned_count = masters.shape[0]
    scale = HDIM ** (-0.5)
    gathered = lax.all_gather(masters.astype(jnp.bfloat16), "dp", axis=0, tiled=True)
    gathered = gathered.reshape(gathered.shape[0], block_edge, block_edge)
    weights = to_matrices(gathered[owner_list], layer_count, width, inner_width)
    hidden = tokens.astype(jnp.float32)
    saved = []
    for layer_num in range(layer_count):
        hidden, kept = forward_layer(
            hidden, weights[layer_num], unpack(vectors[layer_num], width), parts, scale
        )
        saved.append(kept)
    layer_out = hidden.astype(jnp.bfloat16)
    positions = lax.axis_index("seq") * local_len + jnp.arange(local_len, dtype=jnp.int32)
    masked = (positions[None, :] < mask_count[:, None]).astype(jnp.float32)
    factor = tok_weight.astype(jnp.float32) * (1.0 + masked) * 0.25
    incoming = cotangent.astype(jnp.float32) * factor[:, :, None]
    mat_grads = [None] * layer_count
    vec_grads = [None] * layer_count
    for layer_num in reversed(range(layer_count)):
        incoming, mat_grads[layer_num], vec_grads[layer_num] = backward_layer(
            incoming,
            weights[layer_num],
            unpack(vectors[layer_num], width),
            saved[layer_num],
            parts,
            scale,
        )
    grad_blocks = to_blocks(mat_grads, block_edge)
    block_total = grad_blocks.shape[0]
    inverse_list = (
        jnp.zeros_like(owner_list)
        .at[owner_list]
        .set(jnp.arange(owner_list.shape[0], dtype=jnp.int32))
    )
    slot_grads = grad_blocks[inverse_list].reshape(block_total, block_edge * block_edge)
    owned = lax.psum_scatter(slot_grads, "dp", scatter_dimension=0, tiled=True)
    owned = lax.psum(owned.astype(jnp.bfloat16), "seq").astype(jnp.float32)
    vec_total = lax.psum(jnp.stack(vec_grads), ("dp", "seq"))
    cube = (owned_count, block_edge, block_edge)
    flat = (owned_count, block_edge * block_edge)
    owned_sq = owned.reshape(cube)
    left_sq = left_basis.reshape(cube)
    right_sq = right_basis.reshape(cube)
    masters_sq = masters.reshape(cube)
    highest = lax.Precision.HIGHEST
    rotated = jnp.einsum("sji,sjk->sik", left_sq, owned_sq, precision=highest)
    rotated = jnp.einsum("sik,skl->sil", rotated, right_sq, precision=highest)
    new_one = beta_one * moment_one.reshape(cube) + (1.0 - beta_one) * rotated
    new_two = beta_two * moment_two.reshape(cube) + (1.0 - beta_two) * rotated * rotated
    fix_one = 1.0 - beta_one**step_count
    fix_two = 1.0 - beta_two**step_count
    normal_step = new_one / fix_one / (jnp.sqrt(new_two / fix_two) + adam_eps)
    restored = jnp.einsum("sij,sjk->sik", left_sq, normal_step, precision=highest)
    restored = jnp.einsum("sik,slk->sil", restored, right_sq, precision=highest)
    new_masters = (masters_sq - matrix_rate * (restored + decay_rate * masters_sq)).reshape(flat)
    vec_one = beta_one * vec_moment_one + (1.0 - beta_one) * vec_total
    vec_two = beta_two * vec_moment_two + (1.0 - beta_two) * vec_total * vec_total
    new_vectors = vectors - vector_rate * (vec_one / fix_one) / (
        jnp.sqrt(vec_two / fix_two) + adam_eps
    )
    return (
        layer_out,
        incoming,
        new_one.reshape(flat),
        new_two.reshape(flat),
        new_masters,
        new_masters.astype(jnp.bfloat16),
        new_vectors,
        vec_one,
        vec_two,
    )


def solution(mesh):
    placed = (
        P("dp", "seq", None),
        P("dp", "seq", None),
        P("dp", "seq"),
        P("dp"),
        P(),
        P("dp", None),
        P("dp", None),
        P("dp", None),
        P("dp", None),
        P("dp", None),
        P(),
        P(),
        P(),
    )
    return jax.shard_map(
        local,
        mesh=mesh,
        in_specs=placed,
        out_specs=(
            P("dp", "seq", None),
            P("dp", "seq", None),
            P("dp", None),
            P("dp", None),
            P("dp", None),
            P("dp", None),
            P(),
            P(),
            P(),
        ),
        check_vma=False,
    )
```

profile of v0, /device:TPU:0, one launch (start us, length us, event | category | flops | bytes accessed | tf_op | source)
XLA Modules:
  0.0 2175.2 jit_solution(10038803649891000631)
XLA Ops:
  17.3 136.5 %all-gather.2.cloned.1.call-done = bf16[384,36864]{1,0:T(8,128)(2,1)} async-done(((bf16[48,36864]{1,0:T(8,128)(2,1)}), bf16[384,36864]{1,0:T(8,128)(2,1)}) %all-gather.2.cloned.1.call-update) | async-done | bytes 28311568 | tf_op jit(solution)/shard_map/all_gather | solution.py:346
  153.8 36.7 %copy.534 = bf16[384,36864]{0,1:T(8,128)(2,1)} copy(bf16[384,36864]{1,0:T(8,128)(2,1)} %all-gather.2.cloned.1.call-done) | data formatting | bytes 56623104 | tf_op jit(solution)/shard_map/all_gather | solution.py:346
  190.5 50.7 %copy.535 = bf16[384,192,192]{2,1,0:T(8,128)(2,1)} copy(bf16[384,192,192]{0,2,1:T(8,128)(2,1)} %bitcast.556) | data formatting | bytes 56623104 | tf_op jit(solution)/shard_map/reshape | solution.py:347
  241.2 26.4 %gather_fusion = bf16[384,192,192]{2,1,0:T(8,128)(2,1)} fusion(bf16[384,192,192]{2,1,0:T(8,128)(2,1)} %copy.535, s32[1024]{0:T(1024)S(1)} %get-tuple-element.337), kind=kCustom, calls=%fused_computation | custom fusion | bytes 56624640 | tf_op jit(solution)/shard_map/gather | solution.py:348
  267.5 9.4 fusion.195
  295.8 12.4 all-to-all-done
  320.6 11.6 all-to-all-done.1
  341.1 14.4 all-to-all-done.2
  359.6 10.6 while.52
  385.8 17.5 fusion.194
  409.7 11.1 reshape.626
  420.8 10.7 copy.551
  431.5 11.7 reshape.627
  454.3 7.6 fusion.140
  462.0 15.3 multiply_convert_fusion.3
  527.9 8.5 all-to-all-done.5
  547.2 13.4 all-to-all-done.4
  566.5 14.3 while.53
  596.2 9.1 copy.569
  605.3 10.8 reshape.632
  616.1 10.8 copy.570
  626.9 11.6 reshape.633
  649.3 14.4 multiply_convert_fusion.2
  670.6 9.1 convert_reduce_fusion
  701.2 19.2 all-to-all-done.8
  728.3 39.6 %while.54 = (s32[]{:T(128)}, bf16[4,512,3,64]{1,3,2,0:T(8,128)(2,1)}, bf16[4,512,3,64]{1,3,2,0:T(8,128)(2,1)}, bf16[4,512,3,64]{1,3,2,0:T(8,128)(2,1)}, bf16[4,5...) while((s32[]{:T(128)}, ...), condition=%wide.region_22.23_spmd, body=%wide.region_20.22_spmd.sunk | while | flops 513243648 | bytes 28757124 | solution.py:267
  776.8 23.0 %all-to-all-done.9 = bf16[4,512,1,192]{3,0,2,1:T(4,128)(2,1)} async-done(((bf16[4,512,1,192]{3,0,2,1:T(4,128)(2,1)}), bf16[4,512,1,192]{3,0,2,1:T(4,128)(2,1)}, u32[]{:S(2)}, u32[]{:S(2)}) %all-to-all-start.9) | async-done | bytes 786464 | tf_op jit(solution)/shard_map/all_to_all | solution.py:272
  806.6 23.0 %all-to-all-done.10 = bf16[4,512,1,192]{3,0,2,1:T(4,128)(2,1)} async-done(((bf16[4,512,1,192]{3,0,2,1:T(4,128)(2,1)}), bf16[4,512,1,192]{3,0,2,1:T(4,128)(2,1)}, u32[]{:S(2)}, u32[]{:S(2)}) %all-to-all-start.10) | async-done | bytes 786464 | tf_op jit(solution)/shard_map/all_to_all | solution.py:275
  848.1 11.1 all-to-all-done.11
  869.8 9.9 convert_reduce_fusion.1
  902.5 16.2 all-to-all-done.12
  926.6 30.5 %while.55 = (s32[]{:T(128)}, bf16[4,512,3,64]{1,3,2,0:T(8,128)(2,1)}, bf16[4,512,3,64]{1,3,2,0:T(8,128)(2,1)}, bf16[4,512,3,64]{1,3,2,0:T(8,128)(2,1)}, bf16[4,5...) while((s32[]{:T(128)}, ...), condition=%wide.region_29.30_spmd, body=%wide.region_27.29_spmd.sunk | while | flops 513243648 | bytes 28757124 | solution.py:267
  973.0 13.3 reshape.583
  986.3 16.5 copy.625
  1007.9 14.7 reshape.585
  1022.7 11.3 copy.627
  1060.0 9.0 all-to-all-done.15
  1075.9 13.5 reshape.575
  1089.5 16.5 copy.611
  1107.2 15.0 reshape.577
  1122.1 11.4 copy.613
  1202.4 10.7 constant_dynamic-update-slice_fusion.7
  1213.1 10.8 constant_dynamic-update-slice_fusion.6
  1234.9 10.6 constant_dynamic-update-slice_fusion.1
  1245.5 10.6 constant_dynamic-update-slice_fusion
  1256.2 51.8 %gather_fusion.1 = f32[384,192,192]{2,1,0:T(8,128)} fusion(f32[384,192,192]{2,1,0:T(8,128)} %constant_dynamic-update-slice_fusion, s32[1024]{0:T(1024)S(1)} %copy-done.111), kind=kCustom, calls=%fused_computation.1 | custom fusion | bytes 113247744 | tf_op jit(solution)/shard_map/gather | solution.py:379
  1308.0 66.7 %copy.628 = f32[384,192,192]{0,2,1:T(8,128)} copy(f32[384,192,192]{2,1,0:T(8,128)} %gather_fusion.1) | data formatting | bytes 113246208 | tf_op jit(solution)/shard_map/gather | solution.py:379
  1374.7 54.9 %copy.696 = f32[384,36864]{1,0:T(8,128)} copy(f32[384,36864]{0,1:T(8,128)} %bitcast.555) | data formatting | bytes 113246208
  1434.2 9.1 broadcast_multiply_fusion.1
  1443.3 309.7 %reduce-scatter.4.cloned.1.call-done = f32[48,36864]{1,0:T(8,128)} async-done(((f32[384,36864]{1,0:T(8,128)}), f32[48,36864]{1,0:T(8,128)}) %reduce-scatter.4.cloned.1.call-update) | async-done | bytes 7077904 | tf_op jit(solution)/shard_map/reduce_scatter | solution.py:380
  1776.2 9.6 reshape.593
  1785.7 9.6 reshape.589
  1795.3 9.6 reshape.590
  1804.9 9.5 mul.425
  1814.5 9.7 mul.428
  1840.2 39.3 %all-reduce.5.cloned.1.call-done = f32[2,9216]{1,0:T(2,128)} async-done(((f32[2,9216]{1,0:T(2,128)}), f32[2,9216]{1,0:T(2,128)}) %all-reduce.5.cloned.1.call-update) | async-done | bytes 73744 | tf_op jit(solution)/shard_map/psum | solution.py:382
  1881.3 175.1 %all-reduce.3.cloned.1.call-done = bf16[48,192,192]{1,2,0:T(8,128)(2,1)} async-done(((bf16[48,192,192]{1,2,0:T(8,128)(2,1)}), bf16[48,192,192]{1,2,0:T(8,128)(2,1)}) %all-reduce.3.cloned.1.call-update) | async-done | bytes 3538960 | tf_op jit(solution)/shard_map/psum | solution.py:381
  2056.3 14.2 fusion.203
  2070.5 23.4 %fusion.114 = (f32[48,192,192]{2,1,0:T(8,128)}, f32[48,192,192]{2,1,0:T(8,128)}) fusion(f32[48,192,192]{2,1,0:T(8,128)} %mul.428, f32[48,192,192]{2,1,0:T(8,128)} %mul.425, f32[48,192,192]{1,2,0:T(8,128)S(1)} %fusion.203, f32[48,192,192]{2,1,0:T(8,128)} %reshape.590), kind=kOutput, calls=%fused_computation.127 | convolution fusion | flops 4083941376 | bytes 42467328 | tf_op jit(solution)/shard_map/sik,skl->sil/dot_general | solution.py:391
  2093.9 9.5 reshape.591
  2103.4 22.3 %fusion.115 = f32[48,192,192]{1,2,0:T(8,128)} fusion(f32[48,192,192]{2,1,0:T(8,128)} %reshape.589, f32[48,192,192]{2,1,0:T(8,128)} %get-tuple-element.314, f32[48,192,192]{2,1,0:T(8,128)} %get-tuple-element.315), kind=kOutput, calls=%fused_computation.129 | convolution fusion | flops 4083941376 | bytes 28311552 | tf_op jit(solution)/shard_map/sij,sjk->sik/dot_general | solution.py:397
  2125.7 9.7 reshape.592
  2135.4 18.5 multiply_subtract_fusion
  2153.8 9.5 reshape.594
  (612 shorter events, 571.4 us)
Async XLA Ops:
  7.2 146.6 %all-gather.2.cloned.1.call-start = ((), (), s32[]{:S(2)}) async-start(), calls=%async_computation.17 | async-start | bytes 31850496 | tf_op jit(solution)/shard_map/all_gather | solution.py:346
  17.3 437.0 %copy-start.83 = (f32[768]{0:T(1024)}, f32[768]{0:T(1024)S(1)}, u32[]{:S(2)}) copy-start(f32[768]{0:T(1024)S(1)} %get-tuple-element.214) | copy-start | bytes 9220
  283.1 25.1 %all-to-all-start = ((bf16[4,128,4,192]{1,3,0,2:T(8,128)(2,1)}), bf16[4,128,4,192]{1,3,0,2:T(8,128)(2,1)S(1)}, u32[]{:S(2)}, u32[]{:S(2)}) async-start(bf16[4,128,4,192]{1,3,0,2:T(8,128)(2,1)} %copy.537), calls=%async_computation | async-start | bytes 1572864 | tf_op jit(solution)/shard_map/all_to_all | solution.py:125
  308.2 23.9 %all-to-all-start.1 = ((bf16[4,128,4,192]{1,3,0,2:T(8,128)(2,1)}), bf16[4,128,4,192]{1,3,0,2:T(8,128)(2,1)}, u32[]{:S(2)}, u32[]{:S(2)}) async-start(bf16[4,128,4,192]{1,3,0,2:T(8,128)(2,1)} %copy.540), calls=%async_computation.1 | async-start | bytes 1572864 | tf_op jit(solution)/shard_map/all_to_all | solution.py:123
  332.1 23.3 %all-to-all-start.2 = ((bf16[4,128,4,192]{1,3,0,2:T(8,128)(2,1)}), bf16[4,128,4,192]{1,3,0,2:T(8,128)(2,1)S(1)}, u32[]{:S(2)}, u32[]{:S(2)}) async-start(bf16[4,128,4,192]{1,3,0,2:T(8,128)(2,1)} %copy.543), calls=%async_computation.2 | async-start | bytes 1572864 | tf_op jit(solution)/shard_map/all_to_all | solution.py:124
  370.2 12.5 copy-start.5
  370.2 12.5 copy-start.7
  372.9 76.7 %all-to-all-start.3 = ((bf16[4,512,1,192]{3,0,2,1:T(4,128)(2,1)}), bf16[4,512,1,192]{3,0,2,1:T(4,128)(2,1)}, u32[]{:S(2)}, u32[]{:S(2)}) async-start(bf16[4,512,1,192]{3,0,2,1:T(4,128)(2,1)} %copy.545), calls=%async_computation.3 | async-start | bytes 2097152 | tf_op jit(solution)/shard_map/all_to_all | solution.py:152
  378.9 83.1 %copy-start.80 = (f32[1,3072]{1,0:T(1,128)}, f32[1,3072]{1,0:T(1,128)S(1)}, u32[]{:S(2)}) copy-start(f32[1,3072]{1,0:T(1,128)S(1)} %get-tuple-element.318) | copy-start | bytes 36868
  385.8 66.4 %copy-start.49 = (bf16[768,768,1]{1,0,2:T(8,128)(2,1)}, bf16[768,768,1]{1,0,2:T(8,128)(2,1)S(1)}, u32[]{:S(2)}) copy-start(bf16[768,768,1]{1,0,2:T(8,128)(2,1)S(1)} %reshape.625) | copy-start | bytes 3538948
  431.5 11.7 copy-start.45
  453.9 23.4 %copy-start = (f32[4,128,768]{2,1,0:T(8,128)}, f32[4,128,768]{2,1,0:T(8,128)S(1)}, u32[]{:S(2)}) copy-start(f32[4,128,768]{2,1,0:T(8,128)S(1)} %get-tuple-element.320) | copy-start | bytes 4718596
  453.9 23.4 %copy-start.89 = (f32[4,128]{1,0:T(4,128)}, f32[4,128]{1,0:T(4,128)S(1)}, u32[]{:S(2)}) copy-start(f32[4,128]{1,0:T(4,128)S(1)} %broadcast_multiply_fusion.13) | copy-start | bytes 6148
  453.9 23.4 %slice-start.4 = ((s8[4718592]{0:T(1024)(128)(4,1)}), s8[4194304]{0:T(1024)(128)(4,1)S(1)}, s32[]{:S(2)}) async-start(s8[4718592]{0:T(1024)(128)(4,1)} %bitcast.606), calls=%async_computation.25 | async-start | bytes 8388608
  454.3 23.1 %copy-start.92 = (f32[4,128]{1,0:T(4,128)}, f32[4,128]{1,0:T(4,128)S(1)}, u32[]{:S(2)}) copy-start(f32[4,128]{1,0:T(4,128)S(1)} %add_rsqrt_fusion.3) | copy-start | bytes 6148
  454.3 23.1 %slice-start.5 = ((s8[4718592]{0:T(1024)(128)(4,1)}), s8[524288]{0:T(1024)(128)(4,1)S(1)}, s32[]{:S(2)}) async-start(s8[4718592]{0:T(1024)(128)(4,1)} %bitcast.606), calls=%async_computation.26 | async-start | bytes 1048576
  461.9 15.4 copy-start.42
  462.0 15.4 copy-start.84
  462.0 15.4 copy-start.118
  483.5 9.8 copy-start.44
  487.9 24.5 %all-to-all-start.6 = ((bf16[4,128,4,192]{1,3,0,2:T(8,128)(2,1)}), bf16[4,128,4,192]{1,3,0,2:T(8,128)(2,1)}, u32[]{:S(2)}, u32[]{:S(2)}) async-start(bf16[4,128,4,192]{1,3,0,2:T(8,128)(2,1)} %copy.562), calls=%async_computation.6 | async-start | bytes 1572864 | tf_op jit(solution)/shard_map/all_to_all | solution.py:124
  502.6 14.1 copy-start.43
  512.4 23.9 %all-to-all-start.5 = ((bf16[4,128,4,192]{1,3,0,2:T(8,128)(2,1)}), bf16[4,128,4,192]{1,3,0,2:T(8,128)(2,1)}, u32[]{:S(2)}, u32[]{:S(2)}) async-start(bf16[4,128,4,192]{1,3,0,2:T(8,128)(2,1)} %copy.558), calls=%async_computation.5 | async-start | bytes 1572864 | tf_op jit(solution)/shard_map/all_to_all | solution.py:123
  536.4 24.2 %all-to-all-start.4 = ((bf16[4,128,4,192]{1,3,0,2:T(8,128)(2,1)}), bf16[4,128,4,192]{1,3,0,2:T(8,128)(2,1)}, u32[]{:S(2)}, u32[]{:S(2)}) async-start(bf16[4,128,4,192]{1,3,0,2:T(8,128)(2,1)} %copy.554), calls=%async_computation.4 | async-start | bytes 1572864 | tf_op jit(solution)/shard_map/all_to_all | solution.py:125
  580.8 11.4 copy-start.9
  580.8 11.4 copy-start.10
  583.5 54.9 %all-to-all-start.7 = ((bf16[4,512,1,192]{3,0,2,1:T(4,128)(2,1)}), bf16[4,512,1,192]{3,0,2,1:T(4,128)(2,1)}, u32[]{:S(2)}, u32[]{:S(2)}) async-start(bf16[4,512,1,192]{3,0,2,1:T(4,128)(2,1)} %copy.564), calls=%async_computation.7 | async-start | bytes 2097152 | tf_op jit(solution)/shard_map/all_to_all | solution.py:152
  644.3 218.8 %copy-start.3 = (f32[4,128,768]{2,1,0:T(8,128)}, f32[4,128,768]{2,1,0:T(8,128)S(1)}, u32[]{:S(2)}) copy-start(f32[4,128,768]{2,1,0:T(8,128)S(1)} %get-tuple-element.325) | copy-start | bytes 4718596
  644.4 19.4 slice-start.6
  644.7 19.0 slice-start.7
  649.3 14.5 copy-start.115
  670.6 9.1 copy-start.68
  696.2 24.3 %all-to-all-start.8 = ((bf16[4,128,4,192]{1,3,0,2:T(8,128)(2,1)}), bf16[4,128,4,192]{1,3,0,2:T(8,128)(2,1)}, u32[]{:S(2)}, u32[]{:S(2)}) async-start(bf16[4,128,4,192]{1,3,0,2:T(8,128)(2,1)} %copy.572), calls=%async_computation.8 | async-start | bytes 1572864 | tf_op jit(solution)/shard_map/all_to_all | solution.py:234
  770.2 29.6 %all-to-all-start.9 = ((bf16[4,512,1,192]{3,0,2,1:T(4,128)(2,1)}), bf16[4,512,1,192]{3,0,2,1:T(4,128)(2,1)}, u32[]{:S(2)}, u32[]{:S(2)}) async-start(bf16[4,512,1,192]{3,0,2,1:T(4,128)(2,1)} %copy.574), calls=%async_computation.9 | async-start | bytes 2097152 | tf_op jit(solution)/shard_map/all_to_all | solution.py:272
  799.8 29.8 %all-to-all-start.10 = ((bf16[4,512,1,192]{3,0,2,1:T(4,128)(2,1)}), bf16[4,512,1,192]{3,0,2,1:T(4,128)(2,1)}, u32[]{:S(2)}, u32[]{:S(2)}) async-start(bf16[4,512,1,192]{3,0,2,1:T(4,128)(2,1)} %copy.578), calls=%async_computation.10 | async-start | bytes 2097152 | tf_op jit(solution)/shard_map/all_to_all | solution.py:275
  829.6 29.6 %all-to-all-start.11 = ((bf16[4,512,1,192]{3,0,2,1:T(4,128)(2,1)}), bf16[4,512,1,192]{3,0,2,1:T(4,128)(2,1)}, u32[]{:S(2)}, u32[]{:S(2)}) async-start(bf16[4,512,1,192]{3,0,2,1:T(4,128)(2,1)} %copy.582), calls=%async_computation.11 | async-start | bytes 2097152 | tf_op jit(solution)/shard_map/all_to_all | solution.py:278
  863.2 16.5 slice-start.2
  869.7 9.9 copy-start.71
  869.7 9.9 copy-start.1
  869.7 9.9 slice-start.3
  869.7 9.9 copy-start.85
  869.7 9.9 copy-start.90
  869.7 9.9 copy-start.93
  894.7 23.9 %all-to-all-start.12 = ((bf16[4,128,4,192]{1,3,0,2:T(8,128)(2,1)}), bf16[4,128,4,192]{1,3,0,2:T(8,128)(2,1)}, u32[]{:S(2)}, u32[]{:S(2)}) async-start(bf16[4,128,4,192]{1,3,0,2:T(8,128)(2,1)} %copy.587), calls=%async_computation.12 | async-start | bytes 1572864 | tf_op jit(solution)/shard_map/all_to_all | solution.py:234
  902.5 24.1 %copy-start.6 = (bf16[4,512,3,64]{1,3,2,0:T(8,128)(2,1)S(1)}, bf16[4,512,3,64]{1,3,2,0:T(8,128)(2,1)}, u32[]{:S(2)}) copy-start(bf16[4,512,3,64]{1,3,2,0:T(8,128)(2,1)} %copy-done.5) | copy-start | bytes 2359300
  902.5 24.1 %copy-start.8 = (bf16[4,512,3,64]{1,3,2,0:T(8,128)(2,1)S(1)}, bf16[4,512,3,64]{1,3,2,0:T(8,128)(2,1)}, u32[]{:S(2)}) copy-start(bf16[4,512,3,64]{1,3,2,0:T(8,128)(2,1)} %copy-done.7) | copy-start | bytes 2359300
  959.6 79.5 %all-to-all-start.13 = ((bf16[4,512,1,192]{3,0,2,1:T(4,128)(2,1)}), bf16[4,512,1,192]{3,0,2,1:T(4,128)(2,1)}, u32[]{:S(2)}, u32[]{:S(2)}) async-start(bf16[4,512,1,192]{3,0,2,1:T(4,128)(2,1)} %copy.589), calls=%async_computation.13 | async-start | bytes 2097152 | tf_op jit(solution)/shard_map/all_to_all | solution.py:272
  986.3 16.5 copy-start.59
  986.3 16.5 copy-start.69
  1022.7 11.3 copy-start.32
  1039.1 29.9 %all-to-all-start.15 = ((bf16[4,512,1,192]{3,0,2,1:T(4,128)(2,1)}), bf16[4,512,1,192]{3,0,2,1:T(4,128)(2,1)}, u32[]{:S(2)}, u32[]{:S(2)}) async-start(bf16[4,512,1,192]{3,0,2,1:T(4,128)(2,1)} %copy.599), calls=%async_computation.15 | async-start | bytes 2097152 | tf_op jit(solution)/shard_map/all_to_all | solution.py:278
  1057.6 15.7 copy-start.33
  1069.0 92.5 %all-to-all-start.14 = ((bf16[4,512,1,192]{3,0,2,1:T(4,128)(2,1)}), bf16[4,512,1,192]{3,0,2,1:T(4,128)(2,1)}, u32[]{:S(2)}, u32[]{:S(2)}) async-start(bf16[4,512,1,192]{3,0,2,1:T(4,128)(2,1)} %copy.594), calls=%async_computation.14 | async-start | bytes 2097152 | tf_op jit(solution)/shard_map/all_to_all | solution.py:275
  1073.2 679.8 %reduce-scatter.4.cloned.1.call-start = ((), (), s32[]{:S(2)}) async-start(), calls=%async_computation.20 | async-start | bytes 63700992 | tf_op jit(solution)/shard_map/reduce_scatter | solution.py:380
  1089.5 16.5 copy-start.64
  1122.1 11.4 copy-start.19
  1213.1 10.8 copy-start.22
  1245.5 10.6 copy-start.111
  1429.8 449.6 %all-reduce.5.cloned.1.call-start = ((), (), s32[]{:S(2)}) async-start(), calls=%async_computation.19 | async-start | bytes 147456 | tf_op jit(solution)/shard_map/psum | solution.py:382
  1434.1 622.2 %all-reduce.3.cloned.1.call-start = ((), (), s32[]{:S(2)}) async-start(), calls=%async_computation.18 | async-start | bytes 9437184 | tf_op jit(solution)/shard_map/psum | solution.py:381
  1814.5 9.7 copy-start.14
  1837.7 41.8 %copy-start.74 = (f32[2,9216]{1,0:T(2,128)S(1)}, f32[2,9216]{1,0:T(2,128)}, u32[]{:S(2)}) copy-start(f32[2,9216]{1,0:T(2,128)} %param.31) | copy-start | bytes 221188
  1837.7 41.8 %copy-start.77 = (f32[2,9216]{1,0:T(2,128)S(1)}, f32[2,9216]{1,0:T(2,128)}, u32[]{:S(2)}) copy-start(f32[2,9216]{1,0:T(2,128)} %param.32) | copy-start | bytes 221188
  1837.7 41.8 %copy-start.78 = (f32[2,9216]{1,0:T(2,128)S(1)}, f32[2,9216]{1,0:T(2,128)}, u32[]{:S(2)}) copy-start(f32[2,9216]{1,0:T(2,128)} %param.33) | copy-start | bytes 221188
  (97 other events, 331.4 us)
Sparse Core Ops, SparseCore 0:
  12.5 141.2 all-gather.1
  1429.9 323.0 reduce-scatter.3
  1759.2 120.2 all-reduce.4
  1882.3 174.0 all-reduce.2
where the time goes:
time: 2190 us; the launch traced here: 2180 us
  local copies, waits for them, and re-layouts  883 us (40%)
  waiting for transfers between devices  828 us (38%)
  matrix products  291 us (13%)
  other arithmetic  84.9 us (4%)
  starting transfers between devices  72.2 us (3%)
    reduce_scatter x1, waiting for transfers between devices, local(): owned = lax.psum_scatter(slot_grads, 'dp', scatter_dimension=0, tiled=True)  310 us
    psum x1, waiting for transfers between devices, local(): owned = lax.psum(owned.astype(jnp.bfloat16), 'seq').astype(jnp.float32)  175 us
    reshape x14, local copies, waits for them, and re-layouts, to_blocks(): matrix.reshape(row_size // block_edge, block_edge, col_size // block_edge...  141 us
    all_gather x1, waiting for transfers between devices, local(): lax.all_gather(masters.astype(jnp.bfloat16), 'dp', axis=0, tiled=True)  136 us
    unnamed x294, local copies, waits for them, and re-layouts  121 us
    gather x2, local copies, waits for them, and re-layouts, local(): grad_blocks[inverse_list].reshape(block_total, block_edge * block_edge)  119 us
    reshape x15, local copies, waits for them, and re-layouts, to_matrices(): members.append(tile_set.reshape(row_count, col_count, block_edge, block_e...  77.5 us
    transpose x12, local copies, waits for them, and re-layouts, to_matrices(): members.append(tile_set.reshape(row_count, col_count, block_edge, block_e...  60.3 us
  transfers between devices with their start and end apart: 20, of which 16 were waited for; matrix products, arithmetic and copies ran while one was open for 22% of the time, Pallas kernels for 0%

commit v1 on v0

v1 whole, which is shorter than its diff:
```python
import functools
import jax
import jax.numpy as jnp
from jax import lax
from jax.experimental import pallas as pl
from jax.experimental.pallas import tpu as pltpu
from jax.sharding import PartitionSpec as P

HEADS = 12
HDIM = 64
BLK = 192
LANE = 128
HALF = BLK // 2
PACK = BLK * BLK // LANE
GROUP = 8

norm_eps = 1e-05
beta_one = 0.95
beta_two = 0.95
adam_eps = 1e-08
matrix_rate = 0.02
vector_rate = 0.2
decay_rate = 0.01
step_count = 6
fix_one = 1.0 - beta_one**step_count
fix_two = 1.0 - beta_two**step_count
bf16 = jnp.bfloat16
f32 = jnp.float32


def params(**kw):
    return pltpu.CompilerParams(vmem_limit_bytes=56 * 2**20, **kw)


def low_lanes(rows):
    return lax.broadcasted_iota(jnp.int32, (rows, LANE), 1) < HDIM


def swap(value):
    return pltpu.roll(value, HDIM, 1)


def row_view(array):
    count = array.shape[0]
    padded = -count % GROUP
    if padded:
        array = jnp.pad(array, ((0, padded), (0, 0)))
    groups = (count + padded) // GROUP
    return (
        array.reshape(groups, GROUP, PACK, LANE)
        .transpose(0, 2, 1, 3)
        .reshape(groups, GROUP * PACK, LANE)
    )


def row_unview(array, count):
    groups = array.shape[0]
    return (
        array.reshape(groups, PACK, GROUP, LANE)
        .transpose(0, 2, 1, 3)
        .reshape(groups * GROUP, PACK * LANE)[:count]
    )


def triple(ref, row):
    return [ref[0, pl.ds(row + GROUP * part, HALF, stride=3 * GROUP), :] for part in range(3)]


def put_triple(ref, row, pieces):
    for part, piece in enumerate(pieces):
        ref[0, pl.ds(row + GROUP * part, HALF, stride=3 * GROUP), :] = piece


def to_square(pieces, main_ref, tail_ref):
    first, second, third = pieces
    low = low_lanes(HALF)
    second_s, third_s = swap(second), swap(third)
    main_ref[pl.ds(0, HALF, stride=2), :] = first
    main_ref[pl.ds(1, HALF, stride=2), :] = jnp.where(low, second_s, third_s)
    tail_ref[pl.ds(0, HALF, stride=2), :] = second
    tail_ref[pl.ds(1, HALF, stride=2), :] = third_s


def from_square(main_ref, tail_ref):
    low = low_lanes(HALF)
    even_main = main_ref[pl.ds(0, HALF, stride=2), :]
    odd_main = swap(main_ref[pl.ds(1, HALF, stride=2), :])
    even_tail = tail_ref[pl.ds(0, HALF, stride=2), :]
    odd_tail = swap(tail_ref[pl.ds(1, HALF, stride=2), :])
    return [even_main, jnp.where(low, even_tail, odd_main), jnp.where(low, odd_main, odd_tail)]


def pack_kernel(src_ref, out_ref, main_ref, tail_ref):
    low = low_lanes(HALF)
    for row in range(GROUP):
        spot = row % 2
        main, tail = main_ref.at[spot], tail_ref.at[spot]
        to_square(triple(src_ref, row), main, tail)
        out_ref[row, 0:BLK, :] = main[...].astype(bf16)
        out_ref[row, BLK:PACK, :] = jnp.where(
            low, tail[0:HALF, :], swap(tail[HALF:BLK, :])
        ).astype(bf16)


def pack_blocks(view):
    groups = view.shape[0]
    return pl.pallas_call(
        pack_kernel,
        grid=(groups,),
        in_specs=[pl.BlockSpec((1, GROUP * PACK, LANE), lambda i: (i, 0, 0))],
        out_specs=pl.BlockSpec((GROUP, PACK, LANE), lambda i: (i, 0, 0)),
        out_shape=jax.ShapeDtypeStruct((groups * GROUP, PACK, LANE), bf16),
        scratch_shapes=[pltpu.VMEM((2, BLK, LANE), f32), pltpu.VMEM((2, BLK, LANE), f32)],
        compiler_params=params(),
        name="pack",
    )(view)


def unfold(block):
    fold = block[BLK:PACK, :]
    return block[0:BLK, :], jnp.concatenate([fold[:, :HDIM], fold[:, HDIM:]], axis=0)


def assemble_kernel(cells, owner_ref, *refs):
    out_ref = refs[-1]
    for number, (row, lanes) in enumerate(cells):
        main_a, tail_a = unfold(refs[2 * number][0])
        main_b, tail_b = unfold(refs[2 * number + 1][0])
        rows = pl.ds(row, BLK)
        out_ref[rows, pl.ds(lanes[0], LANE)] = main_a
        out_ref[rows, pl.ds(lanes[1], LANE)] = jnp.concatenate([tail_a, main_b[:, :HDIM]], axis=1)
        out_ref[rows, pl.ds(lanes[2], LANE)] = jnp.concatenate([main_b[:, HDIM:], tail_b], axis=1)


def assemble(gathered, owner_list, shape, tile, cells, block_of):
    grid = (shape[0] // tile[0], shape[1] // tile[1])
    count = 2 * len(cells)

    def spec(which):
        return pl.BlockSpec(
            (1, PACK, LANE), lambda i, j, owner: (owner[block_of(i, j, which)], 0, 0)
        )

    return pl.pallas_call(
        functools.partial(assemble_kernel, cells),
        grid_spec=pltpu.PrefetchScalarGridSpec(
            num_scalar_prefetch=1,
            grid=grid,
            in_specs=[spec(which) for which in range(count)],
            out_specs=pl.BlockSpec(tile, lambda i, j, owner: (i, j)),
        ),
        out_shape=jax.ShapeDtypeStruct(shape, bf16),
        compiler_params=params(),
        name="assemble",
    )(owner_list, *([gathered] * count))


def layer_weights(gathered, owner_list, base, width, inner):
    cols = width // BLK
    inner_cols = inner // BLK
    square = cols * cols
    cells = []
    for matrix in range(3):
        for pair in range(cols // 2):
            cells.append((0, [3 * LANE * (3 * pair + part) + LANE * matrix for part in range(3)]))
    per_matrix = cols

    def block_qkv(i, j, which):
        return base + (which // per_matrix) * square + i * cols + which % per_matrix

    w_qkv = assemble(gathered, owner_list, (width, 3 * width), (BLK, 3 * width), cells, block_qkv)
    plain = []
    for row in range(2):
        for pair in range(cols // 2):
            plain.append(
                (row * BLK, [2 * BLK * pair + LANE * part for part in range(3)])
            )

    def block_plain(start, row_blocks):
        def block(i, j, which):
            return start + (2 * i + which // cols) * row_blocks + cols * j + which % cols

        return block

    tile = (2 * BLK, width)
    w_out = assemble(
        gathered, owner_list, (width, width), tile, plain, block_plain(base + 3 * square, cols)
    )
    up_base = base + 4 * square
    w_up = assemble(
        gathered, owner_list, (width, inner), tile, plain, block_plain(up_base, inner_cols)
    )
    down_base = up_base + cols * inner_cols
    w_down = assemble(
        gathered, owner_list, (inner, width), tile, plain, block_plain(down_base, cols)
    )
    return w_qkv, w_out, w_up, w_down
def dot(left, right, left_dim=1, right_dim=0):
    return lax.dot_general(
        left, right, (((left_dim,), (right_dim,)), ((), ())), preferred_element_type=f32
    )


def head_masks():
    lane = lax.broadcasted_iota(jnp.int32, (1, LANE), 1)
    first = (lane < HDIM).astype(f32)
    return [first.astype(bf16), (1.0 - first).astype(bf16)]


def attend_kernel(scale, qkv_ref, mix_ref, lse_ref):
    length = qkv_ref.shape[0]
    query, keys, values = (qkv_ref[:, pl.ds(LANE * part, LANE)] for part in range(3))
    mixed, logs = [], []
    for mask in head_masks():
        scores = dot(query * mask, keys, 1, 1) * scale
        highest = jnp.max(scores, axis=1, keepdims=True)
        raised = jnp.exp(scores - highest)
        total = jnp.sum(raised, axis=1, keepdims=True)
        probs = raised * (1.0 / total)
        mixed.append(dot(probs.astype(bf16), values))
        logs.append(highest + jnp.log(total))
    low = low_lanes(length)
    mix_ref[...] = jnp.where(low, mixed[0], mixed[1]).astype(bf16)
    lse_ref[...] = jnp.where(low, logs[0], logs[1])


def attend(qkv, scale):
    length, wide = qkv.shape
    pairs = wide // (3 * LANE)
    return pl.pallas_call(
        functools.partial(attend_kernel, scale),
        grid=(pairs,),
        in_specs=[pl.BlockSpec((length, 3 * LANE), lambda i: (0, i))],
        out_specs=[pl.BlockSpec((length, LANE), lambda i: (0, i))] * 2,
        out_shape=[
            jax.ShapeDtypeStruct((length, wide // 3), bf16),
            jax.ShapeDtypeStruct((length, wide // 3), f32),
        ],
        compiler_params=params(),
        name="attend",
    )(qkv)


def attend_back_kernel(scale, qkv_ref, lse_ref, grad_ref, out_ref):
    length = qkv_ref.shape[0]
    query, keys, values = (qkv_ref[:, pl.ds(LANE * part, LANE)] for part in range(3))
    grad = grad_ref[...]
    parts = []
    for number, mask in enumerate(head_masks()):
        scores = dot(query * mask, keys, 1, 1) * scale
        probs = jnp.exp(scores - lse_ref[:, number * HDIM : number * HDIM + 1])
        grad_probs = dot(grad * mask, values, 1, 1)
        centre = jnp.sum(probs * grad_probs, axis=1, keepdims=True)
        grad_scores = (probs * (grad_probs - centre)).astype(bf16)
        parts.append(
            (
                dot(grad_scores, keys) * scale,
                dot(grad_scores, query, 0, 0) * scale,
                dot(probs.astype(bf16), grad, 0, 0),
            )
        )
    low = low_lanes(length)
    for part in range(3):
        out_ref[:, pl.ds(LANE * part, LANE)] = jnp.where(
            low, parts[0][part], parts[1][part]
        ).astype(bf16)


def attend_back(qkv, lse, grad, scale):
    length, wide = qkv.shape
    pairs = wide // (3 * LANE)
    return pl.pallas_call(
        functools.partial(attend_back_kernel, scale),
        grid=(pairs,),
        in_specs=[
            pl.BlockSpec((length, 3 * LANE), lambda i: (0, i)),
            pl.BlockSpec((length, LANE), lambda i: (0, i)),
            pl.BlockSpec((length, LANE), lambda i: (0, i)),
        ],
        out_specs=pl.BlockSpec((length, 3 * LANE), lambda i: (0, i)),
        out_shape=jax.ShapeDtypeStruct((length, wide), bf16),
        compiler_params=params(),
        name="attend_back",
    )(qkv, lse, grad)


def weight_grad_kernel(lanes_of, block_of, panel, steps, rows_ref, left_ref, right_ref, *refs):
    out_ref, stage_ref, sems = refs[-3:]
    i, j = pl.program_id(0), pl.program_id(1)
    step = i * pl.num_programs(1) + j
    spot = lax.rem(step, 2)
    pairs = panel // (2 * BLK)
    count = 4 * pairs

    def copy(which, slot, row):
        return pltpu.make_async_copy(
            stage_ref.at[slot, which], out_ref.at[row], sems.at[slot, which]
        )

    @pl.when(step >= 2)
    def _():
        for which in range(count):
            copy(which, spot, 0).wait()

    left = left_ref[:, pl.ds(pl.multiple_of(2 * BLK * i, LANE), 2 * BLK)]
    low_top, low_all = low_lanes(HALF), low_lanes(BLK)
    for pair in range(pairs):
        right = jnp.concatenate(
            [
                right_ref[:, pl.ds(pl.multiple_of(lanes_of(j, 3 * pair + part), LANE), LANE)]
                for part in range(3)
            ],
            axis=1,
        )
        product = dot(left, right, 0, 0)
        for half in range(2):
            tile = product[half * BLK : (half + 1) * BLK, :]
            first, second, third = (tile[:, LANE * part : LANE * (part + 1)] for part in range(3))
            which = half * 2 * pairs + 2 * pair
            stage_ref[spot, which, 0:BLK, :] = first.astype(bf16)
            stage_ref[spot, which, BLK:PACK, :] = jnp.where(
                low_top, second[0:HALF, :], swap(second[HALF:BLK, :])
            ).astype(bf16)
            stage_ref[spot, which + 1, 0:BLK, :] = swap(
                jnp.where(low_all, third, second)
            ).astype(bf16)
            stage_ref[spot, which + 1, BLK:PACK, :] = jnp.where(
                low_top, swap(third[0:HALF, :]), third[HALF:BLK, :]
            ).astype(bf16)
    for which in range(count):
        block = block_of(i, j, which // (2 * pairs), which % (2 * pairs))
        copy(which, spot, rows_ref[block]).start()

    @pl.when(step == steps - 1)
    def _():
        for which in range(count):
            copy(which, spot, 0).wait()
            if steps > 1:
                copy(which, 1 - spot, 0).wait()


def weight_grad(slots, slot_shape, rows, left, right, grid, panel, lanes_of, block_of):
    steps = grid[0] * grid[1]
    count = 4 * (panel // (2 * BLK))
    whole = [pl.BlockSpec(left.shape, lambda i, j, s: (0, 0)), pl.BlockSpec(right.shape, lambda i, j, s: (0, 0))]
    extra, aliases = [], {}
    if slots is not None:
        extra = [slots]
        aliases = {3: 0}
    return pl.pallas_call(
        functools.partial(weight_grad_kernel, lanes_of, block_of, panel, steps),
        grid_spec=pltpu.PrefetchScalarGridSpec(
            num_scalar_prefetch=1,
            grid=grid,
            in_specs=whole + [pl.BlockSpec(memory_space=pl.ANY)] * len(extra),
            out_specs=pl.BlockSpec(memory_space=pl.ANY),
            scratch_shapes=[
                pltpu.VMEM((2, count, PACK, LANE), bf16),
                pltpu.SemaphoreType.DMA((2, count)),
            ],
        ),
        out_shape=jax.ShapeDtypeStruct(slot_shape, bf16),
        input_output_aliases=aliases,
        compiler_params=params(),
        name="weight_grad",
    )(rows, left, right, *extra)


def plain_grad(slots, slot_shape, rows, left, right, base, width):
    cols = right.shape[1] // BLK
    per = width // BLK
    return weight_grad(
        slots,
        slot_shape,
        rows,
        left,
        right,
        (left.shape[1] // (2 * BLK), right.shape[1] // width),
        width,
        lambda j, piece: j * width + piece * LANE,
        lambda i, j, half, col: base + (2 * i + half) * cols + j * per + col,
    )


def qkv_grad(slots, slot_shape, rows, left, right, base, width):
    per = width // BLK
    return weight_grad(
        slots,
        slot_shape,
        rows,
        left,
        right,
        (width // (2 * BLK), 3),
        width,
        lambda j, piece: 3 * LANE * piece + LANE * j,
        lambda i, j, half, col: base + j * per * per + (2 * i + half) * per + col,
    )


def soap_kernel(
    masters_ref, one_ref, two_ref, left_ref, right_ref, grad_ref,
    one_out, two_out, masters_out, copies_out, left_sq, right_sq, work, full,
):
    def square(refs):
        return jnp.concatenate([refs[0][...], refs[1][:, :HDIM]], axis=1).astype(bf16)

    def keep(refs, value):
        refs[0][...] = value[:, :LANE]
        refs[1][:, :HDIM] = value[:, LANE:]

    for row in range(GROUP):
        spot = row % 2
        left_refs = [left_sq.at[spot, 0], left_sq.at[spot, 1]]
        right_refs = [right_sq.at[spot, 0], right_sq.at[spot, 1]]
        refs = [work.at[spot, 0], work.at[spot, 1]]
        to_square(triple(left_ref, row), *left_refs)
        to_square(triple(right_ref, row), *right_refs)
        left, right = square(left_refs), square(right_refs)
        main, tail = unfold(grad_ref[row])
        grad = jnp.concatenate([main, tail], axis=1)
        rotated = dot(dot(left, grad, 0, 0).astype(bf16), right)
        keep(refs, rotated)
        pieces = from_square(*refs)
        ones, twos = triple(one_ref, row), triple(two_ref, row)
        ones = [beta_one * old + (1.0 - beta_one) * new for old, new in zip(ones, pieces)]
        twos = [beta_two * old + (1.0 - beta_two) * new * new for old, new in zip(twos, pieces)]
        put_triple(one_out, row, ones)
        put_triple(two_out, row, twos)
        moves = [
            (one / fix_one) / (jnp.sqrt(two / fix_two) + adam_eps) for one, two in zip(ones, twos)
        ]
        to_square(moves, *refs)
        restored = dot(dot(left, square(refs)).astype(bf16), right, 1, 1)
        keep(refs, restored)
        pieces = from_square(*refs)
        old = triple(masters_ref, row)
        new = [
            value - matrix_rate * (step + decay_rate * value) for value, step in zip(old, pieces)
        ]
        put_triple(masters_out, row, new)
        put_triple(full, row, new)
    copies_out[0] = full[0].astype(bf16)


def soap(views, grads):
    groups = views[0].shape[0]
    view_spec = pl.BlockSpec((1, GROUP * PACK, LANE), lambda i: (i, 0, 0))
    shape = (groups, GROUP * PACK, LANE)
    square = pltpu.VMEM((2, 2, BLK, LANE), f32)
    return pl.pallas_call(
        soap_kernel,
        grid=(groups,),
        in_specs=[view_spec] * 5 + [pl.BlockSpec((GROUP, PACK, LANE), lambda i: (i, 0, 0))],
        out_specs=[view_spec] * 4,
        out_shape=[jax.ShapeDtypeStruct(shape, f32)] * 3 + [jax.ShapeDtypeStruct(shape, bf16)],
        scratch_shapes=[square, square, square, pltpu.VMEM((1, GROUP * PACK, LANE), f32)],
        compiler_params=params(),
        name="soap",
    )(*views, grads)


def norm_forward(hidden, gain, shift):
    center = hidden - jnp.mean(hidden, axis=-1, keepdims=True)
    spread = jnp.mean(center * center, axis=-1, keepdims=True)
    inverse = lax.rsqrt(spread + norm_eps)
    unit = center * inverse
    return (unit * gain + shift, unit, inverse)


def norm_backward(incoming, unit, inverse, gain):
    scaled = incoming * gain
    grad_hidden = inverse * (
        scaled
        - jnp.mean(scaled, axis=-1, keepdims=True)
        - unit * jnp.mean(scaled * unit, axis=-1, keepdims=True)
    )
    return (grad_hidden, jnp.sum(incoming * unit, axis=0), jnp.sum(incoming, axis=0))


def gelu_exact(value):
    return jax.nn.gelu(value, approximate=False)


def unpack(vector, width):
    return [vector[number * width : (number + 1) * width] for number in range(8)] + [
        vector[8 * width :]
    ]


def forward_layer(hidden, matrices, pieces, scale):
    w_qkv, w_out, w_up, w_down = matrices
    bias_q, bias_v, bias_out, bias_down, gain_one, shift_one, gain_two, shift_two, bias_up = pieces
    hid_low = hidden.astype(bf16)
    bias_q = bias_q.reshape(-1, LANE)
    bias_qkv = jnp.stack([bias_q, jnp.zeros_like(bias_q), bias_v.reshape(-1, LANE)], axis=1)
    qkv = (dot(hid_low, w_qkv) + bias_qkv.reshape(-1)).astype(bf16)
    mixed, lse = attend(qkv, scale)
    branch = dot(mixed, w_out) + bias_out
    normed, unit_one, inv_one = norm_forward(hidden + branch, gain_one, shift_one)
    norm_low = normed.astype(bf16)
    pre_act = dot(norm_low, w_up) + bias_up
    act_low = gelu_exact(pre_act).astype(bf16)
    down = dot(act_low, w_down) + bias_down
    result, unit_two, inv_two = norm_forward(normed + down, gain_two, shift_two)
    kept = (
        hid_low, qkv, lse, mixed, unit_one, inv_one, norm_low, pre_act, act_low, unit_two, inv_two
    )
    return (result, kept)


def backward_layer(incoming, matrices, pieces, kept, scale, slots, slot_shape, rows, base):
    w_qkv, w_out, w_up, w_down = matrices
    gain_one, gain_two = pieces[4], pieces[6]
    hid_low, qkv, lse, mixed, unit_one, inv_one, norm_low, pre_act, act_low, unit_two, inv_two = kept
    width = mixed.shape[1]
    square = (width // BLK) ** 2
    up_count = act_low.shape[1] // BLK * (width // BLK)
    grad_two, gain_two_g, shift_two_g = norm_backward(incoming, unit_two, inv_two, gain_two)
    down_low = grad_two.astype(bf16)
    slots = plain_grad(
        slots, slot_shape, rows, act_low, down_low, base + 4 * square + up_count, width
    )
    grad_act = dot(down_low, w_down, 1, 1)
    (grad_pre,) = jax.vjp(gelu_exact, pre_act)[1](grad_act)
    up_low = grad_pre.astype(bf16)
    slots = plain_grad(slots, slot_shape, rows, norm_low, up_low, base + 4 * square, width)
    grad_norm = grad_two + dot(up_low, w_up, 1, 1)
    grad_one, gain_one_g, shift_one_g = norm_backward(grad_norm, unit_one, inv_one, gain_one)
    out_low = grad_one.astype(bf16)
    slots = plain_grad(slots, slot_shape, rows, mixed, out_low, base + 3 * square, width)
    grad_mix = dot(out_low, w_out, 1, 1).astype(bf16)
    grad_qkv = attend_back(qkv, lse, grad_mix, scale)
    slots = qkv_grad(slots, slot_shape, rows, hid_low, grad_qkv, base, width)
    grad_hidden = grad_one + dot(grad_qkv, w_qkv, 1, 1)

    def total(array):
        return jnp.sum(array, axis=0, dtype=f32)

    bias_qkv = total(grad_qkv).reshape(-1, 3, LANE)
    vec_grad = jnp.concatenate(
        [
            bias_qkv[:, 0].reshape(-1),
            bias_qkv[:, 2].reshape(-1),
            total(out_low),
            total(down_low),
            gain_one_g,
            shift_one_g,
            gain_two_g,
            shift_two_g,
            total(up_low),
        ]
    )
    return grad_hidden, slots, vec_grad


def swap_in(array):
    return lax.all_to_all(array, "seq", split_axis=0, concat_axis=1, tiled=True)


def swap_out(array):
    return lax.all_to_all(array, "seq", split_axis=1, concat_axis=0, tiled=True)


def local(
    tokens,
    cotangent,
    tok_weight,
    mask_count,
    owner_list,
    masters,
    moment_one,
    moment_two,
    left_basis,
    right_basis,
    vectors,
    vec_moment_one,
    vec_moment_two,
):
    data_parts = lax.axis_size("dp")
    seq_count, local_len, width = tokens.shape
    layer_count = vectors.shape[0]
    inner = vectors.shape[-1] - 8 * width
    owned_count = masters.shape[0]
    block_total = owner_list.shape[0]
    scale = HDIM ** (-0.5)

    master_view = row_view(masters)
    packed = pack_blocks(master_view)[:owned_count]
    gathered = lax.all_gather(packed, "dp", axis=0, tiled=True)

    positions = lax.axis_index("seq") * local_len + jnp.arange(local_len, dtype=jnp.int32)
    masked = (positions[None, :] < mask_count[:, None]).astype(f32)
    factor = tok_weight.astype(f32) * (1.0 + masked) * 0.25
    hidden = swap_in(tokens)
    per_seq = hidden.shape[0]
    full_len = hidden.shape[1]
    hidden = hidden.reshape(full_len, width).astype(f32)
    incoming = swap_in(cotangent).reshape(full_len, width).astype(f32)
    incoming = incoming * swap_in(factor).reshape(full_len, 1)

    per_layer = block_total // layer_count
    weights = [
        layer_weights(gathered, owner_list, per_layer * number, width, inner)
        for number in range(layer_count)
    ]
    saved = []
    for number in range(layer_count):
        hidden, kept = forward_layer(
            hidden, weights[number], unpack(vectors[number], width), scale
        )
        saved.append(kept)
    layer_out = swap_out(hidden.astype(bf16).reshape(per_seq, full_len, width))

    chunk = owned_count + 1
    rows = owner_list + owner_list // owned_count
    slot_shape = (data_parts * chunk, PACK, LANE)
    slots = None
    vec_grads = [None] * layer_count
    for number in reversed(range(layer_count)):
        incoming, slots, vec_grads[number] = backward_layer(
            incoming,
            weights[number],
            unpack(vectors[number], width),
            saved[number],
            scale,
            slots,
            slot_shape,
            rows,
            per_layer * number,
        )
    vec_grad = jnp.stack(vec_grads)
    vec_high = vec_grad.astype(bf16)
    vec_low = (vec_grad - vec_high.astype(f32)).astype(bf16)
    vec_slot = jnp.concatenate([vec_high.reshape(-1, LANE), vec_low.reshape(-1, LANE)], axis=0)
    for part in range(data_parts):
        slots = lax.dynamic_update_slice(
            slots, vec_slot[None], (part * chunk + owned_count, 0, 0)
        )
    owned = lax.psum_scatter(slots, "dp", scatter_dimension=0, tiled=True)
    owned = lax.psum(owned, "seq")
    input_grad = swap_out(incoming.reshape(per_seq, full_len, width))

    vec_rows = owned[owned_count].astype(f32)
    half = PACK // 2
    vec_total = (vec_rows[:half] + vec_rows[half:]).reshape(vectors.shape)
    views = [master_view] + [
        row_view(array) for array in (moment_one, moment_two, left_basis, right_basis)
    ]
    extra = views[0].shape[0] * GROUP - chunk
    if extra > 0:
        owned = jnp.pad(owned, ((0, extra), (0, 0), (0, 0)))
    new_one, new_two, new_masters, copies = [
        row_unview(array, owned_count) for array in soap(views, owned)
    ]
    vec_one = beta_one * vec_moment_one + (1.0 - beta_one) * vec_total
    vec_two = beta_two * vec_moment_two + (1.0 - beta_two) * vec_total * vec_total
    new_vectors = vectors - vector_rate * (vec_one / fix_one) / (
        jnp.sqrt(vec_two / fix_two) + adam_eps
    )
    return (
        layer_out, input_grad, new_one, new_two, new_masters, copies, new_vectors, vec_one, vec_two
    )


def solution(mesh):
    rows = P("dp", None)
    tokens = P("dp", "seq", None)
    return jax.shard_map(
        local,
        mesh=mesh,
        in_specs=(tokens, tokens, P("dp", "seq"), P("dp"), P()) + (rows,) * 5 + (P(),) * 3,
        out_specs=(tokens, tokens) + (rows,) * 4 + (P(),) * 3,
        check_vma=False,
    )
```

time: 2190 us -> 865 us (0.39)
  local copies, waits for them, and re-layouts: 883 us -> 18.1 us
  waiting for transfers between devices: 828 us -> 451 us
  Pallas kernels: 0 us -> 217 us
  matrix products: 291 us -> 97.7 us
  other arithmetic: 84.9 us -> 27.2 us
  starting transfers between devices: 72.2 us -> 15.9 us
    reshape x62 -> x5, local copies, waits for them, and re-layouts: 384 us -> 5.18 us  [the longest x1 2.76 us: local(): input_grad = swap_out(incoming.reshape(per_seq, full_len, width))]
    reduce_scatter x1 -> x0, waiting for transfers between devices: 310 us -> none  [local(): owned = lax.psum_scatter(slot_grads, 'dp', scatter_dimension=0, tiled=True)]
    pallas_call x0 -> x22, Pallas kernels: none -> 217 us  [the longest x8 64.7 us: weight_grad(): pl.pallas_call(functools.partial(weight_grad_kernel, lanes_of, block_of,...]
    dot_general x96 -> x16, matrix products: 291 us -> 97.7 us  [dot(): lax.dot_general(left, right, (((left_dim,), (right_dim,)), ((), ())), pre...]
    unnamed x4, waiting for transfers between devices: 0.07 us -> 179 us
    psum x2 -> x1, waiting for transfers between devices: 214 us -> 64 us  [local(): owned = lax.psum(owned, 'seq')]
    gather x3 -> x0, local copies, waits for them, and re-layouts: 145 us -> none  [the longest x2 119 us: local(): grad_blocks[inverse_list].reshape(block_total, block_edge * block_edge)]
    unnamed x294 -> x205, local copies, waits for them, and re-layouts: 121 us -> 10.8 us
  transfers between devices with their start and end apart: 20 -> 7, of which waited for: 16 -> 6; matrix products, arithmetic and copies ran while one was open for 22% -> 3% of each run, Pallas kernels for 0% -> 1%
where the time goes in v1:
time: 865 us; the launch traced here: 854 us
  waiting for transfers between devices  451 us (52%)
  Pallas kernels  217 us (25%)
  matrix products  97.7 us (11%)
  other arithmetic  27.2 us (3%)
  local copies, waits for them, and re-layouts  18.1 us (2%)
  starting transfers between devices  15.9 us (2%)
  between operations  15.8 us (2%)
  blocking collectives  11.7 us (1%)
    unnamed x4, waiting for transfers between devices  179 us
    all_gather x1, waiting for transfers between devices, local(): gathered = lax.all_gather(packed, 'dp', axis=0, tiled=True)  100 us
    dot_general x16, matrix products, dot(): lax.dot_general(left, right, (((left_dim,), (right_dim,)), ((), ())), pre...  97.7 us
    all_to_all x2, waiting for transfers between devices, swap_out(): return lax.all_to_all(array, 'seq', split_axis=1, concat_axis=0, tiled=True)  89.4 us
    pallas_call x8, Pallas kernels, weight_grad(): pl.pallas_call(functools.partial(weight_grad_kernel, lanes_of, block_of,...  64.7 us
    psum x1, waiting for transfers between devices, local(): owned = lax.psum(owned, 'seq')  64 us
    pallas_call x8, Pallas kernels, assemble(): pl.pallas_call(functools.partial(assemble_kernel, cells), grid_spec=pltpu...  55.8 us
    pallas_call x1, Pallas kernels, soap(): pl.pallas_call(soap_kernel, grid=(groups,), in_specs=[view_spec] * 5 + [p...  37.9 us
  transfers between devices with their start and end apart: 7, of which 6 were waited for; matrix products, arithmetic and copies ran while one was open for 3% of the time, Pallas kernels for 1%

profile of v1, /device:TPU:0, one launch (start us, length us, event | category | flops | bytes accessed | tf_op | source)
XLA Modules:
  0.0 853.8 jit_solution(4942087651713868509)
XLA Ops:
  7.2 8.2 pack.1
  15.6 11.7 %all_to_all.58 = f32[4,1,128]{2,1,0:T(1,128)S(1)} all-to-all(f32[4,1,128]{2,1,0:T(1,128)S(1)} %bitcast.176), channel_id=1, replica_groups=mesh['dp'=8,'seq'=4] {'seq'}, dimensions={0} | all-to-all | bytes 4096 | tf_op jit(solution)/shard_map/all_to_all | solution.py:557
  27.3 3.5 all-to-all-start.2
  31.7 18.1 %all-to-all-done.2 = bf16[4,128,768]{2,1,0:T(8,128)(2,1)S(1)} async-done(((bf16[4,128,768]{2,1,0:T(8,128)(2,1)}), bf16[4,128,768]{2,1,0:T(8,128)(2,1)S(1)}, u32[]{:S(2)}, u32[]{:S(2)}) %all-to-all-start.2) | async-done | bytes 786464 | tf_op jit(solution)/shard_map/all_to_all | solution.py:557
  49.8 3.5 all-to-all-start
  55.2 0.9 fusion.16
  56.7 100.1 %all-gather.2.cloned.1.call-done.refs_0_.refs_1_.refs_2_.refs_3_.refs_4_.refs_5_.refs_6_.refs_7_.refs_8_.refs_9_.refs_10_.refs_11_ = bf16[384,288,128]{2,1,0:T(8,128)(2,1)} async-done(((bf16[48,288,128]{2,1,0:T(8,128)(2,1)}), bf16[384,288,128]{2,1,0:T(8,128)(2,1)}) %all-gather.2.cloned.1.call-update) | async-done | bytes 28311568 | tf_op jit(solution)/shard_map/all_gather | solution.py:589
  156.9 6.0 assemble.8
  162.9 5.7 fusion.14.qkv_ref
  168.6 10.0 %attend.2 = (bf16[512,768]{1,0:T(8,128)(2,1)}, f32[512,768]{1,0:T(8,128)}) custom-call(bf16[512,2304]{1,0:T(8,128)(2,1)} %fusion.14.qkv_ref), custom_call_target="tpu_custom_call" | custom-call | tf_op jit(solution)/shard_map/attend/pallas_call | solution.py:230
  178.6 3.5 assemble.9
  182.1 2.1 fusion.29
  185.8 8.7 %assemble.10 = bf16[768,3072]{1,0:T(8,128)(2,1)} custom-call(s32[384]{0:T(512)} %owner_ref.15, bf16[384,288,128]{2,1,0:T(8,128)(2,1)} %all-gather.2.cloned.1.call-done.refs_0_.refs_1_.refs_2_.refs_3_.refs_4_.refs_5_.refs_6_.refs_7_.refs_8_.refs_9_.refs_10_.refs_11_, ...), custom_call_target="tpu_custom_call" | custom-call | tf_op jit(solution)/shard_map/assemble/pallas_call | solution.py:144
  194.5 18.5 %multiply_convert_fusion.1 = (bf16[512,3072]{1,0:T(8,128)(2,1)S(1)}, f32[512,3072]{1,0:T(8,128)}, f32[512,3072]{1,0:T(8,128)}) fusion(f32[3072]{0:T(1024)S(1)} %bitcast.172, bf16[512,768]{1,0:T(8,128)(2,1)S(1)} %fusion.17.left_ref, bf16[768,3072]{1,0:T(8,128)(2,1)} %assemble.10), kind=kOutput, calls=%fused_computation.21 | convolution fusion | flops 2519728128 | bytes 21245952 | tf_op jit(solution)/shard_map/dot_general | solution.py:199
  213.0 9.8 %assemble.11 = bf16[3072,768]{1,0:T(8,128)(2,1)} custom-call(s32[384]{0:T(512)} %owner_ref.15, bf16[384,288,128]{2,1,0:T(8,128)(2,1)} %all-gather.2.cloned.1.call-done.refs_0_.refs_1_.refs_2_.refs_3_.refs_4_.refs_5_.refs_6_.refs_7_.refs_8_.refs_9_.refs_10_.refs_11_, ...), custom_call_target="tpu_custom_call" | custom-call | tf_op jit(solution)/shard_map/assemble/pallas_call | solution.py:144
  222.9 5.1 fusion.30
  229.5 6.2 assemble.12
  235.6 5.4 fusion.12.qkv_ref
  241.1 10.0 %attend.3 = (bf16[512,768]{1,0:T(8,128)(2,1)}, f32[512,768]{1,0:T(8,128)}) custom-call(bf16[512,2304]{1,0:T(8,128)(2,1)} %fusion.12.qkv_ref), custom_call_target="tpu_custom_call" | custom-call | tf_op jit(solution)/shard_map/attend/pallas_call | solution.py:230
  251.1 3.5 assemble.13
  254.6 2.2 fusion.31
  258.3 8.9 %assemble.14 = bf16[768,3072]{1,0:T(8,128)(2,1)} custom-call(s32[384]{0:T(512)} %owner_ref.15, bf16[384,288,128]{2,1,0:T(8,128)(2,1)} %all-gather.2.cloned.1.call-done.refs_0_.refs_1_.refs_2_.refs_3_.refs_4_.refs_5_.refs_6_.refs_7_.refs_8_.refs_9_.refs_10_.refs_11_, ...), custom_call_target="tpu_custom_call" | custom-call | tf_op jit(solution)/shard_map/assemble/pallas_call | solution.py:144
  267.3 18.9 %multiply_convert_fusion = (bf16[512,3072]{1,0:T(8,128)(2,1)S(1)}, f32[512,3072]{1,0:T(8,128)}, f32[512,3072]{1,0:T(8,128)}) fusion(f32[3072]{0:T(1024)S(1)} %bitcast.174, bf16[512,768]{1,0:T(8,128)(2,1)S(1)} %fusion.19.left_ref, bf16[768,3072]{1,0:T(8,128)(2,1)} %assemble.14), kind=kOutput, calls=%fused_computation.8 | convolution fusion | flops 2519728128 | bytes 21245952 | tf_op jit(solution)/shard_map/dot_general | solution.py:199
  286.2 9.4 %assemble.15 = bf16[3072,768]{1,0:T(8,128)(2,1)} custom-call(s32[384]{0:T(512)} %owner_ref.15, bf16[384,288,128]{2,1,0:T(8,128)(2,1)} %all-gather.2.cloned.1.call-done.refs_0_.refs_1_.refs_2_.refs_3_.refs_4_.refs_5_.refs_6_.refs_7_.refs_8_.refs_9_.refs_10_.refs_11_, ...), custom_call_target="tpu_custom_call" | custom-call | tf_op jit(solution)/shard_map/assemble/pallas_call | solution.py:144
  295.8 5.2 fusion.32
  302.1 1.6 convert_reduce_fusion.4
  303.8 7.9 convert_reduce_fusion
  311.7 3.1 multiply_reduce_fusion.1
  316.2 1.7 convolution_convert_fusion.1.grad_ref
  317.9 15.2 %attend_back.2.right_ref = bf16[512,2304]{1,0:T(8,128)(2,1)} custom-call(bf16[512,2304]{1,0:T(8,128)(2,1)} %fusion.12.qkv_ref, f32[512,768]{1,0:T(8,128)} %get-tuple-element.19.lse_ref, bf16[512,768]{1,0:T(8,128)(2,1)} %convolution_convert_fusion.1.grad_ref), custom_call_target="tpu_custom_call" | custom-call | tf_op jit(solution)/shard_map/attend_back/pallas_call | solution.py:272
  333.1 2.1 convert_reduce_fusion.2
  335.3 4.3 multiply_reduce_fusion.2
  340.3 8.2 convert_reduce_fusion.1
  348.6 3.1 multiply_reduce_fusion.3
  351.8 1.7 convert_reduce_fusion.7
  353.5 1.7 convolution_convert_fusion.grad_ref
  355.2 15.0 %attend_back.3.right_ref = bf16[512,2304]{1,0:T(8,128)(2,1)} custom-call(bf16[512,2304]{1,0:T(8,128)(2,1)} %fusion.14.qkv_ref, f32[512,768]{1,0:T(8,128)} %get-tuple-element.20.lse_ref, bf16[512,768]{1,0:T(8,128)(2,1)} %convolution_convert_fusion.grad_ref), custom_call_target="tpu_custom_call" | custom-call | tf_op jit(solution)/shard_map/attend_back/pallas_call | solution.py:272
  370.2 2.1 convert_reduce_fusion.3
  372.8 9.8 %weight_grad.8.refs_0_ = bf16[392,288,128]{2,1,0:T(8,128)(2,1)} custom-call(s32[384]{0:T(512)} %fusion.22.rows_ref, bf16[512,3072]{1,0:T(8,128)(2,1)} %copy-done.22, bf16[512,768]{1,0:T(8,128)(2,1)} %copy-done.25), custom_call_target="tpu_custom_call" | custom-call | tf_op jit(solution)/shard_map/weight_grad/pallas_call | solution.py:350
  382.7 9.9 %weight_grad.9.refs_0_ = bf16[392,288,128]{2,1,0:T(8,128)(2,1)} custom-call(s32[384]{0:T(512)} %fusion.22.rows_ref, bf16[512,768]{1,0:T(8,128)(2,1)} %copy-done.15, bf16[512,3072]{1,0:T(8,128)(2,1)} %copy-done.20, bf16[392,288,128]{2,1,0:T(8,128)(2,1)} %weight_grad.8.refs_0_), custom_call_target="tpu_custom_call", output_to_operand_aliasing={{}: (3, {})} | custom-call | tf_op jit(solution)/shard_map/weight_grad/pallas_call | solution.py:350
  392.6 4.5 weight_grad.10.refs_0_
  397.1 8.1 weight_grad.11.refs_0_
  405.2 9.7 %weight_grad.12.refs_0_ = bf16[392,288,128]{2,1,0:T(8,128)(2,1)} custom-call(s32[384]{0:T(512)} %fusion.22.rows_ref, bf16[512,3072]{1,0:T(8,128)(2,1)} %copy-done.19, bf16[512,768]{1,0:T(8,128)(2,1)} %copy-done.17, bf16[392,288,128]{2,1,0:T(8,128)(2,1)} %weight_grad.11.refs_0_), custom_call_target="tpu_custom_call", output_to_operand_aliasing={{}: (3, {})} | custom-call | tf_op jit(solution)/shard_map/weight_grad/pallas_call | solution.py:350
  414.9 10.0 %weight_grad.13.refs_0_ = bf16[392,288,128]{2,1,0:T(8,128)(2,1)} custom-call(s32[384]{0:T(512)} %fusion.22.rows_ref, bf16[512,768]{1,0:T(8,128)(2,1)} %copy-done.13, bf16[512,3072]{1,0:T(8,128)(2,1)} %copy-done.21, bf16[392,288,128]{2,1,0:T(8,128)(2,1)} %weight_grad.12.refs_0_), custom_call_target="tpu_custom_call", output_to_operand_aliasing={{}: (3, {})} | custom-call | tf_op jit(solution)/shard_map/weight_grad/pallas_call | solution.py:350
  424.9 4.5 weight_grad.14.refs_0_
  429.4 8.1 weight_grad.15
  443.0 178.9 %reduce-scatter.4.cloned.1.call-done = bf16[49,288,128]{2,1,0:T(8,128)(2,1)} async-done(((bf16[392,288,128]{2,1,0:T(8,128)(2,1)}), bf16[49,288,128]{2,1,0:T(8,128)(2,1)}) %reduce-scatter.4.cloned.1.call-update) | async-done | bytes 3612688
  621.9 2.4 copy.47
  624.8 6.4 reduce.47
  631.2 1.0 reshape.325
  632.2 4.6 all-to-all-start.1
  636.8 4.5 add_bitcast_fusion
  641.3 2.8 copy.42
  644.0 34.7 %all-to-all-done.1 = bf16[4,2,49152]{2,1,0:T(2,128)(2,1)S(1)} async-done(((bf16[4,2,49152]{2,1,0:T(2,128)(2,1)}), bf16[4,2,49152]{2,1,0:T(2,128)(2,1)S(1)}, u32[]{:S(2)}, u32[]{:S(2)}) %all-to-all-start.1) | async-done | bytes 786464 | tf_op jit(solution)/shard_map/all_to_all | solution.py:561
  678.7 0.9 copy-done.23
  679.6 3.9 all-to-all-start.4
  683.5 2.5 reshape.326
  686.0 1.0 copy.44
  687.0 54.7 %all-to-all-done.4 = f32[1,512,768]{2,0,1:T(1,128)S(1)} async-done(((f32[1,512,768]{2,0,1:T(1,128)}), f32[1,512,768]{2,0,1:T(1,128)S(1)}, u32[]{:S(2)}, u32[]{:S(2)}) %all-to-all-start.4) | async-done | bytes 1572896 | tf_op jit(solution)/shard_map/all_to_all | solution.py:561
  741.7 1.2 copy.45
  742.9 64.0 %all-reduce.3.cloned.1.call-done.grad_ref = bf16[49,288,128]{2,1,0:T(8,128)(2,1)} async-done(((bf16[49,288,128]{2,1,0:T(8,128)(2,1)}), bf16[49,288,128]{2,1,0:T(8,128)(2,1)}) %all-reduce.3.cloned.1.call-update) | async-done | bytes 3612688 | tf_op jit(solution)/shard_map/psum | solution.py:640
  806.9 0.9 slice_convert_fusion
  807.9 0.9 divide_subtract_fusion
  808.8 37.9 %soap.1 = (f32[6,2304,128]{2,1,0:T(8,128)}, f32[6,2304,128]{2,1,0:T(8,128)}, f32[6,2304,128]{2,1,0:T(8,128)}, bf16[6,2304,128]{2,1,0:T(8,128)(2,1)}) custom-call(f32[6,2304,128]{2,1,0:T(8,128)} %bitcast.143, f32[6,2304,128]{2,1,0:T(8,128)} %bitcast.144, f32[6,2304,128]{2,1,0:T(8,128)} %bitcast.145, f32[6,2304,128]{2,1,0:T(8,128)} %bitcast.146, ...), custom_call_target="tpu_custom_call" | custom-call | tf_op jit(solution)/shard_map/soap/pallas_call | solution.py:450
  (268 shorter events, 17.4 us)
Async XLA Ops:
  7.2 149.7 %all-gather.2.cloned.1.call-start = ((), (), s32[]{:S(2)}) async-start(), calls=%async_computation.6 | async-start | bytes 31850496 | tf_op jit(solution)/shard_map/all_gather | solution.py:589
  7.2 8.3 copy-start.82
  7.2 8.3 copy-start.83
  15.4 15.5 %copy-start.30 = (f32[2,9216]{1,0:T(2,128)S(1)}, f32[2,9216]{1,0:T(2,128)}, u32[]{:S(2)}) copy-start(f32[2,9216]{1,0:T(2,128)} %param.23) | copy-start | bytes 221188
  15.5 37.9 %copy-start.32 = (s32[384]{0:T(512)S(1)}, s32[384]{0:T(512)}, u32[]{:S(2)}) copy-start(s32[384]{0:T(512)} %owner_ref.15) | copy-start | bytes 4612
  27.3 135.6 %copy-start.50 = (f32[4,1,128]{2,1,0:T(1,128)}, f32[4,1,128]{2,1,0:T(1,128)S(1)}, u32[]{:S(2)}) copy-start(f32[4,1,128]{2,1,0:T(1,128)S(1)} %all_to_all.58) | copy-start | bytes 6148
  27.3 22.5 %all-to-all-start.2 = ((bf16[4,128,768]{2,1,0:T(8,128)(2,1)}), bf16[4,128,768]{2,1,0:T(8,128)(2,1)S(1)}, u32[]{:S(2)}, u32[]{:S(2)}) async-start(bf16[4,128,768]{2,1,0:T(8,128)(2,1)} %param.14), calls=%async_computation.2 | async-start | bytes 1572864 | tf_op jit(solution)/shard_map/all_to_all | solution.py:557
  31.6 131.2 %copy-start.35 = (f32[768]{0:T(1024)}, f32[768]{0:T(1024)S(1)}, u32[]{:S(2)}) copy-start(f32[768]{0:T(1024)S(1)} %get-tuple-element.41) | copy-start | bytes 9220
  49.8 113.1 %copy-start.9 = (bf16[4,128,768]{2,1,0:T(8,128)(2,1)}, bf16[4,128,768]{2,1,0:T(8,128)(2,1)S(1)}, u32[]{:S(2)}) copy-start(bf16[4,128,768]{2,1,0:T(8,128)(2,1)S(1)} %all-to-all-done.2) | copy-start | bytes 2359300
  49.8 113.1 %all-to-all-start = ((bf16[4,128,768]{2,1,0:T(8,128)(2,1)}), bf16[4,128,768]{2,1,0:T(8,128)(2,1)S(1)}, u32[]{:S(2)}, u32[]{:S(2)}) async-start(bf16[4,128,768]{2,1,0:T(8,128)(2,1)} %param.13), calls=%async_computation | async-start | bytes 1572864 | tf_op jit(solution)/shard_map/all_to_all | solution.py:557
  53.3 568.6 %reduce-scatter.4.cloned.1.call-start = ((), (), s32[]{:S(2)}) async-start(), calls=%async_computation.8 | async-start | bytes 32514048
  162.9 19.2 %copy-start.12 = (bf16[4,128,768]{2,1,0:T(8,128)(2,1)}, bf16[4,128,768]{2,1,0:T(8,128)(2,1)S(1)}, u32[]{:S(2)}) copy-start(bf16[4,128,768]{2,1,0:T(8,128)(2,1)S(1)} %all-to-all-done) | copy-start | bytes 2359300
  185.8 8.7 %copy-start.13 = (bf16[512,768]{1,0:T(8,128)(2,1)}, bf16[512,768]{1,0:T(8,128)(2,1)S(1)}, u32[]{:S(2)}) copy-start(bf16[512,768]{1,0:T(8,128)(2,1)S(1)} %fusion.17.left_ref) | copy-start | bytes 2359300
  185.8 8.7 %copy-start.74 = (f32[1,3072]{1,0:T(1,128)S(1)}, f32[1,3072]{1,0:T(1,128)}, u32[]{:S(2)}) copy-start(f32[1,3072]{1,0:T(1,128)} %get-tuple-element.88) | copy-start | bytes 36868
  213.0 9.8 %copy-start.19 = (bf16[512,3072]{1,0:T(8,128)(2,1)}, bf16[512,3072]{1,0:T(8,128)(2,1)S(1)}, u32[]{:S(2)}) copy-start(bf16[512,3072]{1,0:T(8,128)(2,1)S(1)} %get-tuple-element.82.left_ref) | copy-start | bytes 9437188
  213.0 9.8 %copy-start.2 = (f32[512,768]{1,0:T(8,128)S(1)}, f32[512,768]{1,0:T(8,128)}, u32[]{:S(2)}) copy-start(f32[512,768]{1,0:T(8,128)} %copy-done.1) | copy-start | bytes 4718596
  213.0 9.8 %copy-start.40 = (f32[768]{0:T(1024)S(1)}, f32[768]{0:T(1024)}, u32[]{:S(2)}) copy-start(f32[768]{0:T(1024)} %get-tuple-element.52) | copy-start | bytes 9220
  213.0 9.8 %copy-start.48 = (f32[512]{0:T(512)S(1)}, f32[512]{0:T(512)}, u32[]{:S(2)}) copy-start(f32[512]{0:T(512)} %copy-done.47) | copy-start | bytes 6148
  213.0 9.8 %copy-start.58 = (f32[512]{0:T(512)S(1)}, f32[512]{0:T(512)}, u32[]{:S(2)}) copy-start(f32[512]{0:T(512)} %copy-done.57) | copy-start | bytes 6148
  213.0 9.8 %copy-start.70 = (f32[768]{0:T(1024)S(1)}, f32[768]{0:T(1024)}, u32[]{:S(2)}) copy-start(f32[768]{0:T(1024)} %get-tuple-element.51) | copy-start | bytes 9220
  213.0 9.8 %copy-start.80 = (f32[768]{0:T(1024)S(1)}, f32[768]{0:T(1024)}, u32[]{:S(2)}) copy-start(f32[768]{0:T(1024)} %get-tuple-element.50) | copy-start | bytes 9220
  256.9 10.4 %copy-start.55 = (f32[512]{0:T(512)}, f32[512]{0:T(512)S(1)}, u32[]{:S(2)}) copy-start(f32[512]{0:T(512)S(1)} %broadcast_multiply_fusion.8) | copy-start | bytes 6148
  257.2 10.1 %copy-start.63 = (f32[512]{0:T(512)}, f32[512]{0:T(512)S(1)}, u32[]{:S(2)}) copy-start(f32[512]{0:T(512)S(1)} %add_rsqrt_fusion.1) | copy-start | bytes 6148
  258.3 8.9 %copy-start.15 = (bf16[512,768]{1,0:T(8,128)(2,1)}, bf16[512,768]{1,0:T(8,128)(2,1)S(1)}, u32[]{:S(2)}) copy-start(bf16[512,768]{1,0:T(8,128)(2,1)S(1)} %fusion.19.left_ref) | copy-start | bytes 2359300
  258.3 8.9 %copy-start.76 = (f32[1,3072]{1,0:T(1,128)S(1)}, f32[1,3072]{1,0:T(1,128)}, u32[]{:S(2)}) copy-start(f32[1,3072]{1,0:T(1,128)} %get-tuple-element.87) | copy-start | bytes 36868
  286.2 9.5 %copy-start.22 = (bf16[512,3072]{1,0:T(8,128)(2,1)}, bf16[512,3072]{1,0:T(8,128)(2,1)S(1)}, u32[]{:S(2)}) copy-start(bf16[512,3072]{1,0:T(8,128)(2,1)S(1)} %get-tuple-element.80.left_ref) | copy-start | bytes 9437188
  286.2 9.5 %copy-start.8 = (f32[512,768]{1,0:T(8,128)S(1)}, f32[512,768]{1,0:T(8,128)}, u32[]{:S(2)}) copy-start(f32[512,768]{1,0:T(8,128)} %copy-done.7) | copy-start | bytes 4718596
  286.2 9.5 %copy-start.46 = (f32[768]{0:T(1024)S(1)}, f32[768]{0:T(1024)}, u32[]{:S(2)}) copy-start(f32[768]{0:T(1024)} %get-tuple-element.44) | copy-start | bytes 9220
  286.2 9.5 %copy-start.56 = (f32[512]{0:T(512)S(1)}, f32[512]{0:T(512)}, u32[]{:S(2)}) copy-start(f32[512]{0:T(512)} %copy-done.55) | copy-start | bytes 6148
  286.2 9.5 %copy-start.64 = (f32[512]{0:T(512)S(1)}, f32[512]{0:T(512)}, u32[]{:S(2)}) copy-start(f32[512]{0:T(512)} %copy-done.63) | copy-start | bytes 6148
  286.2 9.5 %copy-start.66 = (f32[768]{0:T(1024)S(1)}, f32[768]{0:T(1024)}, u32[]{:S(2)}) copy-start(f32[768]{0:T(1024)} %get-tuple-element.43) | copy-start | bytes 9220
  286.2 9.5 %copy-start.78 = (f32[768]{0:T(1024)S(1)}, f32[768]{0:T(1024)}, u32[]{:S(2)}) copy-start(f32[768]{0:T(1024)} %get-tuple-element.42) | copy-start | bytes 9220
  295.6 8.1 slice-start.6
  295.7 6.4 copy-start.72
  295.7 6.4 copy-start.77
  295.8 8.0 slice-start.7
  302.1 9.6 %slice-start.4 = ((s8[4718592]{0:T(1024)(128)(4,1)}), s8[4194304]{0:T(1024)(128)(4,1)S(1)}, s32[]{:S(2)}) async-start(s8[4718592]{0:T(1024)(128)(4,1)} %bitcast.154), calls=%async_computation.13 | async-start | bytes 8388608
  303.8 7.9 copy-start.25
  303.8 8.0 slice-start.5
  315.4 17.7 %copy-start.16 = (bf16[512,768]{1,0:T(8,128)(2,1)}, bf16[512,768]{1,0:T(8,128)(2,1)S(1)}, u32[]{:S(2)}) copy-start(bf16[512,768]{1,0:T(8,128)(2,1)S(1)} %get-tuple-element.78.right_ref) | copy-start | bytes 2359300
  317.8 17.4 %copy-start.6 = (f32[512,768]{1,0:T(8,128)S(1)}, f32[512,768]{1,0:T(8,128)}, u32[]{:S(2)}) copy-start(f32[512,768]{1,0:T(8,128)} %copy-done.4) | copy-start | bytes 4718596
  317.8 17.4 %copy-start.11 = (bf16[768,2304]{1,0:T(8,128)(2,1)S(1)}, bf16[768,2304]{1,0:T(8,128)(2,1)}, u32[]{:S(2)}) copy-start(bf16[768,2304]{1,0:T(8,128)(2,1)} %assemble.12) | copy-start | bytes 10616836
  317.8 17.4 %copy-start.44 = (f32[768]{0:T(1024)S(1)}, f32[768]{0:T(1024)}, u32[]{:S(2)}) copy-start(f32[768]{0:T(1024)} %get-tuple-element.49) | copy-start | bytes 9220
  317.9 17.4 %copy-start.54 = (f32[512]{0:T(512)S(1)}, f32[512]{0:T(512)}, u32[]{:S(2)}) copy-start(f32[512]{0:T(512)} %copy-done.52) | copy-start | bytes 6148
  317.9 17.4 %copy-start.62 = (f32[512]{0:T(512)S(1)}, f32[512]{0:T(512)}, u32[]{:S(2)}) copy-start(f32[512]{0:T(512)} %copy-done.60) | copy-start | bytes 6148
  339.6 9.0 %slice-start = ((s8[4718592]{0:T(1024)(128)(4,1)}), s8[4194304]{0:T(1024)(128)(4,1)S(1)}, s32[]{:S(2)}) async-start(s8[4718592]{0:T(1024)(128)(4,1)} %bitcast.150), calls=%async_computation.9 | async-start | bytes 8388608
  340.1 8.4 copy-start.17
  340.2 8.3 copy-start.3
  340.2 8.3 slice-start.1
  340.2 8.3 copy-start.41
  340.2 8.3 copy-start.49
  340.2 8.3 copy-start.59
  353.5 16.8 %copy-start.18 = (bf16[512,768]{1,0:T(8,128)(2,1)}, bf16[512,768]{1,0:T(8,128)(2,1)S(1)}, u32[]{:S(2)}) copy-start(bf16[512,768]{1,0:T(8,128)(2,1)S(1)} %get-tuple-element.70.right_ref) | copy-start | bytes 2359300
  355.2 17.2 %copy-start.38 = (f32[9216]{0:T(1024)S(1)}, f32[9216]{0:T(1024)}, u32[]{:S(2)}) copy-start(f32[9216]{0:T(1024)} %custom-call.1) | copy-start | bytes 110596
  355.2 17.4 %copy-start.37 = (f32[9216]{0:T(1024)S(1)}, f32[9216]{0:T(1024)}, u32[]{:S(2)}) copy-start(f32[9216]{0:T(1024)} %custom-call) | copy-start | bytes 110596
  355.2 17.4 %copy-start.71 = (f32[768]{0:T(1024)S(1)}, f32[768]{0:T(1024)}, u32[]{:S(2)}) copy-start(f32[768]{0:T(1024)} %get-tuple-element.39) | copy-start | bytes 9220
  442.6 179.2 %copy-start.24 = (bf16[1,512,768]{2,1,0:T(8,128)(2,1)S(1)}, bf16[1,512,768]{2,1,0:T(8,128)(2,1)}, u32[]{:S(2)}) copy-start(bf16[1,512,768]{2,1,0:T(8,128)(2,1)} %get-tuple-element.84) | copy-start | bytes 2359300
  442.7 364.3 %all-reduce.3.cloned.1.call-start = ((), (), s32[]{:S(2)}) async-start(), calls=%async_computation.7 | async-start | bytes 7225344 | tf_op jit(solution)/shard_map/psum | solution.py:640
  621.9 14.9 %copy-start = (bf16[512,2304]{1,0:T(8,128)(2,1)S(1)}, bf16[512,2304]{1,0:T(8,128)(2,1)}, u32[]{:S(2)}) copy-start(bf16[512,2304]{1,0:T(8,128)(2,1)} %attend_back.3.right_ref) | copy-start | bytes 7077892
  632.2 46.6 %all-to-all-start.1 = ((bf16[4,2,49152]{2,1,0:T(2,128)(2,1)}), bf16[4,2,49152]{2,1,0:T(2,128)(2,1)S(1)}, u32[]{:S(2)}, u32[]{:S(2)}) async-start(bf16[4,2,49152]{2,1,0:T(2,128)(2,1)} %reshape.325), calls=%async_computation.1 | async-start | bytes 1572864 | tf_op jit(solution)/shard_map/all_to_all | solution.py:561
  679.6 62.1 %all-to-all-start.4 = ((f32[1,512,768]{2,0,1:T(1,128)}), f32[1,512,768]{2,0,1:T(1,128)S(1)}, u32[]{:S(2)}, u32[]{:S(2)}) async-start(f32[1,512,768]{2,0,1:T(1,128)} %copy.42), calls=%async_computation.4 | async-start | bytes 3145728 | tf_op jit(solution)/shard_map/all_to_all | solution.py:561
  683.5 124.4 %copy-start.31 = (f32[2,9216]{1,0:T(2,128)S(1)}, f32[2,9216]{1,0:T(2,128)}, u32[]{:S(2)}) copy-start(f32[2,9216]{1,0:T(2,128)} %param.23) | copy-start | bytes 221188
  683.5 124.4 %copy-start.33 = (f32[2,9216]{1,0:T(2,128)S(1)}, f32[2,9216]{1,0:T(2,128)}, u32[]{:S(2)}) copy-start(f32[2,9216]{1,0:T(2,128)} %param.24) | copy-start | bytes 221188
  683.5 124.4 %copy-start.34 = (f32[2,9216]{1,0:T(2,128)S(1)}, f32[2,9216]{1,0:T(2,128)}, u32[]{:S(2)}) copy-start(f32[2,9216]{1,0:T(2,128)} %param.25) | copy-start | bytes 221188
  (35 other events, 115.4 us)
Sparse Core Ops, SparseCore 0:
  15.6 141.2 all-gather.1
  442.8 179.0 reduce-scatter.3
  624.3 182.6 all-reduce.2

commit v2 on v1

--- a/solution.py
+++ b/solution.py
@@ -1,4 +1,5 @@
 import functools
+import math
 import jax
 import jax.numpy as jnp
 from jax import lax
@@ -13,6 +14,11 @@
 HALF = BLK // 2
 PACK = BLK * BLK // LANE
 GROUP = 8
+GATHER_ROWS = 144
+GATHER_LAG = 2
+REDUCE_ROWS = 144
+REDUCE_LAG = 2
+WAIT_BYTES = 3 * 10**8
 
 norm_eps = 1e-05
 beta_one = 0.95
@@ -459,6 +465,404 @@
     )(*views, grads)
 
 
+MESH = pl.DeviceIdType.MESH
+
+
+def place(size):
+    index = lax.axis_index("dp")
+    core = lax.rem(index, 2)
+    col = lax.rem(lax.div(index, 2), size[1])
+    row = lax.div(index, 2 * size[1])
+    return row, col, core
+
+
+def device(row, col, core, size, depth):
+    return {"dp": (row * size[1] + col) * 2 + core, "seq": depth}
+
+
+def greet(partners, layers, level, above, below):
+    barrier = pltpu.get_barrier_semaphore()
+    for partner in partners:
+        pl.semaphore_signal(barrier, inc=1, device_id=partner, device_id_type=MESH)
+
+    @pl.when(level > 0)
+    def _():
+        pl.semaphore_signal(barrier, inc=1, device_id=below, device_id_type=MESH)
+
+    @pl.when(level < layers - 1)
+    def _():
+        pl.semaphore_signal(barrier, inc=1, device_id=above, device_id_type=MESH)
+
+    inner = (level > 0).astype(jnp.int32) + (level < layers - 1).astype(jnp.int32)
+    pl.semaphore_wait(barrier, len(partners) + inner)
+
+
+def reduce_kernel(
+    steps, rows, layers, lag, slots_ref, out_ref, own, inbox, first, second, up, down, down_sum,
+    own_sem, core_send, core_recv, one_send, one_recv, two_send, two_recv,
+    up_send, up_recv, down_send, down_recv,
+):
+    size = (2, 2)
+    y, x, core = place(size)
+    level = lax.axis_index("seq")
+    other_core = device(y, x, 1 - core, size, level)
+    across_x = device(y, 1 - x, core, size, level)
+    across_y = device(1 - y, x, core, size, level)
+    above = device(y, x, core, size, lax.rem(level + 1, layers))
+    below = device(y, x, core, size, lax.rem(level + layers - 1, layers))
+    firsts, seconds = [across_x, across_y], [across_y, across_x]
+
+    def span(half, step):
+        return pl.ds(pl.multiple_of((half * steps + step) * rows, rows), rows)
+
+    def remote(source, target, send, recv, half, step, where):
+        return pltpu.make_async_remote_copy(
+            src_ref=source,
+            dst_ref=target,
+            send_sem=send.at[half, step],
+            recv_sem=recv.at[half, step],
+            device_id=where,
+            device_id_type=MESH,
+        )
+
+    def own_copy(half, step):
+        part = span(half, step)
+        return pltpu.make_async_copy(
+            slots_ref.at[:, :, core, part], own.at[:, :, part], own_sem.at[half, step]
+        )
+
+    def core_copy(half, step):
+        part = span(half, step)
+        return remote(
+            slots_ref.at[:, :, 1 - core, part], inbox.at[:, :, part],
+            core_send, core_recv, half, step, other_core,
+        )
+
+    def one_copy(half, step):
+        part = span(half, step)
+        source = own.at[:, 1 - x, part] if half == 0 else own.at[1 - y, :, part]
+        return remote(source, first.at[:, part], one_send, one_recv, half, step, firsts[half])
+
+    def two_copy(half, step):
+        part = span(half, step)
+        source = own.at[1 - y, x, part] if half == 0 else own.at[y, 1 - x, part]
+        return remote(source, second.at[part], two_send, two_recv, half, step, seconds[half])
+
+    def up_copy(half, step):
+        part = span(half, step)
+        return remote(up.at[part], up.at[part], up_send, up_recv, half, step, above)
+
+    def down_copy(half, step):
+        part = span(half, step)
+        return remote(down_sum.at[part], down.at[part], down_send, down_recv, half, step, below)
+
+    def inside(step):
+        return jnp.logical_and(step >= 0, step < steps)
+
+    greet([other_core, across_x, across_y], layers, level, above, below)
+
+    @pl.loop(0, steps)
+    def _(step):
+        for half in range(2):
+            own_copy(half, step).start()
+            core_copy(half, step).start()
+
+    @pl.loop(0, steps + lag * (layers + 1))
+    def _(tick):
+        one_step = tick - lag
+        two_step = tick - 2 * lag
+        up_step = two_step - lag * level
+        down_step = two_step - lag * (layers - 1 - level)
+        last_step = two_step - lag * (layers - 1)
+
+        @pl.when(inside(tick))
+        def _():
+            for half in range(2):
+                part = span(half, tick)
+                own_copy(half, tick).wait()
+                core_copy(half, tick).wait_recv()
+                own[:, :, part] = own[:, :, part] + inbox[:, :, part]
+
+        @pl.when(inside(one_step))
+        def _():
+            for half in range(2):
+                part = span(half, one_step)
+                one_copy(half, one_step).wait_recv()
+                if half == 0:
+                    own[:, x, part] = own[:, x, part] + first[:, part]
+                else:
+                    own[y, :, part] = own[y, :, part] + first[:, part]
+
+        @pl.when(inside(two_step))
+        def _():
+            for half in range(2):
+                part = span(half, two_step)
+                two_copy(half, two_step).wait_recv()
+                own[y, x, part] = own[y, x, part] + second[part]
+
+        @pl.when(inside(up_step))
+        def _():
+            for half in range(2):
+                part = span(half, up_step)
+
+                @pl.when(level > 0)
+                def _():
+                    up_copy(half, up_step).wait_recv()
+                    up[part] = up[part] + own[y, x, part]
+
+                @pl.when(level == 0)
+                def _():
+                    up[part] = own[y, x, part]
+
+        @pl.when(inside(down_step))
+        def _():
+            for half in range(2):
+                part = span(half, down_step)
+
+                @pl.when(level < layers - 1)
+                def _():
+                    down_copy(half, down_step).wait_recv()
+                    down_sum[part] = down[part] + own[y, x, part]
+
+                @pl.when(level == layers - 1)
+                def _():
+                    down_sum[part] = own[y, x, part]
+
+        @pl.when(inside(last_step))
+        def _():
+            for half in range(2):
+                part = span(half, last_step)
+
+                @pl.when(level < layers - 1)
+                def _():
+                    out_ref[part] = up[part] + down[part]
+
+                @pl.when(level == layers - 1)
+                def _():
+                    out_ref[part] = up[part]
+
+        @pl.when(inside(tick))
+        def _():
+            for half in range(2):
+                one_copy(half, tick).start()
+
+        @pl.when(inside(one_step))
+        def _():
+            for half in range(2):
+                two_copy(half, one_step).start()
+
+        @pl.when(jnp.logical_and(inside(up_step), level < layers - 1))
+        def _():
+            for half in range(2):
+                up_copy(half, up_step).start()
+
+        @pl.when(jnp.logical_and(inside(down_step), level > 0))
+        def _():
+            for half in range(2):
+                down_copy(half, down_step).start()
+
+    @pl.loop(0, steps)
+    def _(step):
+        for half in range(2):
+            core_copy(half, step).wait_send()
+            one_copy(half, step).wait_send()
+            two_copy(half, step).wait_send()
+
+            @pl.when(level < layers - 1)
+            def _():
+                up_copy(half, step).wait_send()
+
+            @pl.when(level > 0)
+            def _():
+                down_copy(half, step).wait_send()
+
+
+def reduce_slots(slots, layers, rows, lag):
+    total = slots.shape[0] // 8 * PACK
+    steps = total // (2 * rows)
+    chunk = (total, LANE)
+    sems = pltpu.SemaphoreType.DMA((2, steps))
+    out = pl.pallas_call(
+        functools.partial(reduce_kernel, steps, rows, layers, lag),
+        in_specs=[pl.BlockSpec(memory_space=pl.ANY)],
+        out_specs=pl.BlockSpec(memory_space=pltpu.VMEM),
+        out_shape=jax.ShapeDtypeStruct(chunk, bf16),
+        scratch_shapes=[
+            pltpu.VMEM((2, 2) + chunk, bf16),
+            pltpu.VMEM((2, 2) + chunk, bf16),
+            pltpu.VMEM((2,) + chunk, bf16),
+        ]
+        + [pltpu.VMEM(chunk, bf16)] * 4
+        + [sems] * 11,
+        compiler_params=pltpu.CompilerParams(
+            vmem_limit_bytes=62 * 2**20, collective_id=0, has_side_effects=True
+        ),
+        cost_estimate=pl.CostEstimate(flops=0, bytes_accessed=WAIT_BYTES, transcendentals=0),
+        name="reduce_slots",
+    )(slots.reshape((2, 2, 2) + chunk))
+    return out.reshape(total // PACK, PACK, LANE)
+
+
+def gather_kernel(
+    steps, rows, lag, mine_ref, out_ref, own_sem, one_send, one_recv, two_send, two_recv,
+    near_send, near_recv, far_send, far_recv, core_send, core_recv,
+):
+    size = (2, 2)
+    y, x, core = place(size)
+    level = lax.axis_index("seq")
+    side = lax.rem(level, 2)
+    other_core = device(y, x, 1 - core, size, level)
+    across_x = device(y, 1 - x, core, size, level)
+    across_y = device(1 - y, x, core, size, level)
+    beside = device(y, x, core, size, level + 1 - 2 * side)
+    firsts, seconds = [across_x, across_y], [across_y, across_x]
+
+    def span(kind, half, step):
+        return pl.ds(pl.multiple_of(((kind * 2 + half) * steps + step) * rows, rows), rows)
+
+    def kind_of(turn):
+        late = lax.div(turn, steps)
+        return side + (2 - side) * late, lax.rem(turn, steps)
+
+    def remote(source, target, send, recv, where):
+        return pltpu.make_async_remote_copy(
+            src_ref=source,
+            dst_ref=target,
+            send_sem=send,
+            recv_sem=recv,
+            device_id=where,
+            device_id_type=MESH,
+        )
+
+    def own_copy():
+        return pltpu.make_async_copy(mine_ref, out_ref.at[y, x, core], own_sem)
+
+    def one_copy(half, turn):
+        kind, step = kind_of(turn)
+        part = span(kind, half, step)
+        return remote(
+            mine_ref.at[part], out_ref.at[y, x, core, part],
+            one_send.at[half, turn], one_recv.at[half, turn], firsts[half],
+        )
+
+    def two_copy(half, turn):
+        kind, step = kind_of(turn)
+        part = span(kind, half, step)
+        ref = out_ref.at[y, :, core, part] if half == 0 else out_ref.at[:, x, core, part]
+        return remote(
+            ref, ref, two_send.at[half, turn], two_recv.at[half, turn], seconds[half]
+        )
+
+    def near_copy(half, step):
+        part = span(side, half, step)
+        ref = out_ref.at[y, 1 - x, core, part] if half == 0 else out_ref.at[1 - y, x, core, part]
+        return remote(ref, ref, near_send.at[half, step], near_recv.at[half, step], beside)
+
+    def far_copy(half, step):
+        part = span(side, half, step)
+        ref = out_ref.at[1 - y, :, core, part] if half == 0 else out_ref.at[:, 1 - x, core, part]
+        return remote(ref, ref, far_send.at[half, step], far_recv.at[half, step], beside)
+
+    def core_copy(kind, half, step, slot):
+        ref = out_ref.at[:, :, core, span(kind, half, step)]
+        return remote(ref, ref, core_send.at[half, slot], core_recv.at[half, slot], other_core)
+
+    partners = [other_core, across_x, across_y, beside]
+    barrier = pltpu.get_barrier_semaphore()
+    for partner in partners:
+        pl.semaphore_signal(barrier, inc=1, device_id=partner, device_id_type=MESH)
+    pl.semaphore_wait(barrier, len(partners))
+
+    own_copy().start()
+    turns = 2 * steps
+
+    @pl.loop(0, turns + 4 * lag + 2)
+    def _(tick):
+        @pl.when(tick < turns)
+        def _():
+            for half in range(2):
+                one_copy(half, tick).start()
+
+        @pl.when(tick == lag)
+        def _():
+            own_copy().wait()
+
+        turn = tick - lag
+
+        @pl.when(jnp.logical_and(turn >= 0, turn < turns))
+        def _():
+            for half in range(2):
+                one_copy(half, turn).wait_recv()
+                two_copy(half, turn).start()
+
+        @pl.when(jnp.logical_and(turn >= 0, turn < steps))
+        def _():
+            for half in range(2):
+                near_copy(half, turn).start()
+
+        after = tick - 2 * lag
+
+        @pl.when(jnp.logical_and(after >= 0, after < turns))
+        def _():
+            kind, step = kind_of(after)
+            for half in range(2):
+                two_copy(half, after).wait_recv()
+                core_copy(kind, half, step, after).start()
+
+        @pl.when(jnp.logical_and(after >= 0, after < steps))
+        def _():
+            for half in range(2):
+                far_copy(half, after).start()
+
+        late = tick - 4 * lag
+        given = lax.div(late, 2)
+
+        @pl.when(jnp.logical_and(late >= 0, jnp.logical_and(given < steps, late == 2 * given)))
+        def _():
+            for half in range(2):
+                near_copy(half, given).wait_recv()
+                far_copy(half, given).wait_recv()
+                core_copy(1 - side, half, given, turns + given).start()
+
+    @pl.loop(0, turns)
+    def _(turn):
+        kind, step = kind_of(turn)
+        for half in range(2):
+            one_copy(half, turn).wait_send()
+            two_copy(half, turn).wait_send()
+            core_copy(kind, half, step, turn).wait()
+
+    @pl.loop(0, steps)
+    def _(step):
+        for half in range(2):
+            near_copy(half, step).wait_send()
+            far_copy(half, step).wait_send()
+            core_copy(1 - side, half, step, turns + step).wait()
+
+
+def gather_slots(packed, rows, lag):
+    total = packed.shape[0] * PACK
+    steps = total // (6 * rows)
+
+    def sems(count):
+        return [pltpu.SemaphoreType.DMA((2, count))] * 2
+
+    out = pl.pallas_call(
+        functools.partial(gather_kernel, steps, rows, lag),
+        in_specs=[pl.BlockSpec(memory_space=pltpu.VMEM)],
+        out_specs=pl.BlockSpec(memory_space=pl.ANY),
+        out_shape=jax.ShapeDtypeStruct((2, 2, 2, total, LANE), bf16),
+        scratch_shapes=[pltpu.SemaphoreType.DMA]
+        + sems(2 * steps) + sems(2 * steps) + sems(steps) + sems(steps) + sems(3 * steps),
+        compiler_params=pltpu.CompilerParams(
+            vmem_limit_bytes=62 * 2**20, collective_id=1, has_side_effects=True
+        ),
+        cost_estimate=pl.CostEstimate(flops=0, bytes_accessed=WAIT_BYTES, transcendentals=0),
+        name="gather_slots",
+    )(packed.reshape(total, LANE))
+    return out.reshape(8 * packed.shape[0], PACK, LANE)
+
+
 def norm_forward(hidden, gain, shift):
     center = hidden - jnp.mean(hidden, axis=-1, keepdims=True)
     spread = jnp.mean(center * center, axis=-1, keepdims=True)
@@ -477,8 +881,13 @@
     return (grad_hidden, jnp.sum(incoming * unit, axis=0), jnp.sum(incoming, axis=0))
 
 
-def gelu_exact(value):
-    return jax.nn.gelu(value, approximate=False)
+def gelu(value):
+    return 0.5 * value * (1.0 + lax.erf(value * 0.5**0.5))
+
+
+def gelu_slope(value):
+    bell = jnp.exp(-0.5 * value * value) * (0.5 / math.pi) ** 0.5
+    return 0.5 * (1.0 + lax.erf(value * 0.5**0.5)) + value * bell
 
 
 def unpack(vector, width):
@@ -499,7 +908,7 @@
     normed, unit_one, inv_one = norm_forward(hidden + branch, gain_one, shift_one)
     norm_low = normed.astype(bf16)
     pre_act = dot(norm_low, w_up) + bias_up
-    act_low = gelu_exact(pre_act).astype(bf16)
+    act_low = gelu(pre_act).astype(bf16)
     down = dot(act_low, w_down) + bias_down
     result, unit_two, inv_two = norm_forward(normed + down, gain_two, shift_two)
     kept = (
@@ -521,8 +930,7 @@
         slots, slot_shape, rows, act_low, down_low, base + 4 * square + up_count, width
     )
     grad_act = dot(down_low, w_down, 1, 1)
-    (grad_pre,) = jax.vjp(gelu_exact, pre_act)[1](grad_act)
-    up_low = grad_pre.astype(bf16)
+    up_low = (gelu_slope(pre_act) * grad_act).astype(bf16)
     slots = plain_grad(slots, slot_shape, rows, norm_low, up_low, base + 4 * square, width)
     grad_norm = grad_two + dot(up_low, w_up, 1, 1)
     grad_one, gain_one_g, shift_one_g = norm_backward(grad_norm, unit_one, inv_one, gain_one)
@@ -559,6 +967,24 @@
 
 def swap_out(array):
     return lax.all_to_all(array, "seq", split_axis=1, concat_axis=0, tiled=True)
+
+
+def near_group():
+    return lax.axis_size("dp") == 8 and lax.axis_size("seq") % 2 == 0
+
+
+def gather_blocks(packed):
+    total = packed.shape[0] * PACK
+    if near_group() and total % (6 * GATHER_ROWS) == 0:
+        return gather_slots(packed, GATHER_ROWS, GATHER_LAG)
+    return lax.all_gather(packed, "dp", axis=0, tiled=True)
+
+
+def reduce_blocks(slots):
+    total = slots.shape[0] // lax.axis_size("dp") * PACK
+    if near_group() and total % (2 * REDUCE_ROWS) == 0:
+        return reduce_slots(slots, lax.axis_size("seq"), REDUCE_ROWS, REDUCE_LAG)
+    return lax.psum(lax.psum_scatter(slots, "dp", scatter_dimension=0, tiled=True), "seq")
 
 
 def local(
@@ -586,17 +1012,20 @@
 
     master_view = row_view(masters)
     packed = pack_blocks(master_view)[:owned_count]
-    gathered = lax.all_gather(packed, "dp", axis=0, tiled=True)
-
-    positions = lax.axis_index("seq") * local_len + jnp.arange(local_len, dtype=jnp.int32)
-    masked = (positions[None, :] < mask_count[:, None]).astype(f32)
-    factor = tok_weight.astype(f32) * (1.0 + masked) * 0.25
+    gathered = gather_blocks(packed)
+
     hidden = swap_in(tokens)
     per_seq = hidden.shape[0]
     full_len = hidden.shape[1]
     hidden = hidden.reshape(full_len, width).astype(f32)
     incoming = swap_in(cotangent).reshape(full_len, width).astype(f32)
-    incoming = incoming * swap_in(factor).reshape(full_len, 1)
+    first = lax.axis_index("seq") * per_seq
+    weight = lax.all_gather(tok_weight, "seq", axis=1, tiled=True)
+    weight = lax.dynamic_slice_in_dim(weight, first, per_seq, 0).reshape(full_len, 1)
+    count = lax.dynamic_slice_in_dim(mask_count, first, per_seq, 0)
+    positions = jnp.arange(full_len, dtype=jnp.int32)
+    masked = (positions < count[0]).astype(f32)[:, None]
+    incoming = incoming * (weight.astype(f32) * (1.0 + masked) * 0.25)
 
     per_layer = block_total // layer_count
     weights = [
@@ -632,12 +1061,10 @@
     vec_high = vec_grad.astype(bf16)
     vec_low = (vec_grad - vec_high.astype(f32)).astype(bf16)
     vec_slot = jnp.concatenate([vec_high.reshape(-1, LANE), vec_low.reshape(-1, LANE)], axis=0)
-    for part in range(data_parts):
-        slots = lax.dynamic_update_slice(
-            slots, vec_slot[None], (part * chunk + owned_count, 0, 0)
-        )
-    owned = lax.psum_scatter(slots, "dp", scatter_dimension=0, tiled=True)
-    owned = lax.psum(owned, "seq")
+    slots = slots.reshape((data_parts, chunk) + vec_slot.shape)
+    vec_slots = jnp.broadcast_to(vec_slot, (data_parts, 1) + vec_slot.shape)
+    slots = lax.dynamic_update_slice(slots, vec_slots, (0, owned_count, 0, 0))
+    owned = reduce_blocks(slots.reshape(slot_shape))
     input_grad = swap_out(incoming.reshape(per_seq, full_len, width))
 
     vec_rows = owned[owned_count].astype(f32)

time: 865 us -> 616 us (0.71)
  waiting for transfers between devices: 451 us -> 0.01 us
  Pallas kernels: 217 us -> 458 us
  matrix products: 97.7 us -> 59 us
  between operations: 15.8 us -> 2.33 us
  blocking collectives: 11.7 us -> 24.8 us
    pallas_call x0 -> x2, Pallas kernels: none -> 244 us  [the longest x1 153 us: reduce_slots(): pl.pallas_call(functools.partial(reduce_kernel, steps, rows, layers, lag)...]
    unnamed x4 -> x0, waiting for transfers between devices: 179 us -> none
    all_gather x1 -> x0, waiting for transfers between devices: 100 us -> none  [local(): gathered = lax.all_gather(packed, 'dp', axis=0, tiled=True)]
    all_to_all x2, waiting for transfers between devices: 89.4 us -> 0.01 us  [swap_out(): return lax.all_to_all(array, 'seq', split_axis=1, concat_axis=0, tiled=True)]
    psum x1 -> x0, waiting for transfers between devices: 64 us -> none  [local(): owned = lax.psum(owned, 'seq')]
    dot_general x16, matrix products: 97.7 us -> 59 us  [dot(): lax.dot_general(left, right, (((left_dim,), (right_dim,)), ((), ())), pre...]
    all_gather x0 -> x1, blocking collectives: none -> 24.8 us  [local(): weight = lax.all_gather(tok_weight, 'seq', axis=1, tiled=True)]
    all_to_all x2, waiting for transfers between devices: 18.1 us -> 0.01 us  [swap_in(): return lax.all_to_all(array, 'seq', split_axis=0, concat_axis=1, tiled=True)]
  transfers between devices with their start and end apart: 7 -> 4, of which waited for: 6 -> 0; matrix products, arithmetic and copies ran while one was open for 3% -> 2% of each run, Pallas kernels for 1% -> 68%
where the time goes in v2:
time: 616 us; the launch traced here: 604 us
  Pallas kernels  458 us (74%)
  matrix products  59 us (10%)
  blocking collectives  24.8 us (4%)
  other arithmetic  23.8 us (4%)
  starting transfers between devices  18.7 us (3%)
  local copies, waits for them, and re-layouts  17.4 us (3%)
    pallas_call x1, Pallas kernels, reduce_slots(): pl.pallas_call(functools.partial(reduce_kernel, steps, rows, layers, lag)...  153 us
    pallas_call x1, Pallas kernels, gather_slots(): pl.pallas_call(functools.partial(gather_kernel, steps, rows, lag), in_spe...  90.9 us
    pallas_call x8, Pallas kernels, weight_grad(): pl.pallas_call(functools.partial(weight_grad_kernel, lanes_of, block_of,...  64.7 us
    dot_general x16, matrix products, dot(): lax.dot_general(left, right, (((left_dim,), (right_dim,)), ((), ())), pre...  59 us
    pallas_call x8, Pallas kernels, assemble(): pl.pallas_call(functools.partial(assemble_kernel, cells), grid_spec=pltpu...  53.3 us
    pallas_call x1, Pallas kernels, soap(): pl.pallas_call(soap_kernel, grid=(groups,), in_specs=[view_spec] * 5 + [p...  38 us
    pallas_call x2, Pallas kernels, attend_back(): pl.pallas_call(functools.partial(attend_back_kernel, scale), grid=(pairs,...  29.9 us
    all_gather x1, blocking collectives, local(): weight = lax.all_gather(tok_weight, 'seq', axis=1, tiled=True)  24.8 us
  transfers between devices with their start and end apart: 4, of which 0 were waited for; matrix products, arithmetic and copies ran while one was open for 2% of the time, Pallas kernels for 68%

profile of v2, /device:TPU:0, one launch (start us, length us, event | category | flops | bytes accessed | tf_op | source)
XLA Modules:
  0.0 604.2 jit_solution(14481774059346704231)
XLA Ops:
  0.7 6.5 %all-to-all-start.2 = ((bf16[4,128,768]{2,1,0:T(8,128)(2,1)}), bf16[4,128,768]{2,1,0:T(8,128)(2,1)S(1)}, u32[]{:S(2)}, u32[]{:S(2)}) async-start(bf16[4,128,768]{2,1,0:T(8,128)(2,1)} %param.14), calls=%async_computation.2 | async-start | bytes 1572864 | tf_op jit(solution)/shard_map/all_to_all | solution.py:965
  7.9 24.8 %all_gather.3 = s32[4,512]{1,0:T(4,128)S(1)} all-gather(s32[4,128]{1,0:T(4,128)S(1)} %copy-done.48), channel_id=1, replica_groups=mesh['dp'=8,'seq'=4] {'seq'}, dimensions={1}, use_global_device_ids=true | all-gather | bytes 10240 | tf_op jit(solution)/shard_map/all_gather | solution.py:1023
  34.7 4.2 all-to-all-start
  38.9 1.2 multiply_multiply_fusion.3
  40.1 8.2 %pack.1 = bf16[48,288,128]{2,1,0:T(8,128)(2,1)} custom-call(f32[6,2304,128]{2,1,0:T(8,128)} %bitcast.202), custom_call_target="tpu_custom_call" | custom-call | tf_op jit(solution)/shard_map/pack/pallas_call | solution.py:113
  48.3 90.9 %gather_slots.1 = bf16[2,2,2,13824,128]{4,3,2,1,0:T(8,128)(2,1)} custom-call(bf16[13824,128]{1,0:T(8,128)(2,1)} %bitcast.205), custom_call_target="tpu_custom_call" | custom-call | bytes 300000000 | tf_op jit(solution)/shard_map/gather_slots/pallas_call | solution.py:850
  139.2 3.3 assemble.13
  142.6 3.3 assemble.9
  145.9 6.0 assemble.12
  151.9 6.0 assemble.8
  157.9 8.6 %assemble.15 = bf16[3072,768]{1,0:T(8,128)(2,1)} custom-call(s32[384]{0:T(512)} %owner_ref.15, bf16[384,288,128]{2,1,0:T(8,128)(2,1)} %bitcast.168, bf16[384,288,128]{2,1,0:T(8,128)(2,1)} %bitcast.169, bf16[384,288,128]{2,1,0:T(8,128)(2,1)} %bitcast.170, bf16[384,288,128]{2,1,0:T(8,128)(2,1)} %bitcast.171, bf16[384,288,128]{2,1,0:T(8,128)(2,1)} %bitcast.172, ...), custom_call_target="tpu_custom_call" | custom-call | tf_op jit(solution)/shard_map/assemble/pallas_call | solution.py:150
  166.6 8.5 %assemble.14 = bf16[768,3072]{1,0:T(8,128)(2,1)} custom-call(s32[384]{0:T(512)} %owner_ref.15, bf16[384,288,128]{2,1,0:T(8,128)(2,1)} %bitcast.178, bf16[384,288,128]{2,1,0:T(8,128)(2,1)} %bitcast.177, bf16[384,288,128]{2,1,0:T(8,128)(2,1)} %bitcast.176, bf16[384,288,128]{2,1,0:T(8,128)(2,1)} %bitcast.179, bf16[384,288,128]{2,1,0:T(8,128)(2,1)} %bitcast.180, ...), custom_call_target="tpu_custom_call" | custom-call | tf_op jit(solution)/shard_map/assemble/pallas_call | solution.py:150
  175.0 8.7 %assemble.11 = bf16[3072,768]{1,0:T(8,128)(2,1)} custom-call(s32[384]{0:T(512)} %owner_ref.15, bf16[384,288,128]{2,1,0:T(8,128)(2,1)} %bitcast.184, bf16[384,288,128]{2,1,0:T(8,128)(2,1)} %bitcast.185, bf16[384,288,128]{2,1,0:T(8,128)(2,1)} %bitcast.186, bf16[384,288,128]{2,1,0:T(8,128)(2,1)} %bitcast.187, bf16[384,288,128]{2,1,0:T(8,128)(2,1)} %bitcast.188, ...), custom_call_target="tpu_custom_call" | custom-call | tf_op jit(solution)/shard_map/assemble/pallas_call | solution.py:150
  183.8 8.8 %assemble.10 = bf16[768,3072]{1,0:T(8,128)(2,1)} custom-call(s32[384]{0:T(512)} %owner_ref.15, bf16[384,288,128]{2,1,0:T(8,128)(2,1)} %bitcast.192, bf16[384,288,128]{2,1,0:T(8,128)(2,1)} %bitcast.193, bf16[384,288,128]{2,1,0:T(8,128)(2,1)} %bitcast.194, bf16[384,288,128]{2,1,0:T(8,128)(2,1)} %bitcast.195, bf16[384,288,128]{2,1,0:T(8,128)(2,1)} %bitcast.196, ...), custom_call_target="tpu_custom_call" | custom-call | tf_op jit(solution)/shard_map/assemble/pallas_call | solution.py:150
  192.7 0.8 fusion.25
  194.0 5.7 fusion.14.qkv_ref
  199.8 10.1 %attend.2 = (bf16[512,768]{1,0:T(8,128)(2,1)}, f32[512,768]{1,0:T(8,128)}) custom-call(bf16[512,2304]{1,0:T(8,128)(2,1)} %fusion.14.qkv_ref), custom_call_target="tpu_custom_call" | custom-call | tf_op jit(solution)/shard_map/attend/pallas_call | solution.py:236
  209.9 2.2 fusion.26
  213.1 7.1 %multiply_convert_fusion.1 = (bf16[512,3072]{1,0:T(8,128)(2,1)S(1)}, f32[512,3072]{1,0:T(8,128)}) fusion(f32[3072]{0:T(1024)S(1)} %bitcast.232, bf16[512,768]{1,0:T(8,128)(2,1)S(1)} %fusion.17.left_ref, bf16[768,3072]{1,0:T(8,128)(2,1)} %assemble.10), kind=kOutput, calls=%fused_computation.18 | convolution fusion | flops 2425356288 | bytes 14954496 | tf_op jit(solution)/shard_map/dot_general | solution.py:205
  220.3 2.8 fusion.27
  224.1 1.0 copy-done.5
  225.1 3.5 fusion.12.qkv_ref
  228.6 10.1 %attend.3 = (bf16[512,768]{1,0:T(8,128)(2,1)}, f32[512,768]{1,0:T(8,128)}) custom-call(bf16[512,2304]{1,0:T(8,128)(2,1)} %fusion.12.qkv_ref), custom_call_target="tpu_custom_call" | custom-call | tf_op jit(solution)/shard_map/attend/pallas_call | solution.py:236
  238.7 2.1 fusion.28
  241.8 5.9 multiply_convert_fusion
  247.8 2.8 fusion.29
  252.7 1.7 convert_reduce_fusion.4
  254.3 5.1 convert_reduce_fusion
  259.5 3.1 multiply_reduce_fusion.1
  262.7 1.7 convert_reduce_fusion.5
  264.3 1.7 convolution_convert_fusion.1.grad_ref
  266.1 14.9 %attend_back.2.right_ref = bf16[512,2304]{1,0:T(8,128)(2,1)} custom-call(bf16[512,2304]{1,0:T(8,128)(2,1)} %fusion.12.qkv_ref, f32[512,768]{1,0:T(8,128)} %get-tuple-element.19.lse_ref, bf16[512,768]{1,0:T(8,128)(2,1)} %convolution_convert_fusion.1.grad_ref), custom_call_target="tpu_custom_call" | custom-call | tf_op jit(solution)/shard_map/attend_back/pallas_call | solution.py:278
  281.0 2.2 convert_reduce_fusion.2
  283.4 5.2 multiply_reduce_fusion.2
  289.3 4.8 convert_reduce_fusion.1
  294.2 3.1 multiply_reduce_fusion.3
  297.3 1.7 convert_reduce_fusion.7
  299.0 1.7 convolution_convert_fusion.grad_ref
  300.8 15.0 %attend_back.3.right_ref = bf16[512,2304]{1,0:T(8,128)(2,1)} custom-call(bf16[512,2304]{1,0:T(8,128)(2,1)} %fusion.14.qkv_ref, f32[512,768]{1,0:T(8,128)} %get-tuple-element.20.lse_ref, bf16[512,768]{1,0:T(8,128)(2,1)} %convolution_convert_fusion.grad_ref), custom_call_target="tpu_custom_call" | custom-call | tf_op jit(solution)/shard_map/attend_back/pallas_call | solution.py:278
  315.7 2.2 convert_reduce_fusion.3
  318.1 2.0 add_bitcast_fusion
  320.1 2.8 copy.42
  323.0 1.2 copy.47
  324.7 5.4 reduce.47
  330.2 1.0 reshape.348
  331.2 4.2 all-to-all-start.1
  335.8 9.9 %weight_grad.8.refs_0_ = bf16[392,288,128]{2,1,0:T(8,128)(2,1)} custom-call(s32[384]{0:T(512)} %fusion.22.rows_ref, bf16[512,3072]{1,0:T(8,128)(2,1)} %copy-done.15, bf16[512,768]{1,0:T(8,128)(2,1)} %copy-done.18), custom_call_target="tpu_custom_call" | custom-call | tf_op jit(solution)/shard_map/weight_grad/pallas_call | solution.py:356
  345.7 10.0 %weight_grad.9.refs_0_ = bf16[392,288,128]{2,1,0:T(8,128)(2,1)} custom-call(s32[384]{0:T(512)} %fusion.22.rows_ref, bf16[512,768]{1,0:T(8,128)(2,1)} %copy-done.8, bf16[512,3072]{1,0:T(8,128)(2,1)} %copy-done.13, bf16[392,288,128]{2,1,0:T(8,128)(2,1)} %weight_grad.8.refs_0_), custom_call_target="tpu_custom_call", output_to_operand_aliasing={{}: (3, {})} | custom-call | tf_op jit(solution)/shard_map/weight_grad/pallas_call | solution.py:356
  355.6 4.5 weight_grad.10.refs_0_
  360.1 8.1 %weight_grad.11.refs_0_ = bf16[392,288,128]{2,1,0:T(8,128)(2,1)} custom-call(s32[384]{0:T(512)} %fusion.22.rows_ref, bf16[512,768]{1,0:T(8,128)(2,1)} %copy-done.7, bf16[512,2304]{1,0:T(8,128)(2,1)} %attend_back.2.right_ref, bf16[392,288,128]{2,1,0:T(8,128)(2,1)} %weight_grad.10.refs_0_), custom_call_target="tpu_custom_call", output_to_operand_aliasing={{}: (3, {})} | custom-call | tf_op jit(solution)/shard_map/weight_grad/pallas_call | solution.py:356
  368.2 9.7 %weight_grad.12.refs_0_ = bf16[392,288,128]{2,1,0:T(8,128)(2,1)} custom-call(s32[384]{0:T(512)} %fusion.22.rows_ref, bf16[512,3072]{1,0:T(8,128)(2,1)} %copy-done.12, bf16[512,768]{1,0:T(8,128)(2,1)} %copy-done.10, bf16[392,288,128]{2,1,0:T(8,128)(2,1)} %weight_grad.11.refs_0_), custom_call_target="tpu_custom_call", output_to_operand_aliasing={{}: (3, {})} | custom-call | tf_op jit(solution)/shard_map/weight_grad/pallas_call | solution.py:356
  378.0 9.9 %weight_grad.13.refs_0_ = bf16[392,288,128]{2,1,0:T(8,128)(2,1)} custom-call(s32[384]{0:T(512)} %fusion.22.rows_ref, bf16[512,768]{1,0:T(8,128)(2,1)} %copy-done.6, bf16[512,3072]{1,0:T(8,128)(2,1)} %copy-done.14, bf16[392,288,128]{2,1,0:T(8,128)(2,1)} %weight_grad.12.refs_0_), custom_call_target="tpu_custom_call", output_to_operand_aliasing={{}: (3, {})} | custom-call | tf_op jit(solution)/shard_map/weight_grad/pallas_call | solution.py:356
  387.9 4.5 weight_grad.14.refs_0_
  392.4 8.1 %weight_grad.15 = bf16[392,288,128]{2,1,0:T(8,128)(2,1)} custom-call(s32[384]{0:T(512)} %fusion.22.rows_ref, bf16[512,768]{1,0:T(8,128)(2,1)} %bitcast.left_ref, bf16[512,2304]{1,0:T(8,128)(2,1)} %attend_back.3.right_ref, bf16[392,288,128]{2,1,0:T(8,128)(2,1)} %weight_grad.14.refs_0_), custom_call_target="tpu_custom_call", output_to_operand_aliasing={{}: (3, {})} | custom-call | tf_op jit(solution)/shard_map/weight_grad/pallas_call | solution.py:356
  400.6 0.9 broadcast_dynamic-update-slice_fusion
  401.5 152.9 %reduce_slots.1 = bf16[14112,128]{1,0:T(8,128)(2,1)} custom-call(bf16[2,2,2,14112,128]{4,3,2,1,0:T(8,128)(2,1)} %bitcast.201), custom_call_target="tpu_custom_call" | custom-call | bytes 300000000 | tf_op jit(solution)/shard_map/reduce_slots/pallas_call | solution.py:685
  554.5 0.9 copy-done.16
  555.3 3.8 all-to-all-start.3
  559.2 0.9 slice_convert_fusion
  560.2 38.0 %soap.1 = (f32[6,2304,128]{2,1,0:T(8,128)}, f32[6,2304,128]{2,1,0:T(8,128)}, f32[6,2304,128]{2,1,0:T(8,128)}, bf16[6,2304,128]{2,1,0:T(8,128)(2,1)}) custom-call(f32[6,2304,128]{2,1,0:T(8,128)} %bitcast.203, f32[6,2304,128]{2,1,0:T(8,128)} %bitcast.206, f32[6,2304,128]{2,1,0:T(8,128)} %bitcast.207, f32[6,2304,128]{2,1,0:T(8,128)} %bitcast.208, ...), custom_call_target="tpu_custom_call" | custom-call | tf_op jit(solution)/shard_map/soap/pallas_call | solution.py:456
  598.1 0.9 divide_subtract_fusion
  599.0 2.4 reshape.349
  601.5 1.0 copy.44
  602.5 1.2 copy.45
  (199 shorter events, 10.0 us)
Async XLA Ops:
  0.6 6.5 %copy-start.49 = (s32[4]{0:T(128)S(1)}, s32[4]{0:T(128)}, u32[]{:S(2)}) copy-start(s32[4]{0:T(128)} %param.16) | copy-start | bytes 52
  0.7 7.2 %copy-start.48 = (s32[4,128]{1,0:T(4,128)S(1)}, s32[4,128]{1,0:T(4,128)}, u32[]{:S(2)}) copy-start(s32[4,128]{1,0:T(4,128)} %param.15) | copy-start | bytes 6148
  0.7 32.1 %copy-start.24 = (f32[2,9216]{1,0:T(2,128)S(1)}, f32[2,9216]{1,0:T(2,128)}, u32[]{:S(2)}) copy-start(f32[2,9216]{1,0:T(2,128)} %param.23) | copy-start | bytes 221188
  0.7 32.8 %copy-start.26 = (s32[384]{0:T(512)S(1)}, s32[384]{0:T(512)}, u32[]{:S(2)}) copy-start(s32[384]{0:T(512)} %owner_ref.15) | copy-start | bytes 4612
  0.7 34.0 %all-to-all-start.2 = ((bf16[4,128,768]{2,1,0:T(8,128)(2,1)}), bf16[4,128,768]{2,1,0:T(8,128)(2,1)S(1)}, u32[]{:S(2)}, u32[]{:S(2)}) async-start(bf16[4,128,768]{2,1,0:T(8,128)(2,1)} %param.14), calls=%async_computation.2 | async-start | bytes 1572864 | tf_op jit(solution)/shard_map/all_to_all | solution.py:965
  32.7 15.6 %copy-start.37 = (f32[1,512]{1,0:T(1,128)}, f32[1,512]{1,0:T(1,128)S(1)}, u32[]{:S(2)}) copy-start(f32[1,512]{1,0:T(1,128)S(1)} %dynamic-slice_convert_fusion) | copy-start | bytes 6148
  34.7 13.6 %copy-start.2 = (bf16[4,128,768]{2,1,0:T(8,128)(2,1)}, bf16[4,128,768]{2,1,0:T(8,128)(2,1)S(1)}, u32[]{:S(2)}) copy-start(bf16[4,128,768]{2,1,0:T(8,128)(2,1)S(1)} %all-to-all-done.2) | copy-start | bytes 2359300
  34.7 159.3 %all-to-all-start = ((bf16[4,128,768]{2,1,0:T(8,128)(2,1)}), bf16[4,128,768]{2,1,0:T(8,128)(2,1)}, u32[]{:S(2)}, u32[]{:S(2)}) async-start(bf16[4,128,768]{2,1,0:T(8,128)(2,1)} %param.13), calls=%async_computation | async-start | bytes 1572864 | tf_op jit(solution)/shard_map/all_to_all | solution.py:965
  183.7 8.9 %copy-start.31 = (f32[6,3,128]{2,0,1:T(8,128)S(1)}, f32[6,3,128]{2,0,1:T(8,128)}, u32[]{:S(2)}) copy-start(f32[6,3,128]{2,0,1:T(8,128)} %get-tuple-element.81) | copy-start | bytes 27652
  183.7 8.9 %copy-start.30 = (f32[6,3,128]{2,0,1:T(8,128)S(1)}, f32[6,3,128]{2,0,1:T(8,128)}, u32[]{:S(2)}) copy-start(f32[6,3,128]{2,0,1:T(8,128)} %get-tuple-element.82) | copy-start | bytes 27652
  183.8 9.8 %copy-start.3 = (bf16[4,128,768]{2,1,0:T(8,128)(2,1)S(1)}, bf16[4,128,768]{2,1,0:T(8,128)(2,1)}, u32[]{:S(2)}) copy-start(bf16[4,128,768]{2,1,0:T(8,128)(2,1)} %copy-done.2) | copy-start | bytes 2359300
  183.8 9.8 %copy-start.29 = (f32[768]{0:T(1024)S(1)}, f32[768]{0:T(1024)}, u32[]{:S(2)}) copy-start(f32[768]{0:T(1024)} %get-tuple-element.41) | copy-start | bytes 9220
  183.8 9.8 %copy-start.43 = (f32[4,128]{1,0:T(4,128)S(1)}, f32[4,128]{1,0:T(4,128)}, u32[]{:S(2)}) copy-start(f32[4,128]{1,0:T(4,128)} %multiply_multiply_fusion.3) | copy-start | bytes 6148
  199.8 10.1 %copy-start.20 = (bf16[768,768]{1,0:T(8,128)(2,1)S(1)}, bf16[768,768]{1,0:T(8,128)(2,1)}, u32[]{:S(2)}) copy-start(bf16[768,768]{1,0:T(8,128)(2,1)} %assemble.9) | copy-start | bytes 3538948
  199.8 10.1 %copy-start.47 = (f32[768]{0:T(1024)S(1)}, f32[768]{0:T(1024)}, u32[]{:S(2)}) copy-start(f32[768]{0:T(1024)} %get-tuple-element.53) | copy-start | bytes 9220
  212.1 0.7 copy-start.34
  212.1 0.7 copy-start.41
  212.1 8.1 %slice-start.2 = ((s8[4718592]{0:T(1024)(128)(4,1)}), s8[4194304]{0:T(1024)(128)(4,1)S(1)}, s32[]{:S(2)}) async-start(s8[4718592]{0:T(1024)(128)(4,1)} %bitcast.214), calls=%async_computation.6 | async-start | bytes 8388608
  213.1 7.1 %copy-start.6 = (bf16[512,768]{1,0:T(8,128)(2,1)}, bf16[512,768]{1,0:T(8,128)(2,1)S(1)}, u32[]{:S(2)}) copy-start(bf16[512,768]{1,0:T(8,128)(2,1)S(1)} %fusion.17.left_ref) | copy-start | bytes 2359300
  213.1 7.1 %slice-start.3 = ((s8[4718592]{0:T(1024)(128)(4,1)}), s8[524288]{0:T(1024)(128)(4,1)S(1)}, s32[]{:S(2)}) async-start(s8[4718592]{0:T(1024)(128)(4,1)} %bitcast.214), calls=%async_computation.7 | async-start | bytes 1048576
  213.1 7.1 %copy-start.46 = (f32[768]{0:T(1024)S(1)}, f32[768]{0:T(1024)}, u32[]{:S(2)}) copy-start(f32[768]{0:T(1024)} %get-tuple-element.50) | copy-start | bytes 9220
  220.2 2.8 copy-start.12
  223.1 0.7 copy-start.40
  223.1 2.0 copy-start.5
  225.1 3.5 copy-start.7
  228.6 10.1 %copy-start.22 = (bf16[768,768]{1,0:T(8,128)(2,1)S(1)}, bf16[768,768]{1,0:T(8,128)(2,1)}, u32[]{:S(2)}) copy-start(bf16[768,768]{1,0:T(8,128)(2,1)} %assemble.13) | copy-start | bytes 3538948
  228.6 10.1 %copy-start.45 = (f32[768]{0:T(1024)S(1)}, f32[768]{0:T(1024)}, u32[]{:S(2)}) copy-start(f32[768]{0:T(1024)} %get-tuple-element.45) | copy-start | bytes 9220
  240.8 0.7 copy-start.36
  240.8 0.7 copy-start.39
  240.8 6.9 %slice-start.8 = ((s8[4718592]{0:T(1024)(128)(4,1)}), s8[4194304]{0:T(1024)(128)(4,1)S(1)}, s32[]{:S(2)}) async-start(s8[4718592]{0:T(1024)(128)(4,1)} %bitcast.220), calls=%async_computation.12 | async-start | bytes 8388608
  241.8 5.9 copy-start.8
  241.8 5.9 slice-start.9
  241.8 5.9 copy-start.44
  247.7 2.9 copy-start.15
  250.9 1.7 copy-start.42
  252.7 6.8 %slice-start.6 = ((s8[4718592]{0:T(1024)(128)(4,1)}), s8[4194304]{0:T(1024)(128)(4,1)S(1)}, s32[]{:S(2)}) async-start(s8[4718592]{0:T(1024)(128)(4,1)} %bitcast.218), calls=%async_computation.10 | async-start | bytes 8388608
  254.3 5.1 copy-start.18
  254.3 5.1 slice-start.7
  259.5 3.2 copy-start.13
  262.6 1.7 copy-start.23
  262.7 26.5 %slice-start.4 = ((s8[4718592]{0:T(1024)(128)(4,1)}), s8[4194304]{0:T(1024)(128)(4,1)S(1)}, s32[]{:S(2)}) async-start(s8[4718592]{0:T(1024)(128)(4,1)} %bitcast.216), calls=%async_computation.8 | async-start | bytes 8388608
  264.3 1.7 copy-start.9
  281.0 2.4 copy-start
  281.0 8.2 %slice-start.10 = ((s8[6291456]{0:T(1024)(128)(4,1)}), s8[4194304]{0:T(1024)(128)(4,1)S(1)}, s32[]{:S(2)}) async-start(s8[6291456]{0:T(1024)(128)(4,1)} %bitcast.240), calls=%async_computation.14 | async-start | bytes 8388608
  283.4 5.9 slice-start.5
  283.4 5.9 slice-start.11
  288.6 5.5 slice-start
  289.2 4.9 copy-start.10
  289.2 4.9 slice-start.1
  294.1 3.2 copy-start.14
  297.3 1.7 copy-start.21
  299.0 1.8 copy-start.11
  300.7 17.2 %copy-start.4 = (bf16[768,2304]{1,0:T(8,128)(2,1)S(1)}, bf16[768,2304]{1,0:T(8,128)(2,1)}, u32[]{:S(2)}) copy-start(bf16[768,2304]{1,0:T(8,128)(2,1)} %assemble.8) | copy-start | bytes 10616836
  300.7 17.2 %copy-start.19 = (f32[512,768]{1,0:T(8,128)S(1)}, f32[512,768]{1,0:T(8,128)}, u32[]{:S(2)}) copy-start(f32[512,768]{1,0:T(8,128)} %get-tuple-element.71) | copy-start | bytes 4718596
  315.7 2.4 copy-start.1
  320.1 2.9 copy-start.17
  330.2 5.2 copy-start.33
  330.2 5.4 copy-start.32
  331.2 223.3 %all-to-all-start.1 = ((bf16[4,2,49152]{2,1,0:T(2,128)(2,1)}), bf16[4,2,49152]{2,1,0:T(2,128)(2,1)S(1)}, u32[]{:S(2)}, u32[]{:S(2)}) async-start(bf16[4,2,49152]{2,1,0:T(2,128)(2,1)} %reshape.348), calls=%async_computation.1 | async-start | bytes 1572864 | tf_op jit(solution)/shard_map/all_to_all | solution.py:969
  554.4 0.9 copy-start.16
  555.3 47.1 %all-to-all-start.3 = ((f32[1,512,768]{2,0,1:T(1,128)}), f32[1,512,768]{2,0,1:T(1,128)S(1)}, u32[]{:S(2)}, u32[]{:S(2)}) async-start(f32[1,512,768]{2,0,1:T(1,128)} %copy.42), calls=%async_computation.3 | async-start | bytes 3145728 | tf_op jit(solution)/shard_map/all_to_all | solution.py:969
  560.1 38.0 %copy-start.25 = (f32[2,9216]{1,0:T(2,128)S(1)}, f32[2,9216]{1,0:T(2,128)}, u32[]{:S(2)}) copy-start(f32[2,9216]{1,0:T(2,128)} %param.23) | copy-start | bytes 221188
  560.1 38.0 %copy-start.27 = (f32[2,9216]{1,0:T(2,128)S(1)}, f32[2,9216]{1,0:T(2,128)}, u32[]{:S(2)}) copy-start(f32[2,9216]{1,0:T(2,128)} %param.24) | copy-start | bytes 221188
  560.1 38.0 %copy-start.28 = (f32[2,9216]{1,0:T(2,128)S(1)}, f32[2,9216]{1,0:T(2,128)}, u32[]{:S(2)}) copy-start(f32[2,9216]{1,0:T(2,128)} %param.25) | copy-start | bytes 221188
  (2 other events, 1.4 us)

commit v3 on v2

--- a/solution.py
+++ b/solution.py
@@ -16,6 +16,8 @@
 GROUP = 8
 GATHER_ROWS = 144
 GATHER_LAG = 2
+ALONE_SHARE = 0.28
+SPREAD = 3
 REDUCE_ROWS = 144
 REDUCE_LAG = 2
 WAIT_BYTES = 3 * 10**8
@@ -129,13 +131,18 @@
 
 def assemble_kernel(cells, owner_ref, *refs):
     out_ref = refs[-1]
+    low = low_lanes(HALF)
     for number, (row, lanes) in enumerate(cells):
-        main_a, tail_a = unfold(refs[2 * number][0])
-        main_b, tail_b = unfold(refs[2 * number + 1][0])
-        rows = pl.ds(row, BLK)
-        out_ref[rows, pl.ds(lanes[0], LANE)] = main_a
-        out_ref[rows, pl.ds(lanes[1], LANE)] = jnp.concatenate([tail_a, main_b[:, :HDIM]], axis=1)
-        out_ref[rows, pl.ds(lanes[2], LANE)] = jnp.concatenate([main_b[:, HDIM:], tail_b], axis=1)
+        left, right = refs[2 * number], refs[2 * number + 1]
+        fold_a = left[0, BLK:PACK, :].astype(f32)
+        fold_b = right[0, BLK:PACK, :].astype(f32)
+        tails = [(fold_a, swap(fold_b)), (swap(fold_a), fold_b)]
+        out_ref[pl.ds(row, BLK), pl.ds(lanes[0], LANE)] = left[0, 0:BLK, :]
+        for half, (tail_a, tail_b) in enumerate(tails):
+            main_b = swap(right[0, half * HALF : (half + 1) * HALF, :].astype(f32))
+            rows = pl.ds(row + half * HALF, HALF)
+            out_ref[rows, pl.ds(lanes[1], LANE)] = jnp.where(low, tail_a, main_b).astype(bf16)
+            out_ref[rows, pl.ds(lanes[2], LANE)] = jnp.where(low, main_b, tail_b).astype(bf16)
 
 
 def assemble(gathered, owner_list, shape, tile, cells, block_of):
@@ -291,7 +298,7 @@
 
 
 def weight_grad_kernel(lanes_of, block_of, panel, steps, rows_ref, left_ref, right_ref, *refs):
-    out_ref, stage_ref, sems = refs[-3:]
+    out_ref, stage_ref, turned_ref, sems = refs[-4:]
     i, j = pl.program_id(0), pl.program_id(1)
     step = i * pl.num_programs(1) + j
     spot = lax.rem(step, 2)
@@ -308,7 +315,11 @@
         for which in range(count):
             copy(which, spot, 0).wait()
 
-    left = left_ref[:, pl.ds(pl.multiple_of(2 * BLK * i, LANE), 2 * BLK)]
+    @pl.when(j == 0)
+    def _():
+        turned_ref[...] = left_ref[...].T
+
+    left = turned_ref[...]
     low_top, low_all = low_lanes(HALF), low_lanes(BLK)
     for pair in range(pairs):
         right = jnp.concatenate(
@@ -318,7 +329,7 @@
             ],
             axis=1,
         )
-        product = dot(left, right, 0, 0)
+        product = dot(left, right)
         for half in range(2):
             tile = product[half * BLK : (half + 1) * BLK, :]
             first, second, third = (tile[:, LANE * part : LANE * (part + 1)] for part in range(3))
@@ -345,10 +356,10 @@
                 copy(which, 1 - spot, 0).wait()
 
 
-def weight_grad(slots, slot_shape, rows, left, right, grid, panel, lanes_of, block_of):
+def weight_grad(slots, slot_shape, rows, left, right, grid, panel, right_spec, lanes_of, block_of):
     steps = grid[0] * grid[1]
     count = 4 * (panel // (2 * BLK))
-    whole = [pl.BlockSpec(left.shape, lambda i, j, s: (0, 0)), pl.BlockSpec(right.shape, lambda i, j, s: (0, 0))]
+    whole = [pl.BlockSpec((left.shape[0], 2 * BLK), lambda i, j, s: (0, i)), right_spec]
     extra, aliases = [], {}
     if slots is not None:
         extra = [slots]
@@ -362,6 +373,7 @@
             out_specs=pl.BlockSpec(memory_space=pl.ANY),
             scratch_shapes=[
                 pltpu.VMEM((2, count, PACK, LANE), bf16),
+                pltpu.VMEM((2 * BLK, left.shape[0]), bf16),
                 pltpu.SemaphoreType.DMA((2, count)),
             ],
         ),
@@ -383,7 +395,8 @@
         right,
         (left.shape[1] // (2 * BLK), right.shape[1] // width),
         width,
-        lambda j, piece: j * width + piece * LANE,
+        pl.BlockSpec((right.shape[0], width), lambda i, j, s: (0, j)),
+        lambda j, piece: piece * LANE,
         lambda i, j, half, col: base + (2 * i + half) * cols + j * per + col,
     )
 
@@ -398,6 +411,7 @@
         right,
         (width // (2 * BLK), 3),
         width,
+        pl.BlockSpec(right.shape, lambda i, j, s: (0, 0)),
         lambda j, piece: 3 * LANE * piece + LANE * j,
         lambda i, j, half, col: base + j * per * per + (2 * i + half) * per + col,
     )
@@ -415,7 +429,7 @@
         refs[1][:, :HDIM] = value[:, LANE:]
 
     for row in range(GROUP):
-        spot = row % 2
+        spot = row
         left_refs = [left_sq.at[spot, 0], left_sq.at[spot, 1]]
         right_refs = [right_sq.at[spot, 0], right_sq.at[spot, 1]]
         refs = [work.at[spot, 0], work.at[spot, 1]]
@@ -452,7 +466,7 @@
     groups = views[0].shape[0]
     view_spec = pl.BlockSpec((1, GROUP * PACK, LANE), lambda i: (i, 0, 0))
     shape = (groups, GROUP * PACK, LANE)
-    square = pltpu.VMEM((2, 2, BLK, LANE), f32)
+    square = pltpu.VMEM((GROUP, 2, BLK, LANE), f32)
     return pl.pallas_call(
         soap_kernel,
         grid=(groups,),
@@ -480,26 +494,52 @@
     return {"dp": (row * size[1] + col) * 2 + core, "seq": depth}
 
 
-def greet(partners, layers, level, above, below):
+def greet(partners):
     barrier = pltpu.get_barrier_semaphore()
     for partner in partners:
         pl.semaphore_signal(barrier, inc=1, device_id=partner, device_id_type=MESH)
-
-    @pl.when(level > 0)
-    def _():
-        pl.semaphore_signal(barrier, inc=1, device_id=below, device_id_type=MESH)
-
-    @pl.when(level < layers - 1)
-    def _():
-        pl.semaphore_signal(barrier, inc=1, device_id=above, device_id_type=MESH)
-
-    inner = (level > 0).astype(jnp.int32) + (level < layers - 1).astype(jnp.int32)
-    pl.semaphore_wait(barrier, len(partners) + inner)
+    pl.semaphore_wait(barrier, len(partners))
+
+
+def send_to(source, target, send, recv, where):
+    return pltpu.make_async_remote_copy(
+        src_ref=source,
+        dst_ref=target,
+        send_sem=send,
+        recv_sem=recv,
+        device_id=where,
+        device_id_type=MESH,
+    )
+
+
+def exchange(level, layers, pairs, keep_sem, send, recv):
+    copies = []
+    for which, (source, target) in enumerate(pairs):
+        copies.append(
+            pltpu.make_async_copy(source.at[level], target.at[level], keep_sem.at[which])
+        )
+        for hop in range(layers - 1):
+            to = lax.rem(level + hop + 1, layers)
+            copies.append(
+                send_to(
+                    source.at[to], target.at[level],
+                    send.at[which, hop], recv.at[which, hop], {"seq": to},
+                )
+            )
+    return copies
+
+
+def exchange_sems(count, layers):
+    return [
+        pltpu.SemaphoreType.DMA((count,)),
+        pltpu.SemaphoreType.DMA((count, layers - 1)),
+        pltpu.SemaphoreType.DMA((count, layers - 1)),
+    ]
 
 
 def reduce_kernel(
-    steps, rows, layers, lag, slots_ref, out_ref, own, inbox, first, second, up, down, down_sum,
-    own_sem, core_send, core_recv, one_send, one_recv, two_send, two_recv,
+    steps, rows, layers, lag, slots_ref, last_ref, grad_ref, out_ref, last_out, grad_out,
+    own, inbox, first, second, up, down, down_sum, keep_sem, swap_send, swap_recv, own_sem, core_send, core_recv, one_send, one_recv, two_send, two_recv,
     up_send, up_recv, down_send, down_recv,
 ):
     size = (2, 2)
@@ -516,14 +556,7 @@
         return pl.ds(pl.multiple_of((half * steps + step) * rows, rows), rows)
 
     def remote(source, target, send, recv, half, step, where):
-        return pltpu.make_async_remote_copy(
-            src_ref=source,
-            dst_ref=target,
-            send_sem=send.at[half, step],
-            recv_sem=recv.at[half, step],
-            device_id=where,
-            device_id_type=MESH,
-        )
+        return send_to(source, target, send.at[half, step], recv.at[half, step], where)
 
     def own_copy(half, step):
         part = span(half, step)
@@ -559,7 +592,15 @@
     def inside(step):
         return jnp.logical_and(step >= 0, step < steps)
 
-    greet([other_core, across_x, across_y], layers, level, above, below)
+    peers = [
+        device(y, x, core, size, lax.rem(level + hop + 1, layers)) for hop in range(layers - 1)
+    ]
+    greet([other_core, across_x, across_y] + peers)
+    moves = exchange(
+        level, layers, [(last_ref, last_out), (grad_ref, grad_out)], keep_sem, swap_send, swap_recv
+    )
+    for move in moves:
+        move.start()
 
     @pl.loop(0, steps)
     def _(step):
@@ -661,6 +702,9 @@
             for half in range(2):
                 down_copy(half, down_step).start()
 
+    for move in moves:
+        move.wait()
+
     @pl.loop(0, steps)
     def _(step):
         for half in range(2):
@@ -677,34 +721,42 @@
                 down_copy(half, step).wait_send()
 
 
-def reduce_slots(slots, layers, rows, lag):
+def reduce_slots(slots, last, grad, layers, rows, lag):
     total = slots.shape[0] // 8 * PACK
     steps = total // (2 * rows)
     chunk = (total, LANE)
     sems = pltpu.SemaphoreType.DMA((2, steps))
-    out = pl.pallas_call(
+    anywhere = pl.BlockSpec(memory_space=pl.ANY)
+    out, last, grad = pl.pallas_call(
         functools.partial(reduce_kernel, steps, rows, layers, lag),
-        in_specs=[pl.BlockSpec(memory_space=pl.ANY)],
-        out_specs=pl.BlockSpec(memory_space=pltpu.VMEM),
-        out_shape=jax.ShapeDtypeStruct(chunk, bf16),
+        in_specs=[anywhere] * 3,
+        out_specs=[pl.BlockSpec(memory_space=pltpu.VMEM), anywhere, anywhere],
+        out_shape=[
+            jax.ShapeDtypeStruct(chunk, bf16),
+            jax.ShapeDtypeStruct(last.shape, last.dtype),
+            jax.ShapeDtypeStruct(grad.shape, grad.dtype),
+        ],
         scratch_shapes=[
             pltpu.VMEM((2, 2) + chunk, bf16),
             pltpu.VMEM((2, 2) + chunk, bf16),
             pltpu.VMEM((2,) + chunk, bf16),
         ]
         + [pltpu.VMEM(chunk, bf16)] * 4
+        + exchange_sems(2, layers)
         + [sems] * 11,
         compiler_params=pltpu.CompilerParams(
             vmem_limit_bytes=62 * 2**20, collective_id=0, has_side_effects=True
         ),
         cost_estimate=pl.CostEstimate(flops=0, bytes_accessed=WAIT_BYTES, transcendentals=0),
         name="reduce_slots",
-    )(slots.reshape((2, 2, 2) + chunk))
-    return out.reshape(total // PACK, PACK, LANE)
+    )(slots.reshape((2, 2, 2) + chunk), last, grad)
+    return out.reshape(total // PACK, PACK, LANE), last, grad
 
 
 def gather_kernel(
-    steps, rows, lag, mine_ref, out_ref, own_sem, one_send, one_recv, two_send, two_recv,
+    alone, steps, rows, lag, layers, mine_ref, token_ref, cot_ref, weight_ref,
+    out_ref, token_out, cot_out, weight_out, own_sem, keep_sem, swap_send, swap_recv,
+    one_send, one_recv, two_send, two_recv,
     near_send, near_recv, far_send, far_recv, core_send, core_recv,
 ):
     size = (2, 2)
@@ -717,66 +769,61 @@
     beside = device(y, x, core, size, level + 1 - 2 * side)
     firsts, seconds = [across_x, across_y], [across_y, across_x]
 
-    def span(kind, half, step):
-        return pl.ds(pl.multiple_of(((kind * 2 + half) * steps + step) * rows, rows), rows)
-
-    def kind_of(turn):
-        late = lax.div(turn, steps)
-        return side + (2 - side) * late, lax.rem(turn, steps)
-
-    def remote(source, target, send, recv, where):
-        return pltpu.make_async_remote_copy(
-            src_ref=source,
-            dst_ref=target,
-            send_sem=send,
-            recv_sem=recv,
-            device_id=where,
-            device_id_type=MESH,
-        )
+    half_rows = (2 * alone + steps) * rows
+    turns = alone + steps
+
+    def span(half, step):
+        return pl.ds(pl.multiple_of(half * half_rows + step * rows, rows), rows)
+
+    def place_of(turn):
+        late = jnp.where(turn >= alone, 1, 0)
+        return turn + side * alone * (1 - late) + alone * late
+
+    def given_place(step):
+        return (1 - side) * alone + step
 
     def own_copy():
         return pltpu.make_async_copy(mine_ref, out_ref.at[y, x, core], own_sem)
 
     def one_copy(half, turn):
-        kind, step = kind_of(turn)
-        part = span(kind, half, step)
-        return remote(
+        part = span(half, place_of(turn))
+        return send_to(
             mine_ref.at[part], out_ref.at[y, x, core, part],
             one_send.at[half, turn], one_recv.at[half, turn], firsts[half],
         )
 
     def two_copy(half, turn):
-        kind, step = kind_of(turn)
-        part = span(kind, half, step)
+        part = span(half, place_of(turn))
         ref = out_ref.at[y, :, core, part] if half == 0 else out_ref.at[:, x, core, part]
-        return remote(
+        return send_to(
             ref, ref, two_send.at[half, turn], two_recv.at[half, turn], seconds[half]
         )
 
     def near_copy(half, step):
-        part = span(side, half, step)
+        part = span(half, side * alone + step)
         ref = out_ref.at[y, 1 - x, core, part] if half == 0 else out_ref.at[1 - y, x, core, part]
-        return remote(ref, ref, near_send.at[half, step], near_recv.at[half, step], beside)
+        return send_to(ref, ref, near_send.at[half, step], near_recv.at[half, step], beside)
 
     def far_copy(half, step):
-        part = span(side, half, step)
+        part = span(half, side * alone + step)
         ref = out_ref.at[1 - y, :, core, part] if half == 0 else out_ref.at[:, 1 - x, core, part]
-        return remote(ref, ref, far_send.at[half, step], far_recv.at[half, step], beside)
-
-    def core_copy(kind, half, step, slot):
-        ref = out_ref.at[:, :, core, span(kind, half, step)]
-        return remote(ref, ref, core_send.at[half, slot], core_recv.at[half, slot], other_core)
-
-    partners = [other_core, across_x, across_y, beside]
-    barrier = pltpu.get_barrier_semaphore()
-    for partner in partners:
-        pl.semaphore_signal(barrier, inc=1, device_id=partner, device_id_type=MESH)
-    pl.semaphore_wait(barrier, len(partners))
-
+        return send_to(ref, ref, far_send.at[half, step], far_recv.at[half, step], beside)
+
+    def core_copy(half, step, slot):
+        ref = out_ref.at[:, :, core, span(half, step)]
+        return send_to(ref, ref, core_send.at[half, slot], core_recv.at[half, slot], other_core)
+
+    peers = [
+        device(y, x, core, size, lax.rem(level + hop + 1, layers)) for hop in range(layers - 1)
+    ]
+    greet([other_core, across_x, across_y] + peers)
+    pairs = [(weight_ref, weight_out), (token_ref, token_out), (cot_ref, cot_out)]
+    moves = exchange(level, layers, pairs, keep_sem, swap_send, swap_recv)
     own_copy().start()
-    turns = 2 * steps
-
-    @pl.loop(0, turns + 4 * lag + 2)
+    for move in moves:
+        move.start()
+
+    @pl.loop(0, max(turns + 2 * lag, SPREAD * alone + 4 * lag))
     def _(tick):
         @pl.when(tick < turns)
         def _():
@@ -795,7 +842,7 @@
                 one_copy(half, turn).wait_recv()
                 two_copy(half, turn).start()
 
-        @pl.when(jnp.logical_and(turn >= 0, turn < steps))
+        @pl.when(jnp.logical_and(turn >= 0, turn < alone))
         def _():
             for half in range(2):
                 near_copy(half, turn).start()
@@ -804,63 +851,68 @@
 
         @pl.when(jnp.logical_and(after >= 0, after < turns))
         def _():
-            kind, step = kind_of(after)
             for half in range(2):
                 two_copy(half, after).wait_recv()
-                core_copy(kind, half, step, after).start()
-
-        @pl.when(jnp.logical_and(after >= 0, after < steps))
+                core_copy(half, place_of(after), after).start()
+
+        @pl.when(jnp.logical_and(after >= 0, after < alone))
         def _():
             for half in range(2):
                 far_copy(half, after).start()
 
         late = tick - 4 * lag
-        given = lax.div(late, 2)
-
-        @pl.when(jnp.logical_and(late >= 0, jnp.logical_and(given < steps, late == 2 * given)))
+        given = lax.div(jnp.maximum(late, 0), SPREAD)
+
+        @pl.when(jnp.logical_and(given < alone, late == SPREAD * given))
         def _():
             for half in range(2):
                 near_copy(half, given).wait_recv()
                 far_copy(half, given).wait_recv()
-                core_copy(1 - side, half, given, turns + given).start()
+                core_copy(half, given_place(given), turns + given).start()
+
+    for move in moves:
+        move.wait()
 
     @pl.loop(0, turns)
     def _(turn):
-        kind, step = kind_of(turn)
         for half in range(2):
             one_copy(half, turn).wait_send()
             two_copy(half, turn).wait_send()
-            core_copy(kind, half, step, turn).wait()
-
-    @pl.loop(0, steps)
+            core_copy(half, place_of(turn), turn).wait()
+
+    @pl.loop(0, alone)
     def _(step):
         for half in range(2):
             near_copy(half, step).wait_send()
             far_copy(half, step).wait_send()
-            core_copy(1 - side, half, step, turns + step).wait()
-
-
-def gather_slots(packed, rows, lag):
+            core_copy(half, given_place(step), turns + step).wait()
+
+
+def gather_slots(packed, tokens, cotangent, weight, layers, rows, lag):
     total = packed.shape[0] * PACK
-    steps = total // (6 * rows)
+    alone = int(total // (2 * rows) * ALONE_SHARE)
+    steps = total // (2 * rows) - 2 * alone
 
     def sems(count):
         return [pltpu.SemaphoreType.DMA((2, count))] * 2
 
-    out = pl.pallas_call(
-        functools.partial(gather_kernel, steps, rows, lag),
-        in_specs=[pl.BlockSpec(memory_space=pltpu.VMEM)],
-        out_specs=pl.BlockSpec(memory_space=pl.ANY),
-        out_shape=jax.ShapeDtypeStruct((2, 2, 2, total, LANE), bf16),
+    anywhere = pl.BlockSpec(memory_space=pl.ANY)
+    out, tokens, cotangent, weight = pl.pallas_call(
+        functools.partial(gather_kernel, alone, steps, rows, lag, layers),
+        in_specs=[pl.BlockSpec(memory_space=pltpu.VMEM)] + [anywhere] * 3,
+        out_specs=[anywhere] * 4,
+        out_shape=[jax.ShapeDtypeStruct((2, 2, 2, total, LANE), bf16)]
+        + [jax.ShapeDtypeStruct(array.shape, array.dtype) for array in (tokens, cotangent, weight)],
         scratch_shapes=[pltpu.SemaphoreType.DMA]
-        + sems(2 * steps) + sems(2 * steps) + sems(steps) + sems(steps) + sems(3 * steps),
+        + exchange_sems(3, layers)
+        + sems(alone + steps) * 2 + sems(alone) * 2 + sems(2 * alone + steps),
         compiler_params=pltpu.CompilerParams(
             vmem_limit_bytes=62 * 2**20, collective_id=1, has_side_effects=True
         ),
         cost_estimate=pl.CostEstimate(flops=0, bytes_accessed=WAIT_BYTES, transcendentals=0),
         name="gather_slots",
-    )(packed.reshape(total, LANE))
-    return out.reshape(8 * packed.shape[0], PACK, LANE)
+    )(packed.reshape(total, LANE), tokens, cotangent, weight)
+    return out.reshape(8 * packed.shape[0], PACK, LANE), tokens, cotangent, weight
 
 
 def norm_forward(hidden, gain, shift):
@@ -969,22 +1021,36 @@
     return lax.all_to_all(array, "seq", split_axis=1, concat_axis=0, tiled=True)
 
 
-def near_group():
-    return lax.axis_size("dp") == 8 and lax.axis_size("seq") % 2 == 0
-
-
-def gather_blocks(packed):
+def near_group(seq_count):
+    layers = lax.axis_size("seq")
+    return lax.axis_size("dp") == 8 and layers % 2 == 0 and seq_count == layers
+
+
+def gather_blocks(packed, tokens, cotangent, tok_weight):
+    layers = lax.axis_size("seq")
     total = packed.shape[0] * PACK
-    if near_group() and total % (6 * GATHER_ROWS) == 0:
-        return gather_slots(packed, GATHER_ROWS, GATHER_LAG)
-    return lax.all_gather(packed, "dp", axis=0, tiled=True)
-
-
-def reduce_blocks(slots):
+    if near_group(tokens.shape[0]) and total % (2 * GATHER_ROWS) == 0:
+        gathered, hidden, incoming, weight = gather_slots(
+            packed, tokens, cotangent, tok_weight[:, None, :], layers, GATHER_ROWS, GATHER_LAG
+        )
+        width = tokens.shape[-1]
+        return (
+            gathered, hidden.reshape(1, -1, width), incoming.reshape(1, -1, width), weight.reshape(1, -1)
+        )
+    gathered = lax.all_gather(packed, "dp", axis=0, tiled=True)
+    return gathered, swap_in(tokens), swap_in(cotangent), swap_in(tok_weight)
+
+
+def reduce_blocks(slots, last, grad):
+    layers = lax.axis_size("seq")
     total = slots.shape[0] // lax.axis_size("dp") * PACK
-    if near_group() and total % (2 * REDUCE_ROWS) == 0:
-        return reduce_slots(slots, lax.axis_size("seq"), REDUCE_ROWS, REDUCE_LAG)
-    return lax.psum(lax.psum_scatter(slots, "dp", scatter_dimension=0, tiled=True), "seq")
+    if near_group(last.shape[0] * layers) and total % (2 * REDUCE_ROWS) == 0:
+        shape = (layers, last.shape[1] // layers, last.shape[2])
+        return reduce_slots(
+            slots, last.reshape(shape), grad.reshape(shape), layers, REDUCE_ROWS, REDUCE_LAG
+        )
+    owned = lax.psum(lax.psum_scatter(slots, "dp", scatter_dimension=0, tiled=True), "seq")
+    return owned, swap_out(last), swap_out(grad)
 
 
 def local(
@@ -1012,20 +1078,17 @@
 
     master_view = row_view(masters)
     packed = pack_blocks(master_view)[:owned_count]
-    gathered = gather_blocks(packed)
-
-    hidden = swap_in(tokens)
+    gathered, hidden, incoming, weight = gather_blocks(packed, tokens, cotangent, tok_weight)
+
     per_seq = hidden.shape[0]
     full_len = hidden.shape[1]
     hidden = hidden.reshape(full_len, width).astype(f32)
-    incoming = swap_in(cotangent).reshape(full_len, width).astype(f32)
+    incoming = incoming.reshape(full_len, width).astype(f32)
     first = lax.axis_index("seq") * per_seq
-    weight = lax.all_gather(tok_weight, "seq", axis=1, tiled=True)
-    weight = lax.dynamic_slice_in_dim(weight, first, per_seq, 0).reshape(full_len, 1)
     count = lax.dynamic_slice_in_dim(mask_count, first, per_seq, 0)
     positions = jnp.arange(full_len, dtype=jnp.int32)
     masked = (positions < count[0]).astype(f32)[:, None]
-    incoming = incoming * (weight.astype(f32) * (1.0 + masked) * 0.25)
+    incoming = incoming * (weight.reshape(full_len, 1).astype(f32) * (1.0 + masked) * 0.25)
 
     per_layer = block_total // layer_count
     weights = [
@@ -1038,7 +1101,7 @@
             hidden, weights[number], unpack(vectors[number], width), scale
         )
         saved.append(kept)
-    layer_out = swap_out(hidden.astype(bf16).reshape(per_seq, full_len, width))
+    last = hidden.astype(bf16).reshape(per_seq, full_len, width)
 
     chunk = owned_count + 1
     rows = owner_list + owner_list // owned_count
@@ -1064,8 +1127,10 @@
     slots = slots.reshape((data_parts, chunk) + vec_slot.shape)
     vec_slots = jnp.broadcast_to(vec_slot, (data_parts, 1) + vec_slot.shape)
     slots = lax.dynamic_update_slice(slots, vec_slots, (0, owned_count, 0, 0))
-    owned = reduce_blocks(slots.reshape(slot_shape))
-    input_grad = swap_out(incoming.reshape(per_seq, full_len, width))
+    owned, layer_out, input_grad = reduce_blocks(
+        slots.reshape(slot_shape), last, incoming.astype(bf16).reshape(per_seq, full_len, width)
+    )
+    input_grad = input_grad.astype(f32)
 
     vec_rows = owned[owned_count].astype(f32)
     half = PACK // 2

time: 616 us -> 611 us (level)
  Pallas kernels: 458 us -> 501 us
  blocking collectives: 24.8 us -> 0 us
  starting transfers between devices: 18.7 us -> 0 us
    pallas_call x1, Pallas kernels: 90.9 us -> 117 us  [gather_slots(): pl.pallas_call(functools.partial(gather_kernel, alone, steps, rows, lag,...]
    all_gather x1 -> x0, blocking collectives: 24.8 us -> none  [local(): weight = lax.all_gather(tok_weight, 'seq', axis=1, tiled=True)]
    all_to_all x4 -> x0, starting transfers between devices: 18.7 us -> none  [the longest x2 10.7 us: swap_in(): return lax.all_to_all(array, 'seq', split_axis=0, concat_axis=1, tiled=True)]
    pallas_call x1, Pallas kernels: 153 us -> 167 us  [reduce_slots(): pl.pallas_call(functools.partial(reduce_kernel, steps, rows, layers, lag)...]
  transfers between devices with their start and end apart: 4 -> 0, of which waited for: 0 -> 0; matrix products, arithmetic and copies ran while one was open for 2% -> 0% of each run, Pallas kernels for 68% -> 0%
where the time goes in v3:
time: 611 us; the launch traced here: 599 us
  Pallas kernels  501 us (82%)
  matrix products  63.6 us (10%)
  other arithmetic  18.1 us (3%)
  local copies, waits for them, and re-layouts  14.7 us (2%)
    pallas_call x1, Pallas kernels, reduce_slots(): pl.pallas_call(functools.partial(reduce_kernel, steps, rows, layers, lag)...  167 us
    pallas_call x1, Pallas kernels, gather_slots(): pl.pallas_call(functools.partial(gather_kernel, alone, steps, rows, lag,...  117 us
    pallas_call x8, Pallas kernels, weight_grad(): pl.pallas_call(functools.partial(weight_grad_kernel, lanes_of, block_of,...  68.4 us
    dot_general x16, matrix products, dot(): lax.dot_general(left, right, (((left_dim,), (right_dim,)), ((), ())), pre...  63.6 us
    pallas_call x8, Pallas kernels, assemble(): pl.pallas_call(functools.partial(assemble_kernel, cells), grid_spec=pltpu...  52.8 us
    pallas_call x1, Pallas kernels, soap(): pl.pallas_call(soap_kernel, grid=(groups,), in_specs=[view_spec] * 5 + [p...  37.6 us
    pallas_call x2, Pallas kernels, attend_back(): pl.pallas_call(functools.partial(attend_back_kernel, scale), grid=(pairs,...  29.9 us
    pallas_call x2, Pallas kernels, attend(): pl.pallas_call(functools.partial(attend_kernel, scale), grid=(pairs,), in...  20.1 us

profile of v3, /device:TPU:0, one launch (start us, length us, event | category | flops | bytes accessed | tf_op | source)
XLA Modules:
  0.0 599.3 jit_solution(13944914706637605237)
XLA Ops:
  0.6 1.2 dynamic_slice.3
  2.0 1.3 fusion.20.rows_ref
  3.2 1.4 fusion.23
  4.6 1.6 slice_reduce_fusion.4
  6.4 0.6 add.253
  7.0 0.6 add.230
  7.6 8.2 %pack.1 = bf16[48,288,128]{2,1,0:T(8,128)(2,1)} custom-call(f32[6,2304,128]{2,1,0:T(8,128)} %bitcast.193), custom_call_target="tpu_custom_call" | custom-call | tf_op jit(solution)/shard_map/pack/pallas_call | solution.py:115
  15.8 117.2 %gather_slots.1 = (bf16[2,2,2,13824,128]{4,3,2,1,0:T(8,128)(2,1)}, bf16[4,128,768]{2,1,0:T(8,128)(2,1)}, bf16[4,128,768]{2,1,0:T(8,128)(2,1)}, s32[4,1,128]{2,1,0:T(1,128)}) custom-call(bf16[13824,128]{1,0:T(8,128)(2,1)} %bitcast.195, bf16[4,128,768]{2,1,0:T(8,128)(2,1)} %token_ref.1, bf16[4,128,768]{2,1,0:T(8,128)(2,1)} %cot_ref.1, s32[4,1,128]{2,1,0:T(1,128)} %bitcast.224), custom_call_target="tpu_custom_call" | custom-call | bytes 300000000 | tf_op jit(solution)/shard_map/gather_slots/pallas_call | solution.py:900
  132.9 0.6 convert_element_type.143
  133.6 0.6 copy-done.40
  134.7 2.1 fusion.15
  137.4 3.3 assemble.13
  140.7 3.3 assemble.9
  143.9 5.9 assemble.12
  149.8 6.0 %assemble.8 = bf16[768,2304]{1,0:T(8,128)(2,1)} custom-call(s32[384]{0:T(512)} %owner_ref.15, bf16[384,288,128]{2,1,0:T(8,128)(2,1)} %bitcast.154, bf16[384,288,128]{2,1,0:T(8,128)(2,1)} %bitcast.148, bf16[384,288,128]{2,1,0:T(8,128)(2,1)} %bitcast.149, bf16[384,288,128]{2,1,0:T(8,128)(2,1)} %bitcast.150, bf16[384,288,128]{2,1,0:T(8,128)(2,1)} %bitcast.151, ...), custom_call_target="tpu_custom_call" | custom-call | tf_op jit(solution)/shard_map/assemble/pallas_call | solution.py:157
  155.9 5.4 fusion.12.qkv_ref
  161.3 10.1 %attend.2 = (bf16[512,768]{1,0:T(8,128)(2,1)}, f32[512,768]{1,0:T(8,128)}) custom-call(bf16[512,2304]{1,0:T(8,128)(2,1)} %fusion.12.qkv_ref), custom_call_target="tpu_custom_call" | custom-call | tf_op jit(solution)/shard_map/attend/pallas_call | solution.py:243
  171.3 2.0 fusion.24
  173.7 0.8 copy-done.2
  174.5 0.6 copy-done.38
  175.1 1.2 fusion.16.left_ref
  176.3 8.6 %assemble.15 = bf16[3072,768]{1,0:T(8,128)(2,1)} custom-call(s32[384]{0:T(512)} %owner_ref.15, bf16[384,288,128]{2,1,0:T(8,128)(2,1)} %bitcast.159, bf16[384,288,128]{2,1,0:T(8,128)(2,1)} %bitcast.160, bf16[384,288,128]{2,1,0:T(8,128)(2,1)} %bitcast.161, bf16[384,288,128]{2,1,0:T(8,128)(2,1)} %bitcast.162, bf16[384,288,128]{2,1,0:T(8,128)(2,1)} %bitcast.163, ...), custom_call_target="tpu_custom_call" | custom-call | tf_op jit(solution)/shard_map/assemble/pallas_call | solution.py:157
  184.9 8.5 %assemble.14 = bf16[768,3072]{1,0:T(8,128)(2,1)} custom-call(s32[384]{0:T(512)} %owner_ref.15, bf16[384,288,128]{2,1,0:T(8,128)(2,1)} %bitcast.169, bf16[384,288,128]{2,1,0:T(8,128)(2,1)} %bitcast.168, bf16[384,288,128]{2,1,0:T(8,128)(2,1)} %bitcast.167, bf16[384,288,128]{2,1,0:T(8,128)(2,1)} %bitcast.170, bf16[384,288,128]{2,1,0:T(8,128)(2,1)} %bitcast.171, ...), custom_call_target="tpu_custom_call" | custom-call | tf_op jit(solution)/shard_map/assemble/pallas_call | solution.py:157
  193.4 8.5 %assemble.11 = bf16[3072,768]{1,0:T(8,128)(2,1)} custom-call(s32[384]{0:T(512)} %owner_ref.15, bf16[384,288,128]{2,1,0:T(8,128)(2,1)} %bitcast.175, bf16[384,288,128]{2,1,0:T(8,128)(2,1)} %bitcast.176, bf16[384,288,128]{2,1,0:T(8,128)(2,1)} %bitcast.177, bf16[384,288,128]{2,1,0:T(8,128)(2,1)} %bitcast.178, bf16[384,288,128]{2,1,0:T(8,128)(2,1)} %bitcast.179, ...), custom_call_target="tpu_custom_call" | custom-call | tf_op jit(solution)/shard_map/assemble/pallas_call | solution.py:157
  201.9 8.7 %assemble.10 = bf16[768,3072]{1,0:T(8,128)(2,1)} custom-call(s32[384]{0:T(512)} %owner_ref.15, bf16[384,288,128]{2,1,0:T(8,128)(2,1)} %bitcast.183, bf16[384,288,128]{2,1,0:T(8,128)(2,1)} %bitcast.184, bf16[384,288,128]{2,1,0:T(8,128)(2,1)} %bitcast.185, bf16[384,288,128]{2,1,0:T(8,128)(2,1)} %bitcast.186, bf16[384,288,128]{2,1,0:T(8,128)(2,1)} %bitcast.187, ...), custom_call_target="tpu_custom_call" | custom-call | tf_op jit(solution)/shard_map/assemble/pallas_call | solution.py:157
  210.7 6.9 %multiply_convert_fusion.1 = (bf16[512,3072]{1,0:T(8,128)(2,1)S(1)}, f32[512,3072]{1,0:T(8,128)}) fusion(f32[3072]{0:T(1024)S(1)} %bitcast.220, bf16[512,768]{1,0:T(8,128)(2,1)S(1)} %copy-done.8, bf16[768,3072]{1,0:T(8,128)(2,1)} %assemble.10), kind=kOutput, calls=%fused_computation.18 | convolution fusion | flops 2425356288 | bytes 14954496 | tf_op jit(solution)/shard_map/dot_general | solution.py:212
  217.7 2.8 fusion.25
  221.5 0.9 copy-done.9
  222.7 3.4 fusion.13.qkv_ref
  226.1 10.0 %attend.3 = (bf16[512,768]{1,0:T(8,128)(2,1)}, f32[512,768]{1,0:T(8,128)}) custom-call(bf16[512,2304]{1,0:T(8,128)(2,1)} %fusion.13.qkv_ref), custom_call_target="tpu_custom_call" | custom-call | tf_op jit(solution)/shard_map/attend/pallas_call | solution.py:243
  236.1 2.5 fusion.26
  239.7 5.9 multiply_convert_fusion
  245.6 2.8 fusion.27
  249.7 1.7 multiply_reduce_fusion
  251.5 0.7 convert_reduce_fusion.4
  252.2 4.8 convert_reduce_fusion
  257.1 3.1 multiply_reduce_fusion.1
  260.2 1.7 convert_reduce_fusion.5
  261.9 0.9 copy-done.11
  262.8 1.7 convolution_convert_fusion.1.grad_ref
  264.5 14.9 %attend_back.2.right_ref = bf16[512,2304]{1,0:T(8,128)(2,1)} custom-call(bf16[512,2304]{1,0:T(8,128)(2,1)} %fusion.13.qkv_ref, f32[512,768]{1,0:T(8,128)} %get-tuple-element.31.lse_ref, bf16[512,768]{1,0:T(8,128)(2,1)} %convolution_convert_fusion.1.grad_ref), custom_call_target="tpu_custom_call" | custom-call | tf_op jit(solution)/shard_map/attend_back/pallas_call | solution.py:285
  279.4 5.6 multiply_reduce_fusion.2
  285.6 7.1 %convert_reduce_fusion.1 = (f32[3072]{0:T(1024)S(1)}, bf16[512,3072]{1,0:T(8,128)(2,1)S(1)}) fusion(bf16[512,768]{1,0:T(8,128)(2,1)S(1)} %get-tuple-element.81.right_ref, bf16[3072,768]{1,0:T(8,128)(2,1)S(1)} %copy-done.5, f32[512,3072]{1,0:T(8,128)} %get-tuple-element.100, f32[3072]{0:T(1024)S(1)} %bitcast.221), kind=kOutput, calls=%fused_computation.15 | convolution fusion | flops 2436363264 | bytes 14966784 | tf_op jit(solution)/shard_map/dot_general | solution.py:212
  292.8 3.1 multiply_reduce_fusion.3
  296.5 0.7 copy-done.20
  297.2 1.7 convolution_convert_fusion.grad_ref
  298.9 15.0 %attend_back.3.right_ref = bf16[512,2304]{1,0:T(8,128)(2,1)} custom-call(bf16[512,2304]{1,0:T(8,128)(2,1)} %fusion.12.qkv_ref, f32[512,768]{1,0:T(8,128)} %get-tuple-element.26.lse_ref, bf16[512,768]{1,0:T(8,128)(2,1)} %convolution_convert_fusion.grad_ref), custom_call_target="tpu_custom_call" | custom-call | tf_op jit(solution)/shard_map/attend_back/pallas_call | solution.py:285
  313.9 4.7 add_convert_fusion
  319.5 0.8 copy-done
  321.1 10.2 %weight_grad.8.refs_0_ = bf16[392,288,128]{2,1,0:T(8,128)(2,1)} custom-call(s32[384]{0:T(512)} %fusion.20.rows_ref, bf16[512,3072]{1,0:T(8,128)(2,1)} %copy-done.17, bf16[512,768]{1,0:T(8,128)(2,1)} %copy-done.18), custom_call_target="tpu_custom_call" | custom-call | tf_op jit(solution)/shard_map/weight_grad/pallas_call | solution.py:367
  331.3 10.9 %weight_grad.9.refs_0_ = bf16[392,288,128]{2,1,0:T(8,128)(2,1)} custom-call(s32[384]{0:T(512)} %fusion.20.rows_ref, bf16[512,768]{1,0:T(8,128)(2,1)} %copy-done.10, bf16[512,3072]{1,0:T(8,128)(2,1)} %copy-done.15, bf16[392,288,128]{2,1,0:T(8,128)(2,1)} %weight_grad.8.refs_0_), custom_call_target="tpu_custom_call", output_to_operand_aliasing={{}: (3, {})} | custom-call | tf_op jit(solution)/shard_map/weight_grad/pallas_call | solution.py:367
  342.2 4.3 weight_grad.10.refs_0_
  346.6 8.6 %weight_grad.11.refs_0_ = bf16[392,288,128]{2,1,0:T(8,128)(2,1)} custom-call(s32[384]{0:T(512)} %fusion.20.rows_ref, bf16[512,768]{1,0:T(8,128)(2,1)} %copy-done.9, bf16[512,2304]{1,0:T(8,128)(2,1)} %attend_back.2.right_ref, bf16[392,288,128]{2,1,0:T(8,128)(2,1)} %weight_grad.10.refs_0_), custom_call_target="tpu_custom_call", output_to_operand_aliasing={{}: (3, {})} | custom-call | tf_op jit(solution)/shard_map/weight_grad/pallas_call | solution.py:367
  355.1 10.2 %weight_grad.12.refs_0_ = bf16[392,288,128]{2,1,0:T(8,128)(2,1)} custom-call(s32[384]{0:T(512)} %fusion.20.rows_ref, bf16[512,3072]{1,0:T(8,128)(2,1)} %copy-done.14, bf16[512,768]{1,0:T(8,128)(2,1)} %copy-done.12, bf16[392,288,128]{2,1,0:T(8,128)(2,1)} %weight_grad.11.refs_0_), custom_call_target="tpu_custom_call", output_to_operand_aliasing={{}: (3, {})} | custom-call | tf_op jit(solution)/shard_map/weight_grad/pallas_call | solution.py:367
  365.4 11.2 %weight_grad.13.refs_0_ = bf16[392,288,128]{2,1,0:T(8,128)(2,1)} custom-call(s32[384]{0:T(512)} %fusion.20.rows_ref, bf16[512,768]{1,0:T(8,128)(2,1)} %fusion.16.left_ref, bf16[512,3072]{1,0:T(8,128)(2,1)} %copy-done.16, bf16[392,288,128]{2,1,0:T(8,128)(2,1)} %weight_grad.12.refs_0_), custom_call_target="tpu_custom_call", output_to_operand_aliasing={{}: (3, {})} | custom-call | tf_op jit(solution)/shard_map/weight_grad/pallas_call | solution.py:367
  376.6 4.3 weight_grad.14.refs_0_
  380.9 8.6 %weight_grad.15 = bf16[392,288,128]{2,1,0:T(8,128)(2,1)} custom-call(s32[384]{0:T(512)} %fusion.20.rows_ref, bf16[512,768]{1,0:T(8,128)(2,1)} %bitcast.208, bf16[512,2304]{1,0:T(8,128)(2,1)} %attend_back.3.right_ref, bf16[392,288,128]{2,1,0:T(8,128)(2,1)} %weight_grad.14.refs_0_), custom_call_target="tpu_custom_call", output_to_operand_aliasing={{}: (3, {})} | custom-call | tf_op jit(solution)/shard_map/weight_grad/pallas_call | solution.py:367
  389.6 0.9 broadcast_dynamic-update-slice_fusion
  390.5 166.6 %reduce_slots.1 = (bf16[14112,128]{1,0:T(8,128)(2,1)}, bf16[4,128,768]{2,1,0:T(8,128)(2,1)}, bf16[4,128,768]{2,1,0:T(8,128)(2,1)}) custom-call(bf16[2,2,2,14112,128]{4,3,2,1,0:T(8,128)(2,1)} %bitcast.192, bf16[4,128,768]{2,1,0:T(8,128)(2,1)} %bitcast.207, bf16[4,128,768]{2,1,0:T(8,128)(2,1)} %bitcast.211), custom_call_target="tpu_custom_call" | custom-call | bytes 300000000 | tf_op jit(solution)/shard_map/reduce_slots/pallas_call | solution.py:730
  557.1 1.0 slice_convert_fusion
  558.2 0.9 divide_subtract_fusion
  559.1 1.3 convert_element_type.170
  560.4 37.6 %soap.1 = (f32[6,2304,128]{2,1,0:T(8,128)}, f32[6,2304,128]{2,1,0:T(8,128)}, f32[6,2304,128]{2,1,0:T(8,128)}, bf16[6,2304,128]{2,1,0:T(8,128)(2,1)}) custom-call(f32[6,2304,128]{2,1,0:T(8,128)} %bitcast.194, f32[6,2304,128]{2,1,0:T(8,128)} %bitcast.196, f32[6,2304,128]{2,1,0:T(8,128)} %bitcast.197, f32[6,2304,128]{2,1,0:T(8,128)} %bitcast.198, ...), custom_call_target="tpu_custom_call" | custom-call | tf_op jit(solution)/shard_map/soap/pallas_call | solution.py:470
  598.0 0.9 copy.58
  (183 shorter events, 7.8 us)
Async XLA Ops:
  6.3 128.5 %copy-start.28 = (f32[768]{0:T(1024)}, f32[768]{0:T(1024)S(1)}, u32[]{:S(2)}) copy-start(f32[768]{0:T(1024)S(1)} %get-tuple-element.56) | copy-start | bytes 9220
  133.6 0.6 copy-start.40
  149.8 6.0 %copy-start.22 = (bf16[4,128,768]{2,1,0:T(8,128)(2,1)S(1)}, bf16[4,128,768]{2,1,0:T(8,128)(2,1)}, u32[]{:S(2)}) copy-start(bf16[4,128,768]{2,1,0:T(8,128)(2,1)} %get-tuple-element.24) | copy-start | bytes 2359300
  149.8 6.0 %copy-start.49 = (f32[2304]{0:T(1024)S(1)}, f32[2304]{0:T(1024)}, u32[]{:S(2)}) copy-start(f32[2304]{0:T(1024)} %add.230) | copy-start | bytes 27652
  161.3 10.1 %copy-start.19 = (bf16[768,768]{1,0:T(8,128)(2,1)S(1)}, bf16[768,768]{1,0:T(8,128)(2,1)}, u32[]{:S(2)}) copy-start(bf16[768,768]{1,0:T(8,128)(2,1)} %assemble.9) | copy-start | bytes 3538948
  161.3 10.1 %copy-start.56 = (f32[768]{0:T(1024)S(1)}, f32[768]{0:T(1024)}, u32[]{:S(2)}) copy-start(f32[768]{0:T(1024)} %get-tuple-element.68) | copy-start | bytes 9220
  173.4 1.2 copy-start.2
  173.4 1.7 copy-start.32
  173.4 1.7 copy-start.45
  173.4 1.1 copy-start.36
  174.5 0.6 copy-start.38
  201.9 8.7 %copy-start.8 = (bf16[512,768]{1,0:T(8,128)(2,1)S(1)}, bf16[512,768]{1,0:T(8,128)(2,1)}, u32[]{:S(2)}) copy-start(bf16[512,768]{1,0:T(8,128)(2,1)} %fusion.16.left_ref) | copy-start | bytes 2359300
  201.9 8.7 %copy-start.50 = (f32[1,3072]{1,0:T(1,128)S(1)}, f32[1,3072]{1,0:T(1,128)}, u32[]{:S(2)}) copy-start(f32[1,3072]{1,0:T(1,128)} %get-tuple-element.94) | copy-start | bytes 36868
  210.7 7.0 %copy-start.3 = (f32[512,768]{1,0:T(8,128)S(1)}, f32[512,768]{1,0:T(8,128)}, u32[]{:S(2)}) copy-start(f32[512,768]{1,0:T(8,128)} %copy-done.2) | copy-start | bytes 4718596
  210.7 7.0 %copy-start.5 = (bf16[3072,768]{1,0:T(8,128)(2,1)S(1)}, bf16[3072,768]{1,0:T(8,128)(2,1)}, u32[]{:S(2)}) copy-start(bf16[3072,768]{1,0:T(8,128)(2,1)} %assemble.11) | copy-start | bytes 14155780
  210.7 7.0 %copy-start.33 = (f32[768]{0:T(1024)S(1)}, f32[768]{0:T(1024)}, u32[]{:S(2)}) copy-start(f32[768]{0:T(1024)} %get-tuple-element.67) | copy-start | bytes 9220
  210.7 7.0 %copy-start.37 = (f32[512]{0:T(512)S(1)}, f32[512]{0:T(512)}, u32[]{:S(2)}) copy-start(f32[512]{0:T(512)} %copy-done.36) | copy-start | bytes 6148
  210.7 7.0 %copy-start.39 = (f32[512]{0:T(512)S(1)}, f32[512]{0:T(512)}, u32[]{:S(2)}) copy-start(f32[512]{0:T(512)} %copy-done.38) | copy-start | bytes 6148
  210.7 7.0 %copy-start.46 = (f32[768]{0:T(1024)S(1)}, f32[768]{0:T(1024)}, u32[]{:S(2)}) copy-start(f32[768]{0:T(1024)} %get-tuple-element.66) | copy-start | bytes 9220
  210.7 7.0 %copy-start.55 = (f32[768]{0:T(1024)S(1)}, f32[768]{0:T(1024)}, u32[]{:S(2)}) copy-start(f32[768]{0:T(1024)} %get-tuple-element.65) | copy-start | bytes 9220
  217.6 2.8 copy-start.14
  220.5 0.7 copy-start.34
  220.5 0.7 copy-start.44
  220.5 2.2 copy-start.7
  220.8 1.9 copy-start.48
  221.5 0.9 copy-start.9
  226.1 10.0 %copy-start.54 = (f32[768]{0:T(1024)S(1)}, f32[768]{0:T(1024)}, u32[]{:S(2)}) copy-start(f32[768]{0:T(1024)} %get-tuple-element.60) | copy-start | bytes 9220
  236.1 3.5 copy-start.51
  238.6 0.7 copy-start.35
  238.6 0.7 copy-start.43
  238.6 6.9 %slice-start.4 = ((s8[4718592]{0:T(1024)(128)(4,1)}), s8[4194304]{0:T(1024)(128)(4,1)S(1)}, s32[]{:S(2)}) async-start(s8[4718592]{0:T(1024)(128)(4,1)} %bitcast.204), calls=%async_computation.4 | async-start | bytes 8388608
  239.6 5.9 copy-start.10
  239.6 6.0 slice-start.5
  239.6 6.0 copy-start.53
  245.6 2.9 copy-start.17
  248.5 0.7 copy-start.41
  248.5 1.2 copy-start.4
  248.5 1.2 copy-start.29
  248.5 1.2 copy-start.42
  249.7 1.7 copy-start.52
  251.5 5.5 slice-start.2
  252.1 4.9 copy-start.18
  252.2 4.9 slice-start.3
  257.0 3.2 copy-start.15
  260.2 2.6 copy-start.21
  261.9 0.9 copy-start.11
  285.0 7.8 %slice-start = ((s8[4718592]{0:T(1024)(128)(4,1)}), s8[4194304]{0:T(1024)(128)(4,1)S(1)}, s32[]{:S(2)}) async-start(s8[4718592]{0:T(1024)(128)(4,1)} %bitcast.200), calls=%async_computation | async-start | bytes 8388608
  285.6 7.2 %copy-start.12 = (bf16[512,768]{1,0:T(8,128)(2,1)}, bf16[512,768]{1,0:T(8,128)(2,1)S(1)}, u32[]{:S(2)}) copy-start(bf16[512,768]{1,0:T(8,128)(2,1)S(1)} %get-tuple-element.81.right_ref) | copy-start | bytes 2359300
  285.6 7.2 %slice-start.1 = ((s8[4718592]{0:T(1024)(128)(4,1)}), s8[524288]{0:T(1024)(128)(4,1)S(1)}, s32[]{:S(2)}) async-start(s8[4718592]{0:T(1024)(128)(4,1)} %bitcast.200), calls=%async_computation.1 | async-start | bytes 1048576
  292.8 3.2 copy-start.16
  296.0 1.3 copy-start.20
  296.5 2.4 copy-start.13
  298.9 15.0 %copy-start.6 = (bf16[768,2304]{1,0:T(8,128)(2,1)S(1)}, bf16[768,2304]{1,0:T(8,128)(2,1)}, u32[]{:S(2)}) copy-start(bf16[768,2304]{1,0:T(8,128)(2,1)} %assemble.8) | copy-start | bytes 10616836
  313.9 4.7 copy-start.1
  318.6 0.8 copy-start.31
  318.6 1.7 copy-start
  319.1 1.7 copy-start.30
  319.1 1.8 copy-start.47
  390.5 167.7 %copy-start.25 = (f32[2,9216]{1,0:T(2,128)S(1)}, f32[2,9216]{1,0:T(2,128)}, u32[]{:S(2)}) copy-start(f32[2,9216]{1,0:T(2,128)} %param.23) | copy-start | bytes 221188
  390.5 167.7 %copy-start.26 = (f32[2,9216]{1,0:T(2,128)S(1)}, f32[2,9216]{1,0:T(2,128)}, u32[]{:S(2)}) copy-start(f32[2,9216]{1,0:T(2,128)} %param.24) | copy-start | bytes 221188
  390.5 167.7 %copy-start.27 = (f32[2,9216]{1,0:T(2,128)S(1)}, f32[2,9216]{1,0:T(2,128)}, u32[]{:S(2)}) copy-start(f32[2,9216]{1,0:T(2,128)} %param.25) | copy-start | bytes 221188
  557.1 2.0 copy-start.24
  560.4 37.6 %copy-start.23 = (bf16[4,128,768]{2,1,0:T(8,128)(2,1)S(1)}, bf16[4,128,768]{2,1,0:T(8,128)(2,1)}, u32[]{:S(2)}) copy-start(bf16[4,128,768]{2,1,0:T(8,128)(2,1)} %get-tuple-element.127) | copy-start | bytes 2359300

commit v4 on v3

--- a/solution.py
+++ b/solution.py
@@ -16,10 +16,12 @@
 GROUP = 8
 GATHER_ROWS = 144
 GATHER_LAG = 2
-ALONE_SHARE = 0.28
-SPREAD = 3
+ALONE_SHARE = 0.23
+SPREAD = 2
+LOADS = 8
+STORES = 4
 REDUCE_ROWS = 144
-REDUCE_LAG = 2
+REDUCE_LAG = 3
 WAIT_BYTES = 3 * 10**8
 
 norm_eps = 1e-05
@@ -129,85 +131,121 @@
     return block[0:BLK, :], jnp.concatenate([fold[:, :HDIM], fold[:, HDIM:]], axis=0)
 
 
-def assemble_kernel(cells, owner_ref, *refs):
-    out_ref = refs[-1]
+def assemble_kernel(plan, panels, owner_ref, gathered_ref, *refs):
+    outs, (blocks, stage, in_sems, out_sems) = refs[:-4], refs[-4:]
+    groups = 2 * BLK // LANE * 2
+
+    def load(panel, which):
+        spot = lax.rem(panel, LOADS)
+        return pltpu.make_async_copy(
+            gathered_ref.at[owner_ref[4 * panel + which]],
+            blocks.at[spot, which],
+            in_sems.at[spot, which],
+        )
+
+    def store(panel, out_ref, row, lanes_of, group):
+        spot = lax.rem(panel, STORES)
+        return pltpu.make_async_copy(
+            stage.at[spot, group],
+            out_ref.at[pl.ds(row, BLK), pl.ds(lanes_of(group), LANE)],
+            out_sems.at[spot, group],
+        )
+
+    def freed(panel):
+        for group in range(groups):
+            store(panel, outs[0], 0, lambda group: group * LANE, group).wait()
+
+    @pl.loop(0, LOADS - 1)
+    def _(panel):
+        for which in range(4):
+            load(panel, which).start()
+
     low = low_lanes(HALF)
-    for number, (row, lanes) in enumerate(cells):
-        left, right = refs[2 * number], refs[2 * number + 1]
-        fold_a = left[0, BLK:PACK, :].astype(f32)
-        fold_b = right[0, BLK:PACK, :].astype(f32)
-        tails = [(fold_a, swap(fold_b)), (swap(fold_a), fold_b)]
-        out_ref[pl.ds(row, BLK), pl.ds(lanes[0], LANE)] = left[0, 0:BLK, :]
-        for half, (tail_a, tail_b) in enumerate(tails):
-            main_b = swap(right[0, half * HALF : (half + 1) * HALF, :].astype(f32))
-            rows = pl.ds(row + half * HALF, HALF)
-            out_ref[rows, pl.ds(lanes[1], LANE)] = jnp.where(low, tail_a, main_b).astype(bf16)
-            out_ref[rows, pl.ds(lanes[2], LANE)] = jnp.where(low, main_b, tail_b).astype(bf16)
-
-
-def assemble(gathered, owner_list, shape, tile, cells, block_of):
-    grid = (shape[0] // tile[0], shape[1] // tile[1])
-    count = 2 * len(cells)
-
-    def spec(which):
-        return pl.BlockSpec(
-            (1, PACK, LANE), lambda i, j, owner: (owner[block_of(i, j, which)], 0, 0)
-        )
-
-    return pl.pallas_call(
-        functools.partial(assemble_kernel, cells),
+
+    def work(panel, out_ref, row, lanes_of):
+        @pl.when(panel + LOADS - 1 < panels)
+        def _():
+            for which in range(4):
+                load(panel + LOADS - 1, which).start()
+
+        for which in range(4):
+            load(panel, which).wait()
+
+        @pl.when(panel >= STORES)
+        def _():
+            freed(panel)
+
+        spot, target = lax.rem(panel, LOADS), lax.rem(panel, STORES)
+        for pair in range(2):
+            fold_a = blocks[spot, 2 * pair, BLK:PACK, :].astype(f32)
+            fold_b = blocks[spot, 2 * pair + 1, BLK:PACK, :].astype(f32)
+            tails = [(fold_a, swap(fold_b)), (swap(fold_a), fold_b)]
+            stage[target, 3 * pair] = blocks[spot, 2 * pair, 0:BLK, :]
+            for half, (tail_a, tail_b) in enumerate(tails):
+                rows = pl.ds(half * HALF, HALF)
+                main_b = swap(blocks[spot, 2 * pair + 1, rows, :].astype(f32))
+                stage[target, 3 * pair + 1, rows] = jnp.where(low, tail_a, main_b).astype(bf16)
+                stage[target, 3 * pair + 2, rows] = jnp.where(low, main_b, tail_b).astype(bf16)
+        for group in range(groups):
+            store(panel, out_ref, row, lanes_of, group).start()
+
+    for start, count, number, kind in plan:
+        out_ref = outs[number]
+
+        @pl.loop(0, count)
+        def _(step):
+            if kind is None:
+                across = out_ref.shape[1] // (4 * BLK)
+                row, col = lax.div(step, across), lax.rem(step, across)
+                first, stride = col * 4 * BLK, LANE
+            else:
+                row, first, stride = step, kind * LANE, 3 * LANE
+            work(
+                start + step,
+                out_ref,
+                pl.multiple_of(row * BLK, BLK),
+                lambda group: pl.multiple_of(first + group * stride, LANE),
+            )
+
+    for panel in range(max(panels - STORES, 0), panels):
+        freed(panel)
+
+
+def all_weights(gathered, owner_list, layers, width, inner):
+    side = width // BLK
+    plan, shapes, start = [], [], 0
+    for layer in range(layers):
+        number = len(shapes)
+        shapes += [(width, 3 * width), (width, width), (width, inner), (inner, width)]
+        parts = [(number, kind, side) for kind in range(3)] + [
+            (number + 1, None, side),
+            (number + 2, None, side * (inner // width)),
+            (number + 3, None, inner // BLK),
+        ]
+        for out, kind, count in parts:
+            plan.append((start, count, out, kind))
+            start += count
+    anywhere = pl.BlockSpec(memory_space=pl.ANY)
+    groups = 4 * BLK // LANE
+    outs = pl.pallas_call(
+        functools.partial(assemble_kernel, plan, start),
         grid_spec=pltpu.PrefetchScalarGridSpec(
             num_scalar_prefetch=1,
-            grid=grid,
-            in_specs=[spec(which) for which in range(count)],
-            out_specs=pl.BlockSpec(tile, lambda i, j, owner: (i, j)),
+            grid=(1,),
+            in_specs=[anywhere],
+            out_specs=[anywhere] * len(shapes),
+            scratch_shapes=[
+                pltpu.VMEM((LOADS, 4, PACK, LANE), bf16),
+                pltpu.VMEM((STORES, groups, BLK, LANE), bf16),
+                pltpu.SemaphoreType.DMA((LOADS, 4)),
+                pltpu.SemaphoreType.DMA((STORES, groups)),
+            ],
         ),
-        out_shape=jax.ShapeDtypeStruct(shape, bf16),
+        out_shape=[jax.ShapeDtypeStruct(shape, bf16) for shape in shapes],
         compiler_params=params(),
         name="assemble",
-    )(owner_list, *([gathered] * count))
-
-
-def layer_weights(gathered, owner_list, base, width, inner):
-    cols = width // BLK
-    inner_cols = inner // BLK
-    square = cols * cols
-    cells = []
-    for matrix in range(3):
-        for pair in range(cols // 2):
-            cells.append((0, [3 * LANE * (3 * pair + part) + LANE * matrix for part in range(3)]))
-    per_matrix = cols
-
-    def block_qkv(i, j, which):
-        return base + (which // per_matrix) * square + i * cols + which % per_matrix
-
-    w_qkv = assemble(gathered, owner_list, (width, 3 * width), (BLK, 3 * width), cells, block_qkv)
-    plain = []
-    for row in range(2):
-        for pair in range(cols // 2):
-            plain.append(
-                (row * BLK, [2 * BLK * pair + LANE * part for part in range(3)])
-            )
-
-    def block_plain(start, row_blocks):
-        def block(i, j, which):
-            return start + (2 * i + which // cols) * row_blocks + cols * j + which % cols
-
-        return block
-
-    tile = (2 * BLK, width)
-    w_out = assemble(
-        gathered, owner_list, (width, width), tile, plain, block_plain(base + 3 * square, cols)
-    )
-    up_base = base + 4 * square
-    w_up = assemble(
-        gathered, owner_list, (width, inner), tile, plain, block_plain(up_base, inner_cols)
-    )
-    down_base = up_base + cols * inner_cols
-    w_down = assemble(
-        gathered, owner_list, (inner, width), tile, plain, block_plain(down_base, cols)
-    )
-    return w_qkv, w_out, w_up, w_down
+    )(owner_list, gathered)
+    return [outs[4 * layer : 4 * layer + 4] for layer in range(layers)]
 def dot(left, right, left_dim=1, right_dim=0):
     return lax.dot_general(
         left, right, (((left_dim,), (right_dim,)), ((), ())), preferred_element_type=f32
@@ -599,8 +637,6 @@
     moves = exchange(
         level, layers, [(last_ref, last_out), (grad_ref, grad_out)], keep_sem, swap_send, swap_recv
     )
-    for move in moves:
-        move.start()
 
     @pl.loop(0, steps)
     def _(step):
@@ -615,6 +651,12 @@
         up_step = two_step - lag * level
         down_step = two_step - lag * (layers - 1 - level)
         last_step = two_step - lag * (layers - 1)
+
+        for turn, move in enumerate(moves):
+
+            @pl.when(tick == lag + turn * steps // len(moves))
+            def _():
+                move.start()
 
         @pl.when(inside(tick))
         def _():
@@ -820,10 +862,10 @@
     pairs = [(weight_ref, weight_out), (token_ref, token_out), (cot_ref, cot_out)]
     moves = exchange(level, layers, pairs, keep_sem, swap_send, swap_recv)
     own_copy().start()
-    for move in moves:
+    for move in moves[:layers]:
         move.start()
 
-    @pl.loop(0, max(turns + 2 * lag, SPREAD * alone + 4 * lag))
+    @pl.loop(0, max(turns + 2 * lag, SPREAD * alone + 6 * lag))
     def _(tick):
         @pl.when(tick < turns)
         def _():
@@ -860,7 +902,12 @@
             for half in range(2):
                 far_copy(half, after).start()
 
-        late = tick - 4 * lag
+        @pl.when(tick == alone + 2 * lag)
+        def _():
+            for move in moves[layers:]:
+                move.start()
+
+        late = tick - 6 * lag
         given = lax.div(jnp.maximum(late, 0), SPREAD)
 
         @pl.when(jnp.logical_and(given < alone, late == SPREAD * given))
@@ -1091,10 +1138,7 @@
     incoming = incoming * (weight.reshape(full_len, 1).astype(f32) * (1.0 + masked) * 0.25)
 
     per_layer = block_total // layer_count
-    weights = [
-        layer_weights(gathered, owner_list, per_layer * number, width, inner)
-        for number in range(layer_count)
-    ]
+    weights = all_weights(gathered, owner_list, layer_count, width, inner)
     saved = []
     for number in range(layer_count):
         hidden, kept = forward_layer(

time: 611 us -> 541 us (0.89)
  Pallas kernels: 501 us -> 444 us
    pallas_call x8 -> x1, Pallas kernels: 52.8 us -> 22.6 us  [all_weights(): pl.pallas_call(functools.partial(assemble_kernel, plan, start), grid_spec...]
    pallas_call x1, Pallas kernels: 167 us -> 152 us  [reduce_slots(): pl.pallas_call(functools.partial(reduce_kernel, steps, rows, layers, lag)...]
    pallas_call x1, Pallas kernels: 117 us -> 105 us  [gather_slots(): pl.pallas_call(functools.partial(gather_kernel, alone, steps, rows, lag,...]
where the time goes in v4:
time: 541 us; the launch traced here: 532 us
  Pallas kernels  444 us (82%)
  matrix products  63.8 us (12%)
  other arithmetic  13.4 us (2%)
  local copies, waits for them, and re-layouts  9.27 us (2%)
    pallas_call x1, Pallas kernels, reduce_slots(): pl.pallas_call(functools.partial(reduce_kernel, steps, rows, layers, lag)...  152 us
    pallas_call x1, Pallas kernels, gather_slots(): pl.pallas_call(functools.partial(gather_kernel, alone, steps, rows, lag,...  105 us
    pallas_call x8, Pallas kernels, weight_grad(): pl.pallas_call(functools.partial(weight_grad_kernel, lanes_of, block_of,...  68.2 us
    dot_general x16, matrix products, dot(): lax.dot_general(left, right, (((left_dim,), (right_dim,)), ((), ())), pre...  63.8 us
    pallas_call x1, Pallas kernels, soap(): pl.pallas_call(soap_kernel, grid=(groups,), in_specs=[view_spec] * 5 + [p...  37.6 us
    pallas_call x2, Pallas kernels, attend_back(): pl.pallas_call(functools.partial(attend_back_kernel, scale), grid=(pairs,...  29.9 us
    pallas_call x1, Pallas kernels, all_weights(): pl.pallas_call(functools.partial(assemble_kernel, plan, start), grid_spec...  22.6 us
    pallas_call x2, Pallas kernels, attend(): pl.pallas_call(functools.partial(attend_kernel, scale), grid=(pairs,), in...  20.2 us

profile of v4, /device:TPU:0, one launch (start us, length us, event | category | flops | bytes accessed | tf_op | source)
XLA Modules:
  0.0 532.2 jit_solution(5998521850883351757)
XLA Ops:
  0.6 1.2 dynamic_slice.3
  2.0 1.3 fusion.20.rows_ref
  3.2 0.8 fusion.23
  4.1 1.0 slice_reduce_fusion.4
  5.1 0.1 pad_maximum_fusion.3
  5.2 8.2 %pack.1 = bf16[48,288,128]{2,1,0:T(8,128)(2,1)} custom-call(f32[6,2304,128]{2,1,0:T(8,128)} %bitcast.122), custom_call_target="tpu_custom_call" | custom-call | tf_op jit(solution)/shard_map/pack/pallas_call | solution.py:117
  13.4 104.8 %gather_slots.1 = (bf16[2,2,2,13824,128]{4,3,2,1,0:T(8,128)(2,1)}, bf16[4,128,768]{2,1,0:T(8,128)(2,1)}, bf16[4,128,768]{2,1,0:T(8,128)(2,1)}, s32[4,1,128]{2,1,0:T(1,128)}) custom-call(bf16[13824,128]{1,0:T(8,128)(2,1)} %bitcast.124, bf16[4,128,768]{2,1,0:T(8,128)(2,1)} %token_ref.1, bf16[4,128,768]{2,1,0:T(8,128)(2,1)} %cot_ref.1, s32[4,1,128]{2,1,0:T(1,128)} %bitcast.147), custom_call_target="tpu_custom_call" | custom-call | bytes 300000000 | tf_op jit(solution)/shard_map/gather_slots/pallas_call | solution.py:947
  118.3 22.6 %assemble.1 = (bf16[768,2304]{1,0:T(8,128)(2,1)}, bf16[768,768]{1,0:T(8,128)(2,1)}, bf16[768,3072]{1,0:T(8,128)(2,1)}, bf16[3072,768]{1,0:T(8,128)(2,1)}, bf16[7...) custom-call(s32[384]{0:T(512)} %owner_ref.1, ...), custom_call_target="tpu_custom_call" | custom-call | tf_op jit(solution)/shard_map/assemble/pallas_call | solution.py:230
  140.9 0.7 multiply_multiply_fusion.3
  141.6 0.4 fusion.15
  142.1 5.4 %fusion.12.qkv_ref = bf16[512,2304]{1,0:T(8,128)(2,1)} fusion(bf16[512,768]{1,0:T(8,128)(2,1)S(1)} %bitcast.132, bf16[768,2304]{1,0:T(8,128)(2,1)} %get-tuple-element.34, f32[2304]{0:T(1024)S(1)} %add.230), kind=kOutput, calls=%fused_computation.24 | convolution fusion | flops 1814298624 | bytes 6693888 | tf_op jit(solution)/shard_map/dot_general | solution.py:250
  147.5 10.1 %attend.2 = (bf16[512,768]{1,0:T(8,128)(2,1)}, f32[512,768]{1,0:T(8,128)}) custom-call(bf16[512,2304]{1,0:T(8,128)(2,1)} %fusion.12.qkv_ref), custom_call_target="tpu_custom_call" | custom-call | tf_op jit(solution)/shard_map/attend/pallas_call | solution.py:281
  157.6 2.0 fusion.24
  159.6 0.3 multiply_reduce_fusion.12
  159.9 0.3 fusion.16.left_ref
  160.2 7.2 %multiply_convert_fusion.1 = (bf16[512,3072]{1,0:T(8,128)(2,1)S(1)}, f32[512,3072]{1,0:T(8,128)}) fusion(f32[3072]{0:T(1024)S(1)} %bitcast.143, bf16[512,768]{1,0:T(8,128)(2,1)S(1)} %fusion.16.left_ref, bf16[768,3072]{1,0:T(8,128)(2,1)} %get-tuple-element.38), kind=kOutput, calls=%fused_computation.18 | convolution fusion | flops 2425356288 | bytes 14954496 | tf_op jit(solution)/shard_map/dot_general | solution.py:250
  167.5 2.8 fusion.25
  170.3 0.3 multiply_reduce_fusion.11
  170.6 0.3 fusion.17.left_ref
  171.0 1.4 copy-done.22
  172.3 3.4 fusion.13.qkv_ref
  175.7 10.1 %attend.3 = (bf16[512,768]{1,0:T(8,128)(2,1)}, f32[512,768]{1,0:T(8,128)}) custom-call(bf16[512,2304]{1,0:T(8,128)(2,1)} %fusion.13.qkv_ref), custom_call_target="tpu_custom_call" | custom-call | tf_op jit(solution)/shard_map/attend/pallas_call | solution.py:281
  185.8 2.1 fusion.26
  187.9 0.3 multiply_reduce_fusion.10
  188.2 0.3 fusion.18.left_ref
  188.6 5.8 %multiply_convert_fusion = (bf16[512,3072]{1,0:T(8,128)(2,1)S(1)}, f32[512,3072]{1,0:T(8,128)S(1)}) fusion(f32[3072]{0:T(1024)S(1)} %bitcast.145, bf16[512,768]{1,0:T(8,128)(2,1)S(1)} %fusion.18.left_ref, bf16[768,3072]{1,0:T(8,128)(2,1)} %get-tuple-element.43), kind=kOutput, calls=%fused_computation.16 | convolution fusion | flops 2425356288 | bytes 14954496 | tf_op jit(solution)/shard_map/dot_general | solution.py:250
  194.4 2.9 fusion.27
  197.3 0.3 multiply_reduce_fusion.9
  197.6 0.7 multiply_multiply_fusion.4
  198.3 1.7 multiply_reduce_fusion
  199.9 0.6 convert_reduce_fusion.4
  200.6 4.8 convert_reduce_fusion
  205.5 3.1 multiply_reduce_fusion.1
  208.7 0.5 convert_reduce_fusion.5
  209.2 0.7 copy-done.26
  209.9 1.7 convolution_convert_fusion.1.grad_ref
  211.7 14.9 %attend_back.2.right_ref = bf16[512,2304]{1,0:T(8,128)(2,1)} custom-call(bf16[512,2304]{1,0:T(8,128)(2,1)} %fusion.13.qkv_ref, f32[512,768]{1,0:T(8,128)} %get-tuple-element.47.lse_ref, bf16[512,768]{1,0:T(8,128)(2,1)} %convolution_convert_fusion.1.grad_ref), custom_call_target="tpu_custom_call" | custom-call | tf_op jit(solution)/shard_map/attend_back/pallas_call | solution.py:323
  226.6 5.2 multiply_reduce_fusion.2
  231.8 0.5 convert_reduce_fusion.6
  232.3 7.9 %convert_reduce_fusion.1 = (f32[3072]{0:T(1024)S(1)}, bf16[512,3072]{1,0:T(8,128)(2,1)S(1)}) fusion(bf16[512,768]{1,0:T(8,128)(2,1)S(1)} %get-tuple-element.97.right_ref, bf16[3072,768]{1,0:T(8,128)(2,1)} %get-tuple-element.39, f32[512,3072]{1,0:T(8,128)} %get-tuple-element.116, f32[3072]{0:T(1024)S(1)} %bitcast.144), kind=kOutput, calls=%fused_computation.15 | convolution fusion | flops 2436363264 | bytes 14966784 | tf_op jit(solution)/shard_map/dot_general | solution.py:250
  240.3 3.1 multiply_reduce_fusion.3
  243.4 0.5 convert_reduce_fusion.7
  244.0 0.7 copy-done.24
  244.7 1.7 convolution_convert_fusion.grad_ref
  246.4 15.0 %attend_back.3.right_ref = bf16[512,2304]{1,0:T(8,128)(2,1)} custom-call(bf16[512,2304]{1,0:T(8,128)(2,1)} %fusion.12.qkv_ref, f32[512,768]{1,0:T(8,128)} %get-tuple-element.35.lse_ref, bf16[512,768]{1,0:T(8,128)(2,1)} %convolution_convert_fusion.grad_ref), custom_call_target="tpu_custom_call" | custom-call | tf_op jit(solution)/shard_map/attend_back/pallas_call | solution.py:323
  261.4 4.7 add_convert_fusion
  266.1 0.4 convert_reduce_fusion.3
  266.7 1.1 copy-done
  267.7 0.4 convert_reduce_fusion.2
  268.5 10.2 %weight_grad.8.refs_0_ = bf16[392,288,128]{2,1,0:T(8,128)(2,1)} custom-call(s32[384]{0:T(512)} %fusion.20.rows_ref, bf16[512,3072]{1,0:T(8,128)(2,1)} %copy-done.12, bf16[512,768]{1,0:T(8,128)(2,1)} %copy-done.13), custom_call_target="tpu_custom_call" | custom-call | tf_op jit(solution)/shard_map/weight_grad/pallas_call | solution.py:405
  278.7 10.9 %weight_grad.9.refs_0_ = bf16[392,288,128]{2,1,0:T(8,128)(2,1)} custom-call(s32[384]{0:T(512)} %fusion.20.rows_ref, bf16[512,768]{1,0:T(8,128)(2,1)} %copy-done.5, bf16[512,3072]{1,0:T(8,128)(2,1)} %copy-done.10, bf16[392,288,128]{2,1,0:T(8,128)(2,1)} %weight_grad.8.refs_0_), custom_call_target="tpu_custom_call", output_to_operand_aliasing={{}: (3, {})} | custom-call | tf_op jit(solution)/shard_map/weight_grad/pallas_call | solution.py:405
  289.6 4.3 weight_grad.10.refs_0_
  293.9 8.6 %weight_grad.11.refs_0_ = bf16[392,288,128]{2,1,0:T(8,128)(2,1)} custom-call(s32[384]{0:T(512)} %fusion.20.rows_ref, bf16[512,768]{1,0:T(8,128)(2,1)} %copy-done.4, bf16[512,2304]{1,0:T(8,128)(2,1)} %attend_back.2.right_ref, bf16[392,288,128]{2,1,0:T(8,128)(2,1)} %weight_grad.10.refs_0_), custom_call_target="tpu_custom_call", output_to_operand_aliasing={{}: (3, {})} | custom-call | tf_op jit(solution)/shard_map/weight_grad/pallas_call | solution.py:405
  302.5 10.2 %weight_grad.12.refs_0_ = bf16[392,288,128]{2,1,0:T(8,128)(2,1)} custom-call(s32[384]{0:T(512)} %fusion.20.rows_ref, bf16[512,3072]{1,0:T(8,128)(2,1)} %copy-done.9, bf16[512,768]{1,0:T(8,128)(2,1)} %copy-done.7, bf16[392,288,128]{2,1,0:T(8,128)(2,1)} %weight_grad.11.refs_0_), custom_call_target="tpu_custom_call", output_to_operand_aliasing={{}: (3, {})} | custom-call | tf_op jit(solution)/shard_map/weight_grad/pallas_call | solution.py:405
  312.7 11.2 %weight_grad.13.refs_0_ = bf16[392,288,128]{2,1,0:T(8,128)(2,1)} custom-call(s32[384]{0:T(512)} %fusion.20.rows_ref, bf16[512,768]{1,0:T(8,128)(2,1)} %copy-done.3, bf16[512,3072]{1,0:T(8,128)(2,1)} %copy-done.11, bf16[392,288,128]{2,1,0:T(8,128)(2,1)} %weight_grad.12.refs_0_), custom_call_target="tpu_custom_call", output_to_operand_aliasing={{}: (3, {})} | custom-call | tf_op jit(solution)/shard_map/weight_grad/pallas_call | solution.py:405
  323.9 4.4 weight_grad.14.refs_0_
  328.2 8.6 %weight_grad.15 = bf16[392,288,128]{2,1,0:T(8,128)(2,1)} custom-call(s32[384]{0:T(512)} %fusion.20.rows_ref, bf16[512,768]{1,0:T(8,128)(2,1)} %bitcast.131, bf16[512,2304]{1,0:T(8,128)(2,1)} %attend_back.3.right_ref, bf16[392,288,128]{2,1,0:T(8,128)(2,1)} %weight_grad.14.refs_0_), custom_call_target="tpu_custom_call", output_to_operand_aliasing={{}: (3, {})} | custom-call | tf_op jit(solution)/shard_map/weight_grad/pallas_call | solution.py:405
  336.8 0.9 broadcast_dynamic-update-slice_fusion
  337.8 152.2 %reduce_slots.1 = (bf16[14112,128]{1,0:T(8,128)(2,1)}, bf16[4,128,768]{2,1,0:T(8,128)(2,1)}, bf16[4,128,768]{2,1,0:T(8,128)(2,1)}) custom-call(bf16[2,2,2,14112,128]{4,3,2,1,0:T(8,128)(2,1)} %bitcast.120, bf16[4,128,768]{2,1,0:T(8,128)(2,1)} %bitcast.130, bf16[4,128,768]{2,1,0:T(8,128)(2,1)} %bitcast.134), custom_call_target="tpu_custom_call" | custom-call | bytes 300000000 | tf_op jit(solution)/shard_map/reduce_slots/pallas_call | solution.py:772
  490.0 1.0 slice_convert_fusion
  491.0 0.9 divide_subtract_fusion
  491.9 1.3 convert_element_type.170
  493.2 37.6 %soap.1 = (f32[6,2304,128]{2,1,0:T(8,128)}, f32[6,2304,128]{2,1,0:T(8,128)}, f32[6,2304,128]{2,1,0:T(8,128)}, bf16[6,2304,128]{2,1,0:T(8,128)(2,1)}) custom-call(f32[6,2304,128]{2,1,0:T(8,128)} %bitcast.123, f32[6,2304,128]{2,1,0:T(8,128)} %bitcast.125, f32[6,2304,128]{2,1,0:T(8,128)} %bitcast.126, f32[6,2304,128]{2,1,0:T(8,128)} %bitcast.127, ...), custom_call_target="tpu_custom_call" | custom-call | tf_op jit(solution)/shard_map/soap/pallas_call | solution.py:508
  530.8 0.9 copy.58
  (121 shorter events, 0.7 us)
Async XLA Ops:
  118.3 22.6 %copy-start.20 = (s32[4,1,128]{2,1,0:T(1,128)S(1)}, s32[4,1,128]{2,1,0:T(1,128)}, u32[]{:S(2)}) copy-start(s32[4,1,128]{2,1,0:T(1,128)} %get-tuple-element.46) | copy-start | bytes 6148
  118.3 23.3 %copy-start.2 = (bf16[4,128,768]{2,1,0:T(8,128)(2,1)S(1)}, bf16[4,128,768]{2,1,0:T(8,128)(2,1)}, u32[]{:S(2)}) copy-start(bf16[4,128,768]{2,1,0:T(8,128)(2,1)} %get-tuple-element.45) | copy-start | bytes 2359300
  118.3 23.8 %copy-start.14 = (bf16[4,128,768]{2,1,0:T(8,128)(2,1)S(1)}, bf16[4,128,768]{2,1,0:T(8,128)(2,1)}, u32[]{:S(2)}) copy-start(bf16[4,128,768]{2,1,0:T(8,128)(2,1)} %get-tuple-element.32) | copy-start | bytes 2359300
  147.5 10.1 %copy-start.23 = (bf16[768,768]{1,0:T(8,128)(2,1)S(1)}, bf16[768,768]{1,0:T(8,128)(2,1)}, u32[]{:S(2)}) copy-start(bf16[768,768]{1,0:T(8,128)(2,1)} %get-tuple-element.37) | copy-start | bytes 3538948
  159.9 7.6 %slice-start.2 = ((s8[4718592]{0:T(1024)(128)(4,1)}), s8[4194304]{0:T(1024)(128)(4,1)S(1)}, s32[]{:S(2)}) async-start(s8[4718592]{0:T(1024)(128)(4,1)} %bitcast.153), calls=%async_computation.2 | async-start | bytes 8388608
  160.2 7.3 %copy-start.3 = (bf16[512,768]{1,0:T(8,128)(2,1)}, bf16[512,768]{1,0:T(8,128)(2,1)S(1)}, u32[]{:S(2)}) copy-start(bf16[512,768]{1,0:T(8,128)(2,1)S(1)} %fusion.16.left_ref) | copy-start | bytes 2359300
  160.2 7.3 %slice-start.3 = ((s8[4718592]{0:T(1024)(128)(4,1)}), s8[524288]{0:T(1024)(128)(4,1)S(1)}, s32[]{:S(2)}) async-start(s8[4718592]{0:T(1024)(128)(4,1)} %bitcast.153), calls=%async_computation.3 | async-start | bytes 1048576
  167.5 2.8 copy-start.9
  170.3 2.0 copy-start.22
  172.3 3.4 copy-start.4
  175.7 10.1 %copy-start.25 = (bf16[768,768]{1,0:T(8,128)(2,1)S(1)}, bf16[768,768]{1,0:T(8,128)(2,1)}, u32[]{:S(2)}) copy-start(bf16[768,768]{1,0:T(8,128)(2,1)} %get-tuple-element.42) | copy-start | bytes 3538948
  188.2 6.1 %slice-start.6 = ((s8[4718592]{0:T(1024)(128)(4,1)}), s8[4194304]{0:T(1024)(128)(4,1)S(1)}, s32[]{:S(2)}) async-start(s8[4718592]{0:T(1024)(128)(4,1)} %bitcast.157), calls=%async_computation.6 | async-start | bytes 8388608
  188.6 5.8 %copy-start.5 = (bf16[512,768]{1,0:T(8,128)(2,1)}, bf16[512,768]{1,0:T(8,128)(2,1)S(1)}, u32[]{:S(2)}) copy-start(bf16[512,768]{1,0:T(8,128)(2,1)S(1)} %fusion.18.left_ref) | copy-start | bytes 2359300
  188.6 5.8 %slice-start.7 = ((s8[4718592]{0:T(1024)(128)(4,1)}), s8[524288]{0:T(1024)(128)(4,1)S(1)}, s32[]{:S(2)}) async-start(s8[4718592]{0:T(1024)(128)(4,1)} %bitcast.157), calls=%async_computation.7 | async-start | bytes 1048576
  194.4 2.9 copy-start.12
  199.9 5.5 %slice-start.4 = ((s8[4718592]{0:T(1024)(128)(4,1)}), s8[4194304]{0:T(1024)(128)(4,1)S(1)}, s32[]{:S(2)}) async-start(s8[4718592]{0:T(1024)(128)(4,1)} %bitcast.155), calls=%async_computation.4 | async-start | bytes 8388608
  200.6 4.9 copy-start.13
  200.6 4.9 slice-start.5
  205.5 3.2 copy-start.10
  208.7 1.3 copy-start.26
  209.2 2.4 copy-start.6
  231.7 8.5 %slice-start = ((s8[4718592]{0:T(1024)(128)(4,1)}), s8[4194304]{0:T(1024)(128)(4,1)S(1)}, s32[]{:S(2)}) async-start(s8[4718592]{0:T(1024)(128)(4,1)} %bitcast.151), calls=%async_computation | async-start | bytes 8388608
  232.3 7.9 %copy-start.7 = (bf16[512,768]{1,0:T(8,128)(2,1)}, bf16[512,768]{1,0:T(8,128)(2,1)S(1)}, u32[]{:S(2)}) copy-start(bf16[512,768]{1,0:T(8,128)(2,1)S(1)} %get-tuple-element.97.right_ref) | copy-start | bytes 2359300
  232.3 8.0 %slice-start.1 = ((s8[4718592]{0:T(1024)(128)(4,1)}), s8[524288]{0:T(1024)(128)(4,1)S(1)}, s32[]{:S(2)}) async-start(s8[4718592]{0:T(1024)(128)(4,1)} %bitcast.151), calls=%async_computation.1 | async-start | bytes 1048576
  240.3 3.1 copy-start.11
  243.4 1.3 copy-start.24
  244.0 2.4 copy-start.8
  246.4 15.0 %copy-start.21 = (bf16[768,2304]{1,0:T(8,128)(2,1)S(1)}, bf16[768,2304]{1,0:T(8,128)(2,1)}, u32[]{:S(2)}) copy-start(bf16[768,2304]{1,0:T(8,128)(2,1)} %get-tuple-element.34) | copy-start | bytes 10616836
  261.4 4.7 copy-start.1
  266.1 1.7 copy-start
  337.8 153.3 %copy-start.17 = (f32[2,9216]{1,0:T(2,128)S(1)}, f32[2,9216]{1,0:T(2,128)}, u32[]{:S(2)}) copy-start(f32[2,9216]{1,0:T(2,128)} %param.23) | copy-start | bytes 221188
  337.8 153.3 %copy-start.18 = (f32[2,9216]{1,0:T(2,128)S(1)}, f32[2,9216]{1,0:T(2,128)}, u32[]{:S(2)}) copy-start(f32[2,9216]{1,0:T(2,128)} %param.24) | copy-start | bytes 221188
  337.8 153.3 %copy-start.19 = (f32[2,9216]{1,0:T(2,128)S(1)}, f32[2,9216]{1,0:T(2,128)}, u32[]{:S(2)}) copy-start(f32[2,9216]{1,0:T(2,128)} %param.25) | copy-start | bytes 221188
  490.0 2.0 copy-start.16
  493.2 37.6 %copy-start.15 = (bf16[4,128,768]{2,1,0:T(8,128)(2,1)S(1)}, bf16[4,128,768]{2,1,0:T(8,128)(2,1)}, u32[]{:S(2)}) copy-start(bf16[4,128,768]{2,1,0:T(8,128)(2,1)} %get-tuple-element.143) | copy-start | bytes 2359300

commit v5 on v4

--- a/solution.py
+++ b/solution.py
@@ -20,6 +20,7 @@
 SPREAD = 2
 LOADS = 8
 STORES = 4
+RING = 6
 REDUCE_ROWS = 144
 REDUCE_LAG = 3
 WAIT_BYTES = 3 * 10**8
@@ -73,12 +74,12 @@
 
 
 def triple(ref, row):
-    return [ref[0, pl.ds(row + GROUP * part, HALF, stride=3 * GROUP), :] for part in range(3)]
+    return [ref[pl.ds(row + GROUP * part, HALF, stride=3 * GROUP), :] for part in range(3)]
 
 
 def put_triple(ref, row, pieces):
     for part, piece in enumerate(pieces):
-        ref[0, pl.ds(row + GROUP * part, HALF, stride=3 * GROUP), :] = piece
+        ref[pl.ds(row + GROUP * part, HALF, stride=3 * GROUP), :] = piece
 
 
 def to_square(pieces, main_ref, tail_ref):
@@ -105,7 +106,7 @@
     for row in range(GROUP):
         spot = row % 2
         main, tail = main_ref.at[spot], tail_ref.at[spot]
-        to_square(triple(src_ref, row), main, tail)
+        to_square(triple(src_ref.at[0], row), main, tail)
         out_ref[row, 0:BLK, :] = main[...].astype(bf16)
         out_ref[row, BLK:PACK, :] = jnp.where(
             low, tail[0:HALF, :], swap(tail[HALF:BLK, :])
@@ -455,63 +456,69 @@
     )
 
 
+def square_of(refs):
+    return jnp.concatenate([refs[0][...], refs[1][:, :HDIM]], axis=1).astype(bf16)
+
+
+def keep(refs, value):
+    refs[0][...] = value[:, :LANE]
+    refs[1][:, :HDIM] = value[:, LANE:]
+
+
+def update_block(row, grad, sources, targets, squares):
+    masters_ref, one_ref, two_ref, left_ref, right_ref = sources
+    one_out, two_out, masters_out = targets
+    left_refs, right_refs, refs = [[pair.at[0], pair.at[1]] for pair in squares]
+    to_square(triple(left_ref, row), *left_refs)
+    to_square(triple(right_ref, row), *right_refs)
+    left, right = square_of(left_refs), square_of(right_refs)
+    main, tail = unfold(grad)
+    grad = jnp.concatenate([main, tail], axis=1)
+    keep(refs, dot(dot(left, grad, 0, 0).astype(bf16), right))
+    pieces = from_square(*refs)
+    ones, twos = triple(one_ref, row), triple(two_ref, row)
+    ones = [beta_one * old + (1.0 - beta_one) * new for old, new in zip(ones, pieces)]
+    twos = [beta_two * old + (1.0 - beta_two) * new * new for old, new in zip(twos, pieces)]
+    put_triple(one_out, row, ones)
+    put_triple(two_out, row, twos)
+    moves = [
+        (one / fix_one) / (jnp.sqrt(two / fix_two) + adam_eps) for one, two in zip(ones, twos)
+    ]
+    to_square(moves, *refs)
+    keep(refs, dot(dot(left, square_of(refs)).astype(bf16), right, 1, 1))
+    pieces = from_square(*refs)
+    old = triple(masters_ref, row)
+    new = [value - matrix_rate * (step + decay_rate * value) for value, step in zip(old, pieces)]
+    put_triple(masters_out, row, new)
+
+
 def soap_kernel(
     masters_ref, one_ref, two_ref, left_ref, right_ref, grad_ref,
-    one_out, two_out, masters_out, copies_out, left_sq, right_sq, work, full,
+    one_out, two_out, masters_out, copies_out, squares,
 ):
-    def square(refs):
-        return jnp.concatenate([refs[0][...], refs[1][:, :HDIM]], axis=1).astype(bf16)
-
-    def keep(refs, value):
-        refs[0][...] = value[:, :LANE]
-        refs[1][:, :HDIM] = value[:, LANE:]
-
-    for row in range(GROUP):
-        spot = row
-        left_refs = [left_sq.at[spot, 0], left_sq.at[spot, 1]]
-        right_refs = [right_sq.at[spot, 0], right_sq.at[spot, 1]]
-        refs = [work.at[spot, 0], work.at[spot, 1]]
-        to_square(triple(left_ref, row), *left_refs)
-        to_square(triple(right_ref, row), *right_refs)
-        left, right = square(left_refs), square(right_refs)
-        main, tail = unfold(grad_ref[row])
-        grad = jnp.concatenate([main, tail], axis=1)
-        rotated = dot(dot(left, grad, 0, 0).astype(bf16), right)
-        keep(refs, rotated)
-        pieces = from_square(*refs)
-        ones, twos = triple(one_ref, row), triple(two_ref, row)
-        ones = [beta_one * old + (1.0 - beta_one) * new for old, new in zip(ones, pieces)]
-        twos = [beta_two * old + (1.0 - beta_two) * new * new for old, new in zip(twos, pieces)]
-        put_triple(one_out, row, ones)
-        put_triple(two_out, row, twos)
-        moves = [
-            (one / fix_one) / (jnp.sqrt(two / fix_two) + adam_eps) for one, two in zip(ones, twos)
-        ]
-        to_square(moves, *refs)
-        restored = dot(dot(left, square(refs)).astype(bf16), right, 1, 1)
-        keep(refs, restored)
-        pieces = from_square(*refs)
-        old = triple(masters_ref, row)
-        new = [
-            value - matrix_rate * (step + decay_rate * value) for value, step in zip(old, pieces)
-        ]
-        put_triple(masters_out, row, new)
-        put_triple(full, row, new)
-    copies_out[0] = full[0].astype(bf16)
+    sources = [ref.at[0] for ref in (masters_ref, one_ref, two_ref, left_ref, right_ref)]
+    targets = [ref.at[0] for ref in (one_out, two_out, masters_out)]
+
+    @pl.loop(0, GROUP)
+    def _(row):
+        update_block(
+            row, grad_ref[row], sources, targets, [squares.at[which] for which in range(3)]
+        )
+
+    copies_out[...] = masters_out[...].astype(bf16)
 
 
 def soap(views, grads):
     groups = views[0].shape[0]
     view_spec = pl.BlockSpec((1, GROUP * PACK, LANE), lambda i: (i, 0, 0))
     shape = (groups, GROUP * PACK, LANE)
-    square = pltpu.VMEM((GROUP, 2, BLK, LANE), f32)
     return pl.pallas_call(
         soap_kernel,
         grid=(groups,),
         in_specs=[view_spec] * 5 + [pl.BlockSpec((GROUP, PACK, LANE), lambda i: (i, 0, 0))],
         out_specs=[view_spec] * 4,
         out_shape=[jax.ShapeDtypeStruct(shape, f32)] * 3 + [jax.ShapeDtypeStruct(shape, bf16)],
-        scratch_shapes=[square, square, square, pltpu.VMEM((1, GROUP * PACK, LANE), f32)],
+        scratch_shapes=[pltpu.VMEM((3, 2, BLK, LANE), f32)],
         compiler_params=params(),
         name="soap",
     )(*views, grads)
@@ -576,11 +583,16 @@
 
 
 def reduce_kernel(
-    steps, rows, layers, lag, slots_ref, last_ref, grad_ref, out_ref, last_out, grad_out,
-    own, inbox, first, second, up, down, down_sum, keep_sem, swap_send, swap_recv, own_sem, core_send, core_recv, one_send, one_recv, two_send, two_recv,
+    steps, layers, lag, slots_ref, last_ref, grad_ref,
+    masters_ref, one_ref, two_ref, left_ref, right_ref,
+    vec_out, last_out, grad_out, one_out, two_out, masters_out, copies_out,
+    ring, own, first, second, up, down, down_sum, grad_buf, loaded, made, copied, squares,
+    load_sem, store_sem, keep_sem, swap_send, swap_recv, own_sem, core_send, core_recv, one_send, one_recv, two_send, two_recv,
     up_send, up_recv, down_send, down_recv,
 ):
     size = (2, 2)
+    rows = PACK // 2
+    groups = one_out.shape[0]
     y, x, core = place(size)
     level = lax.axis_index("seq")
     other_core = device(y, x, 1 - core, size, level)
@@ -591,7 +603,7 @@
     firsts, seconds = [across_x, across_y], [across_y, across_x]
 
     def span(half, step):
-        return pl.ds(pl.multiple_of((half * steps + step) * rows, rows), rows)
+        return pl.ds(pl.multiple_of((2 * step + half) * rows, rows), rows)
 
     def remote(source, target, send, recv, half, step, where):
         return send_to(source, target, send.at[half, step], recv.at[half, step], where)
@@ -599,13 +611,13 @@
     def own_copy(half, step):
         part = span(half, step)
         return pltpu.make_async_copy(
-            slots_ref.at[:, :, core, part], own.at[:, :, part], own_sem.at[half, step]
+            slots_ref.at[:, :, core, part], ring.at[lax.rem(step, RING), half], own_sem.at[half, step]
         )
 
     def core_copy(half, step):
         part = span(half, step)
         return remote(
-            slots_ref.at[:, :, 1 - core, part], inbox.at[:, :, part],
+            slots_ref.at[:, :, 1 - core, part], own.at[:, :, part],
             core_send, core_recv, half, step, other_core,
         )
 
@@ -638,11 +650,65 @@
         level, layers, [(last_ref, last_out), (grad_ref, grad_out)], keep_sem, swap_send, swap_recv
     )
 
+    def load(group, which):
+        source = (masters_ref, one_ref, two_ref, left_ref, right_ref)[which]
+        spot = lax.rem(group, 2)
+        return pltpu.make_async_copy(
+            source.at[group], loaded.at[which, spot], load_sem.at[which, spot]
+        )
+
+    def store(group, which):
+        spot = lax.rem(group, 2)
+        source = copied.at[spot] if which == 3 else made.at[which, spot]
+        target = (one_out, two_out, masters_out, copies_out)[which]
+        return pltpu.make_async_copy(source, target.at[group], store_sem.at[which, spot])
+
+    def update(block):
+        group, row = lax.div(block, GROUP), lax.rem(block, GROUP)
+        spot = lax.rem(group, 2)
+
+        @pl.when(row == 0)
+        def _():
+            for which in range(5):
+                load(group, which).wait()
+
+            @pl.when(group >= 2)
+            def _():
+                for which in range(4):
+                    store(group - 2, which).wait()
+
+        update_block(
+            row,
+            grad_buf[...],
+            [loaded.at[which, spot] for which in range(5)],
+            [made.at[which, spot] for which in range(3)],
+            [squares.at[which] for which in range(3)],
+        )
+
+        @pl.when(row == GROUP - 1)
+        def _():
+            copied[spot] = made[2, spot].astype(bf16)
+            for which in range(4):
+                store(group, which).start()
+
+            @pl.when(group + 2 < groups)
+            def _():
+                for which in range(5):
+                    load(group + 2, which).start()
+
     @pl.loop(0, steps)
     def _(step):
         for half in range(2):
+            core_copy(half, step).start()
+
+    @pl.loop(0, RING - 1)
+    def _(step):
+        for half in range(2):
             own_copy(half, step).start()
-            core_copy(half, step).start()
+
+    for group in range(min(2, groups)):
+        for which in range(5):
+            load(group, which).start()
 
     @pl.loop(0, steps + lag * (layers + 1))
     def _(tick):
@@ -658,13 +724,18 @@
             def _():
                 move.start()
 
+        @pl.when(tick + RING - 1 < steps)
+        def _():
+            for half in range(2):
+                own_copy(half, tick + RING - 1).start()
+
         @pl.when(inside(tick))
         def _():
             for half in range(2):
                 part = span(half, tick)
                 own_copy(half, tick).wait()
                 core_copy(half, tick).wait_recv()
-                own[:, :, part] = own[:, :, part] + inbox[:, :, part]
+                own[:, :, part] = own[:, :, part] + ring[lax.rem(tick, RING), half]
 
         @pl.when(inside(one_step))
         def _():
@@ -716,13 +787,15 @@
             for half in range(2):
                 part = span(half, last_step)
 
+                half_rows = pl.ds(half * rows, rows)
+
                 @pl.when(level < layers - 1)
                 def _():
-                    out_ref[part] = up[part] + down[part]
+                    grad_buf[half_rows] = up[part] + down[part]
 
                 @pl.when(level == layers - 1)
                 def _():
-                    out_ref[part] = up[part]
+                    grad_buf[half_rows] = up[part]
 
         @pl.when(inside(tick))
         def _():
@@ -743,9 +816,20 @@
         def _():
             for half in range(2):
                 down_copy(half, down_step).start()
+
+        @pl.when(jnp.logical_and(last_step >= 0, last_step < steps - 1))
+        def _():
+            update(last_step)
+
+        @pl.when(last_step == steps - 1)
+        def _():
+            vec_out[...] = grad_buf[...]
 
     for move in moves:
         move.wait()
+    for group in range(max(groups - 2, 0), groups):
+        for which in range(4):
+            store(group, which).wait()
 
     @pl.loop(0, steps)
     def _(step):
@@ -763,36 +847,47 @@
                 down_copy(half, step).wait_send()
 
 
-def reduce_slots(slots, last, grad, layers, rows, lag):
+def reduce_slots(slots, last, grad, views, layers, lag):
     total = slots.shape[0] // 8 * PACK
-    steps = total // (2 * rows)
+    steps = total // PACK
     chunk = (total, LANE)
+    view = views[0].shape
     sems = pltpu.SemaphoreType.DMA((2, steps))
     anywhere = pl.BlockSpec(memory_space=pl.ANY)
-    out, last, grad = pl.pallas_call(
-        functools.partial(reduce_kernel, steps, rows, layers, lag),
-        in_specs=[anywhere] * 3,
-        out_specs=[pl.BlockSpec(memory_space=pltpu.VMEM), anywhere, anywhere],
+    vec_slot, last, grad, *updated = pl.pallas_call(
+        functools.partial(reduce_kernel, steps, layers, lag),
+        in_specs=[anywhere] * 8,
+        out_specs=[pl.BlockSpec(memory_space=pltpu.VMEM)] + [anywhere] * 6,
         out_shape=[
-            jax.ShapeDtypeStruct(chunk, bf16),
+            jax.ShapeDtypeStruct((PACK, LANE), bf16),
             jax.ShapeDtypeStruct(last.shape, last.dtype),
             jax.ShapeDtypeStruct(grad.shape, grad.dtype),
-        ],
+        ]
+        + [jax.ShapeDtypeStruct(view, f32)] * 3
+        + [jax.ShapeDtypeStruct(view, bf16)],
         scratch_shapes=[
-            pltpu.VMEM((2, 2) + chunk, bf16),
+            pltpu.VMEM((RING, 2, 2, 2, PACK // 2, LANE), bf16),
             pltpu.VMEM((2, 2) + chunk, bf16),
             pltpu.VMEM((2,) + chunk, bf16),
         ]
         + [pltpu.VMEM(chunk, bf16)] * 4
+        + [
+            pltpu.VMEM((PACK, LANE), bf16),
+            pltpu.VMEM((5, 2) + view[1:], f32),
+            pltpu.VMEM((3, 2) + view[1:], f32),
+            pltpu.VMEM((2,) + view[1:], bf16),
+            pltpu.VMEM((3, 2, BLK, LANE), f32),
+            pltpu.SemaphoreType.DMA((5, 2)),
+            pltpu.SemaphoreType.DMA((4, 2)),
+        ]
         + exchange_sems(2, layers)
         + [sems] * 11,
         compiler_params=pltpu.CompilerParams(
-            vmem_limit_bytes=62 * 2**20, collective_id=0, has_side_effects=True
+            vmem_limit_bytes=63 * 2**20, collective_id=0, has_side_effects=True
         ),
-        cost_estimate=pl.CostEstimate(flops=0, bytes_accessed=WAIT_BYTES, transcendentals=0),
         name="reduce_slots",
-    )(slots.reshape((2, 2, 2) + chunk), last, grad)
-    return out.reshape(total // PACK, PACK, LANE), last, grad
+    )(slots.reshape((2, 2, 2) + chunk), last, grad, *views)
+    return updated, vec_slot, last, grad
 
 
 def gather_kernel(
@@ -1088,16 +1183,19 @@
     return gathered, swap_in(tokens), swap_in(cotangent), swap_in(tok_weight)
 
 
-def reduce_blocks(slots, last, grad):
+def reduce_blocks(slots, last, grad, views, owned_count):
     layers = lax.axis_size("seq")
-    total = slots.shape[0] // lax.axis_size("dp") * PACK
-    if near_group(last.shape[0] * layers) and total % (2 * REDUCE_ROWS) == 0:
+    if near_group(last.shape[0] * layers) and owned_count % GROUP == 0:
         shape = (layers, last.shape[1] // layers, last.shape[2])
         return reduce_slots(
-            slots, last.reshape(shape), grad.reshape(shape), layers, REDUCE_ROWS, REDUCE_LAG
+            slots, last.reshape(shape), grad.reshape(shape), views, layers, REDUCE_LAG
         )
     owned = lax.psum(lax.psum_scatter(slots, "dp", scatter_dimension=0, tiled=True), "seq")
-    return owned, swap_out(last), swap_out(grad)
+    vec_slot = owned[owned_count]
+    extra = views[0].shape[0] * GROUP - owned.shape[0]
+    if extra > 0:
+        owned = jnp.pad(owned, ((0, extra), (0, 0), (0, 0)))
+    return soap(views, owned), vec_slot, swap_out(last), swap_out(grad)
 
 
 def local(
@@ -1171,23 +1269,22 @@
     slots = slots.reshape((data_parts, chunk) + vec_slot.shape)
     vec_slots = jnp.broadcast_to(vec_slot, (data_parts, 1) + vec_slot.shape)
     slots = lax.dynamic_update_slice(slots, vec_slots, (0, owned_count, 0, 0))
-    owned, layer_out, input_grad = reduce_blocks(
-        slots.reshape(slot_shape), last, incoming.astype(bf16).reshape(per_seq, full_len, width)
-    )
-    input_grad = input_grad.astype(f32)
-
-    vec_rows = owned[owned_count].astype(f32)
-    half = PACK // 2
-    vec_total = (vec_rows[:half] + vec_rows[half:]).reshape(vectors.shape)
     views = [master_view] + [
         row_view(array) for array in (moment_one, moment_two, left_basis, right_basis)
     ]
-    extra = views[0].shape[0] * GROUP - chunk
-    if extra > 0:
-        owned = jnp.pad(owned, ((0, extra), (0, 0), (0, 0)))
-    new_one, new_two, new_masters, copies = [
-        row_unview(array, owned_count) for array in soap(views, owned)
-    ]
+    updated, vec_slot, layer_out, input_grad = reduce_blocks(
+        slots.reshape(slot_shape),
+        last,
+        incoming.astype(bf16).reshape(per_seq, full_len, width),
+        views,
+        owned_count,
+    )
+    input_grad = input_grad.astype(f32)
+    new_one, new_two, new_masters, copies = [row_unview(array, owned_count) for array in updated]
+
+    vec_rows = vec_slot.astype(f32)
+    half = PACK // 2
+    vec_total = (vec_rows[:half] + vec_rows[half:]).reshape(vectors.shape)
     vec_one = beta_one * vec_moment_one + (1.0 - beta_one) * vec_total
     vec_two = beta_two * vec_moment_two + (1.0 - beta_two) * vec_total * vec_total
     new_vectors = vectors - vector_rate * (vec_one / fix_one) / (

time: 541 us -> 523 us (0.967)
  Pallas kernels: 444 us -> 409 us
  local copies, waits for them, and re-layouts: 9.27 us -> 26.1 us
    pallas_call x2 -> x1, Pallas kernels: 190 us -> 155 us  [reduce_slots(): pl.pallas_call(functools.partial(reduce_kernel, steps, layers, lag), in_s...]
    unnamed x87 -> x101, local copies, waits for them, and re-layouts: 4.96 us -> 21.8 us
where the time goes in v5:
time: 523 us; the launch traced here: 514 us
  Pallas kernels  409 us (78%)
  matrix products  63.8 us (12%)
  local copies, waits for them, and re-layouts  26.1 us (5%)
  other arithmetic  13.4 us (3%)
    pallas_call x1, Pallas kernels, reduce_slots(): pl.pallas_call(functools.partial(reduce_kernel, steps, layers, lag), in_s...  155 us
    pallas_call x1, Pallas kernels, gather_slots(): pl.pallas_call(functools.partial(gather_kernel, alone, steps, rows, lag,...  105 us
    pallas_call x8, Pallas kernels, weight_grad(): pl.pallas_call(functools.partial(weight_grad_kernel, lanes_of, block_of,...  68.2 us
    dot_general x16, matrix products, dot(): lax.dot_general(left, right, (((left_dim,), (right_dim,)), ((), ())), pre...  63.8 us
    pallas_call x2, Pallas kernels, attend_back(): pl.pallas_call(functools.partial(attend_back_kernel, scale), grid=(pairs,...  29.9 us
    pallas_call x1, Pallas kernels, all_weights(): pl.pallas_call(functools.partial(assemble_kernel, plan, start), grid_spec...  22.6 us
    unnamed x101, local copies, waits for them, and re-layouts  21.8 us
    pallas_call x2, Pallas kernels, attend(): pl.pallas_call(functools.partial(attend_kernel, scale), grid=(pairs,), in...  20.2 us

profile of v5, /device:TPU:0, one launch (start us, length us, event | category | flops | bytes accessed | tf_op | source)
XLA Modules:
  0.0 514.1 jit_solution(16414166634707305878)
XLA Ops:
  0.6 1.2 dynamic_slice.3
  2.0 1.3 fusion.20.rows_ref
  3.2 0.8 fusion.23
  4.1 1.0 slice_reduce_fusion.4
  5.2 8.2 %pack.1 = bf16[48,288,128]{2,1,0:T(8,128)(2,1)} custom-call(f32[6,2304,128]{2,1,0:T(8,128)} %bitcast.120), custom_call_target="tpu_custom_call" | custom-call | tf_op jit(solution)/shard_map/pack/pallas_call | solution.py:118
  13.4 104.8 %gather_slots.1 = (bf16[2,2,2,13824,128]{4,3,2,1,0:T(8,128)(2,1)}, bf16[4,128,768]{2,1,0:T(8,128)(2,1)}, bf16[4,128,768]{2,1,0:T(8,128)(2,1)}, s32[4,1,128]{2,1,0:T(1,128)}) custom-call(bf16[13824,128]{1,0:T(8,128)(2,1)} %bitcast.123, bf16[4,128,768]{2,1,0:T(8,128)(2,1)} %token_ref.1, bf16[4,128,768]{2,1,0:T(8,128)(2,1)} %cot_ref.1, s32[4,1,128]{2,1,0:T(1,128)} %bitcast.153), custom_call_target="tpu_custom_call" | custom-call | bytes 300000000 | tf_op jit(solution)/shard_map/gather_slots/pallas_call | solution.py:1042
  118.3 22.6 %assemble.1 = (bf16[768,2304]{1,0:T(8,128)(2,1)}, bf16[768,768]{1,0:T(8,128)(2,1)}, bf16[768,3072]{1,0:T(8,128)(2,1)}, bf16[3072,768]{1,0:T(8,128)(2,1)}, bf16[7...) custom-call(s32[384]{0:T(512)} %owner_ref.1, ...), custom_call_target="tpu_custom_call" | custom-call | tf_op jit(solution)/shard_map/assemble/pallas_call | solution.py:231
  140.9 0.7 multiply_multiply_fusion.3
  141.6 0.4 fusion.15
  142.1 5.4 %fusion.12.qkv_ref = bf16[512,2304]{1,0:T(8,128)(2,1)} fusion(bf16[512,768]{1,0:T(8,128)(2,1)S(1)} %bitcast.138, bf16[768,2304]{1,0:T(8,128)(2,1)} %get-tuple-element.34, f32[2304]{0:T(1024)S(1)} %add.230), kind=kOutput, calls=%fused_computation.24 | convolution fusion | flops 1814298624 | bytes 6693888 | tf_op jit(solution)/shard_map/dot_general | solution.py:251
  147.5 10.1 %attend.2 = (bf16[512,768]{1,0:T(8,128)(2,1)}, f32[512,768]{1,0:T(8,128)}) custom-call(bf16[512,2304]{1,0:T(8,128)(2,1)} %fusion.12.qkv_ref), custom_call_target="tpu_custom_call" | custom-call | tf_op jit(solution)/shard_map/attend/pallas_call | solution.py:282
  157.6 2.0 fusion.24
  159.9 0.3 fusion.16.left_ref
  160.2 7.2 %multiply_convert_fusion.1 = (bf16[512,3072]{1,0:T(8,128)(2,1)S(1)}, f32[512,3072]{1,0:T(8,128)}) fusion(f32[3072]{0:T(1024)S(1)} %bitcast.149, bf16[512,768]{1,0:T(8,128)(2,1)S(1)} %fusion.16.left_ref, bf16[768,3072]{1,0:T(8,128)(2,1)} %get-tuple-element.38), kind=kOutput, calls=%fused_computation.18 | convolution fusion | flops 2425356288 | bytes 14954496 | tf_op jit(solution)/shard_map/dot_general | solution.py:251
  167.5 2.8 fusion.25
  170.6 0.3 fusion.17.left_ref
  170.9 1.4 copy-done.23
  172.3 3.4 fusion.13.qkv_ref
  175.7 10.1 %attend.3 = (bf16[512,768]{1,0:T(8,128)(2,1)}, f32[512,768]{1,0:T(8,128)}) custom-call(bf16[512,2304]{1,0:T(8,128)(2,1)} %fusion.13.qkv_ref), custom_call_target="tpu_custom_call" | custom-call | tf_op jit(solution)/shard_map/attend/pallas_call | solution.py:282
  185.8 2.1 fusion.26
  188.2 0.3 fusion.18.left_ref
  188.6 5.8 %multiply_convert_fusion = (bf16[512,3072]{1,0:T(8,128)(2,1)S(1)}, f32[512,3072]{1,0:T(8,128)S(1)}) fusion(f32[3072]{0:T(1024)S(1)} %bitcast.151, bf16[512,768]{1,0:T(8,128)(2,1)S(1)} %fusion.18.left_ref, bf16[768,3072]{1,0:T(8,128)(2,1)} %get-tuple-element.43), kind=kOutput, calls=%fused_computation.16 | convolution fusion | flops 2425356288 | bytes 14954496 | tf_op jit(solution)/shard_map/dot_general | solution.py:251
  194.4 2.9 fusion.27
  197.6 0.7 multiply_multiply_fusion.4
  198.2 1.7 multiply_reduce_fusion
  200.0 0.6 convert_reduce_fusion.4
  200.7 4.8 convert_reduce_fusion
  205.5 3.1 multiply_reduce_fusion.1
  208.7 0.5 convert_reduce_fusion.5
  209.3 0.7 copy-done.27
  210.0 1.7 convolution_convert_fusion.1.grad_ref
  211.7 14.9 %attend_back.2.right_ref = bf16[512,2304]{1,0:T(8,128)(2,1)} custom-call(bf16[512,2304]{1,0:T(8,128)(2,1)} %fusion.13.qkv_ref, f32[512,768]{1,0:T(8,128)} %get-tuple-element.47.lse_ref, bf16[512,768]{1,0:T(8,128)(2,1)} %convolution_convert_fusion.1.grad_ref), custom_call_target="tpu_custom_call" | custom-call | tf_op jit(solution)/shard_map/attend_back/pallas_call | solution.py:324
  226.6 5.2 %multiply_reduce_fusion.2 = (f32[768]{0:T(1024)S(1)}, f32[512]{0:T(512)S(1)}, f32[512]{0:T(512)S(1)}, f32[768]{0:T(1024)S(1)}, f32[512,768]{1,0:T(8,128)S(1)}) fusion(f32[512,768]{1,0:T(8,128)S(1)} %get-tuple-element.118, f32[512]{0:T(512)S(1)} %add_rsqrt_fusion.2, f32[512]{0:T(512)S(1)} %broadcast_multiply_fusion.9, f32[768]{0:T(1024)S(1)} %get-tuple-element.80, ...), kind=kOutput, calls=%fused_computation.33 | convolution fusion | flops 1815868928 | bytes 10634240 | tf_op jit(solution)/shard_map/dot_general | solution.py:251
  231.8 0.5 convert_reduce_fusion.6
  232.4 7.9 %convert_reduce_fusion.1 = (f32[3072]{0:T(1024)S(1)}, bf16[512,3072]{1,0:T(8,128)(2,1)S(1)}) fusion(bf16[512,768]{1,0:T(8,128)(2,1)S(1)} %get-tuple-element.97.right_ref, bf16[3072,768]{1,0:T(8,128)(2,1)} %get-tuple-element.39, f32[512,3072]{1,0:T(8,128)} %get-tuple-element.116, f32[3072]{0:T(1024)S(1)} %bitcast.150), kind=kOutput, calls=%fused_computation.15 | convolution fusion | flops 2436363264 | bytes 14966784 | tf_op jit(solution)/shard_map/dot_general | solution.py:251
  240.3 3.1 multiply_reduce_fusion.3
  243.5 0.5 convert_reduce_fusion.7
  244.0 0.7 copy-done.25
  244.7 1.7 convolution_convert_fusion.grad_ref
  246.4 15.0 %attend_back.3.right_ref = bf16[512,2304]{1,0:T(8,128)(2,1)} custom-call(bf16[512,2304]{1,0:T(8,128)(2,1)} %fusion.12.qkv_ref, f32[512,768]{1,0:T(8,128)} %get-tuple-element.35.lse_ref, bf16[512,768]{1,0:T(8,128)(2,1)} %convolution_convert_fusion.grad_ref), custom_call_target="tpu_custom_call" | custom-call | tf_op jit(solution)/shard_map/attend_back/pallas_call | solution.py:324
  261.4 4.7 add_convert_fusion
  266.1 0.4 convert_reduce_fusion.3
  266.7 1.1 copy-done
  267.8 0.4 convert_reduce_fusion.2
  268.6 10.2 %weight_grad.8.refs_0_ = bf16[392,288,128]{2,1,0:T(8,128)(2,1)} custom-call(s32[384]{0:T(512)} %fusion.20.rows_ref, bf16[512,3072]{1,0:T(8,128)(2,1)} %copy-done.13, bf16[512,768]{1,0:T(8,128)(2,1)} %copy-done.14), custom_call_target="tpu_custom_call" | custom-call | tf_op jit(solution)/shard_map/weight_grad/pallas_call | solution.py:406
  278.8 10.9 %weight_grad.9.refs_0_ = bf16[392,288,128]{2,1,0:T(8,128)(2,1)} custom-call(s32[384]{0:T(512)} %fusion.20.rows_ref, bf16[512,768]{1,0:T(8,128)(2,1)} %copy-done.6, bf16[512,3072]{1,0:T(8,128)(2,1)} %copy-done.11, bf16[392,288,128]{2,1,0:T(8,128)(2,1)} %weight_grad.8.refs_0_), custom_call_target="tpu_custom_call", output_to_operand_aliasing={{}: (3, {})} | custom-call | tf_op jit(solution)/shard_map/weight_grad/pallas_call | solution.py:406
  289.7 4.3 weight_grad.10.refs_0_
  294.0 8.6 %weight_grad.11.refs_0_ = bf16[392,288,128]{2,1,0:T(8,128)(2,1)} custom-call(s32[384]{0:T(512)} %fusion.20.rows_ref, bf16[512,768]{1,0:T(8,128)(2,1)} %copy-done.5, bf16[512,2304]{1,0:T(8,128)(2,1)} %attend_back.2.right_ref, bf16[392,288,128]{2,1,0:T(8,128)(2,1)} %weight_grad.10.refs_0_), custom_call_target="tpu_custom_call", output_to_operand_aliasing={{}: (3, {})} | custom-call | tf_op jit(solution)/shard_map/weight_grad/pallas_call | solution.py:406
  302.6 10.2 %weight_grad.12.refs_0_ = bf16[392,288,128]{2,1,0:T(8,128)(2,1)} custom-call(s32[384]{0:T(512)} %fusion.20.rows_ref, bf16[512,3072]{1,0:T(8,128)(2,1)} %copy-done.10, bf16[512,768]{1,0:T(8,128)(2,1)} %copy-done.8, bf16[392,288,128]{2,1,0:T(8,128)(2,1)} %weight_grad.11.refs_0_), custom_call_target="tpu_custom_call", output_to_operand_aliasing={{}: (3, {})} | custom-call | tf_op jit(solution)/shard_map/weight_grad/pallas_call | solution.py:406
  312.8 11.2 %weight_grad.13.refs_0_ = bf16[392,288,128]{2,1,0:T(8,128)(2,1)} custom-call(s32[384]{0:T(512)} %fusion.20.rows_ref, bf16[512,768]{1,0:T(8,128)(2,1)} %copy-done.4, bf16[512,3072]{1,0:T(8,128)(2,1)} %copy-done.12, bf16[392,288,128]{2,1,0:T(8,128)(2,1)} %weight_grad.12.refs_0_), custom_call_target="tpu_custom_call", output_to_operand_aliasing={{}: (3, {})} | custom-call | tf_op jit(solution)/shard_map/weight_grad/pallas_call | solution.py:406
  324.0 4.3 weight_grad.14.refs_0_
  328.3 8.5 %weight_grad.15 = bf16[392,288,128]{2,1,0:T(8,128)(2,1)} custom-call(s32[384]{0:T(512)} %fusion.20.rows_ref, bf16[512,768]{1,0:T(8,128)(2,1)} %bitcast.137, bf16[512,2304]{1,0:T(8,128)(2,1)} %attend_back.3.right_ref, bf16[392,288,128]{2,1,0:T(8,128)(2,1)} %weight_grad.14.refs_0_), custom_call_target="tpu_custom_call", output_to_operand_aliasing={{}: (3, {})} | custom-call | tf_op jit(solution)/shard_map/weight_grad/pallas_call | solution.py:406
  336.9 0.9 broadcast_dynamic-update-slice_fusion
  337.8 154.8 %reduce_slots.1 = (bf16[288,128]{1,0:T(8,128)(2,1)}, bf16[4,128,768]{2,1,0:T(8,128)(2,1)}, bf16[4,128,768]{2,1,0:T(8,128)(2,1)}, f32[6,2304,128]{2,1,0:T(8,128)}...) custom-call(bf16[2,2,2,14112,128]{4,3,2,1,0:T(8,128)(2,1)} %bitcast.119, ...), custom_call_target="tpu_custom_call" | custom-call | tf_op jit(solution)/shard_map/reduce_slots/pallas_call | solution.py:857
  492.6 1.0 convert_element_type.171
  493.7 0.9 divide_subtract_fusion
  494.6 1.3 convert_element_type.170
  495.9 0.9 copy.62
  496.8 6.6 %copy.63 = f32[48,36864]{1,0:T(8,128)} copy(f32[48,36864]{1,0:T(8,128)} %bitcast.134) | data formatting | bytes 14155776
  503.3 3.4 copy.64
  506.7 0.5 slice-done.1
  507.3 3.6 copy.65
  510.9 1.0 copy-done.3
  511.8 1.8 copy.66
  (136 shorter events, 2.0 us)
Async XLA Ops:
  118.3 22.6 %copy-start.21 = (s32[4,1,128]{2,1,0:T(1,128)S(1)}, s32[4,1,128]{2,1,0:T(1,128)}, u32[]{:S(2)}) copy-start(s32[4,1,128]{2,1,0:T(1,128)} %get-tuple-element.46) | copy-start | bytes 6148
  118.3 23.3 %copy-start.2 = (bf16[4,128,768]{2,1,0:T(8,128)(2,1)S(1)}, bf16[4,128,768]{2,1,0:T(8,128)(2,1)}, u32[]{:S(2)}) copy-start(bf16[4,128,768]{2,1,0:T(8,128)(2,1)} %get-tuple-element.45) | copy-start | bytes 2359300
  118.3 23.8 %copy-start.15 = (bf16[4,128,768]{2,1,0:T(8,128)(2,1)S(1)}, bf16[4,128,768]{2,1,0:T(8,128)(2,1)}, u32[]{:S(2)}) copy-start(bf16[4,128,768]{2,1,0:T(8,128)(2,1)} %get-tuple-element.32) | copy-start | bytes 2359300
  147.5 10.1 %copy-start.24 = (bf16[768,768]{1,0:T(8,128)(2,1)S(1)}, bf16[768,768]{1,0:T(8,128)(2,1)}, u32[]{:S(2)}) copy-start(bf16[768,768]{1,0:T(8,128)(2,1)} %get-tuple-element.37) | copy-start | bytes 3538948
  159.9 7.6 %slice-start.6 = ((s8[4718592]{0:T(1024)(128)(4,1)}), s8[4194304]{0:T(1024)(128)(4,1)S(1)}, s32[]{:S(2)}) async-start(s8[4718592]{0:T(1024)(128)(4,1)} %bitcast.156), calls=%async_computation.6 | async-start | bytes 8388608
  160.2 7.2 %copy-start.4 = (bf16[512,768]{1,0:T(8,128)(2,1)}, bf16[512,768]{1,0:T(8,128)(2,1)S(1)}, u32[]{:S(2)}) copy-start(bf16[512,768]{1,0:T(8,128)(2,1)S(1)} %fusion.16.left_ref) | copy-start | bytes 2359300
  160.2 7.3 %slice-start.7 = ((s8[4718592]{0:T(1024)(128)(4,1)}), s8[524288]{0:T(1024)(128)(4,1)S(1)}, s32[]{:S(2)}) async-start(s8[4718592]{0:T(1024)(128)(4,1)} %bitcast.156), calls=%async_computation.7 | async-start | bytes 1048576
  167.5 2.8 copy-start.10
  170.3 2.0 copy-start.23
  172.3 3.4 copy-start.5
  175.7 10.1 %copy-start.26 = (bf16[768,768]{1,0:T(8,128)(2,1)S(1)}, bf16[768,768]{1,0:T(8,128)(2,1)}, u32[]{:S(2)}) copy-start(bf16[768,768]{1,0:T(8,128)(2,1)} %get-tuple-element.42) | copy-start | bytes 3538948
  188.2 6.1 %slice-start.10 = ((s8[4718592]{0:T(1024)(128)(4,1)}), s8[4194304]{0:T(1024)(128)(4,1)S(1)}, s32[]{:S(2)}) async-start(s8[4718592]{0:T(1024)(128)(4,1)} %bitcast.160), calls=%async_computation.10 | async-start | bytes 8388608
  188.5 5.8 %copy-start.6 = (bf16[512,768]{1,0:T(8,128)(2,1)}, bf16[512,768]{1,0:T(8,128)(2,1)S(1)}, u32[]{:S(2)}) copy-start(bf16[512,768]{1,0:T(8,128)(2,1)S(1)} %fusion.18.left_ref) | copy-start | bytes 2359300
  188.5 5.8 %slice-start.11 = ((s8[4718592]{0:T(1024)(128)(4,1)}), s8[524288]{0:T(1024)(128)(4,1)S(1)}, s32[]{:S(2)}) async-start(s8[4718592]{0:T(1024)(128)(4,1)} %bitcast.160), calls=%async_computation.11 | async-start | bytes 1048576
  194.3 2.9 copy-start.13
  200.0 5.5 %slice-start.8 = ((s8[4718592]{0:T(1024)(128)(4,1)}), s8[4194304]{0:T(1024)(128)(4,1)S(1)}, s32[]{:S(2)}) async-start(s8[4718592]{0:T(1024)(128)(4,1)} %bitcast.158), calls=%async_computation.8 | async-start | bytes 8388608
  200.6 4.9 copy-start.14
  200.6 4.9 slice-start.9
  205.5 3.2 copy-start.11
  208.7 1.3 copy-start.27
  209.3 2.4 copy-start.7
  231.8 8.5 %slice-start.4 = ((s8[4718592]{0:T(1024)(128)(4,1)}), s8[4194304]{0:T(1024)(128)(4,1)S(1)}, s32[]{:S(2)}) async-start(s8[4718592]{0:T(1024)(128)(4,1)} %bitcast.154), calls=%async_computation.4 | async-start | bytes 8388608
  232.3 7.9 %copy-start.8 = (bf16[512,768]{1,0:T(8,128)(2,1)}, bf16[512,768]{1,0:T(8,128)(2,1)S(1)}, u32[]{:S(2)}) copy-start(bf16[512,768]{1,0:T(8,128)(2,1)S(1)} %get-tuple-element.97.right_ref) | copy-start | bytes 2359300
  232.4 8.0 %slice-start.5 = ((s8[4718592]{0:T(1024)(128)(4,1)}), s8[524288]{0:T(1024)(128)(4,1)S(1)}, s32[]{:S(2)}) async-start(s8[4718592]{0:T(1024)(128)(4,1)} %bitcast.154), calls=%async_computation.5 | async-start | bytes 1048576
  240.3 3.1 copy-start.12
  243.5 1.3 copy-start.25
  244.0 2.4 copy-start.9
  246.4 15.0 %copy-start.22 = (bf16[768,2304]{1,0:T(8,128)(2,1)S(1)}, bf16[768,2304]{1,0:T(8,128)(2,1)}, u32[]{:S(2)}) copy-start(bf16[768,2304]{1,0:T(8,128)(2,1)} %get-tuple-element.34) | copy-start | bytes 10616836
  261.4 4.7 copy-start.1
  266.1 1.7 copy-start
  337.8 155.9 %copy-start.18 = (f32[2,9216]{1,0:T(2,128)S(1)}, f32[2,9216]{1,0:T(2,128)}, u32[]{:S(2)}) copy-start(f32[2,9216]{1,0:T(2,128)} %param.23) | copy-start | bytes 221188
  337.8 155.9 %copy-start.19 = (f32[2,9216]{1,0:T(2,128)S(1)}, f32[2,9216]{1,0:T(2,128)}, u32[]{:S(2)}) copy-start(f32[2,9216]{1,0:T(2,128)} %param.24) | copy-start | bytes 221188
  337.8 155.9 %copy-start.20 = (f32[2,9216]{1,0:T(2,128)S(1)}, f32[2,9216]{1,0:T(2,128)}, u32[]{:S(2)}) copy-start(f32[2,9216]{1,0:T(2,128)} %param.25) | copy-start | bytes 221188
  492.6 2.0 copy-start.17
  493.6 2.3 copy-start.16
  494.6 8.7 %slice-start.2 = ((s8[7077888]{0:T(1024)(128)(4,1)}), s8[4194304]{0:T(1024)(128)(4,1)S(1)}, s32[]{:S(2)}) async-start(s8[7077888]{0:T(1024)(128)(4,1)} %bitcast.131), calls=%async_computation.2 | async-start | bytes 8388608
  496.8 6.6 %slice-start.3 = ((s8[7077888]{0:T(1024)(128)(4,1)}), s8[2883584]{0:T(1024)(128)(4,1)S(1)}, s32[]{:S(2)}) async-start(s8[7077888]{0:T(1024)(128)(4,1)} %bitcast.131), calls=%async_computation.3 | async-start | bytes 5767168
  496.8 10.0 %slice-start = ((s8[7077888]{0:T(1024)(128)(4,1)}), s8[4194304]{0:T(1024)(128)(4,1)S(1)}, s32[]{:S(2)}) async-start(s8[7077888]{0:T(1024)(128)(4,1)} %bitcast.128), calls=%async_computation | async-start | bytes 8388608
  503.3 3.9 slice-start.1
  507.3 4.6 copy-start.3
